TPU v7x, 256 devices: a whole 4x4x8 slice. The times are simulated.
256 devices in a mesh: ex: 32 (over z, y), ckpt: 8 (over x, core).
Axes of the slice: x: 4, y: 4, z: 8, core: 2. Of those that a mesh axis runs over, the one named last changes fastest.
Arguments:
- grads: bfloat16 [8, 10240, 4096], P('ckpt', 'ex'), may hold values from -6 to 6
- second_moment: float32 [8, 4096], P('ckpt'), may hold values from 0.25 to 4
- step_size: float32 [8], P('ckpt'), may hold values from 0.25 to 1
- partners: int32 [32, 8], P('ex'), may hold values from -1 to 31, as said below
- counts: int32 [32], P('ex'), may hold values from 1 to 8, as said below
Outputs:
- band_rows: float32 [10240, 5120], P('ex', 'ckpt')
Inputs may be any that keep to these rules, and one draw needn't show every extreme that they name: For s < counts[b], partners[b, s] are distinct blocks among (b + 1) mod 32 to (b + 8) mod 32; slots from counts[b] on hold -1. `counts`: some block has 8 live slots in every draw.
All inputs are finite; a program needn't handle non-finite values.
Results may differ from a plain program's by a relative error of at most 0.0029.
Values may be sent and summed in bfloat16 or wider, within the bound.
No kernel may reach another device: no remote copies, remote signals or barrier semaphores. Data moves between devices by JAX's collectives and lax.ppermute only.
A program may use at most 64 MiB of HBM per device.

v0:
```python
import jax
import jax.numpy as jnp
from jax import lax
from jax.sharding import PartitionSpec as P

EPSILON = 1e-08


def passed_along(value, axis, by):
    length = lax.axis_size(axis)
    return lax.ppermute(value, axis, [(i, (i + by) % length) for i in range(length)])


def local(grads, second_moment, step_size, partners, counts):
    width = grads.shape[2]
    block_rows = grads.shape[1]
    reach = partners.shape[1]
    blocks = lax.axis_size("ex")
    position = lax.axis_index("ex")
    factor = step_size[:, None] / (jnp.sqrt(second_moment) + EPSILON) * width ** (-0.5)
    scaled = (grads.astype(jnp.float32) * factor[:, None, :]).astype(jnp.bfloat16)
    offsets = jnp.mod(partners[0] - position, blocks)
    alive_slot = jnp.arange(reach, dtype=jnp.int32) < counts[0]
    wanted = jnp.arange(1, reach + 1, dtype=jnp.int32)
    matched = jnp.logical_and(offsets[:, None] == wanted[None, :], alive_slot[:, None])
    listed = jnp.sum(matched.astype(jnp.float32), axis=0)
    empty_tile = jnp.zeros((block_rows, block_rows), jnp.float32)

    def product(visitor):
        return lax.dot_general(
            scaled, visitor, (((0, 2), (0, 2)), ((), ())), preferred_element_type=jnp.float32
        )

    def make_tile(visitor, weight):
        return lax.cond(weight > 0, product, lambda unused: empty_tile, visitor)

    def advance(step, carry):
        visitor, stacked = carry
        visitor = passed_along(visitor, "ex", -1)
        fresh = make_tile(visitor, listed[step])
        stacked = lax.dynamic_update_slice_in_dim(stacked, fresh[:, None, :], step, 1)
        return (visitor, stacked)

    initial = jnp.zeros((block_rows, reach, block_rows), jnp.float32)
    unused, stacked = lax.fori_loop(0, reach, advance, (grads, initial))
    returned = []
    for offset in range(reach, 0, -1):
        arrived = passed_along(stacked[:, offset - 1, :], "ex", offset)
        returned.append(arrived.T)
    panel = jnp.concatenate([jnp.stack(returned, axis=1), stacked], axis=1)
    panel = panel.reshape(block_rows, 2 * reach * block_rows)
    return lax.psum_scatter(panel, "ckpt", scatter_dimension=1, tiled=True)


def solution(mesh):
    in_specs = (P("ckpt", "ex", None), P("ckpt", None), P("ckpt"), P("ex", None), P("ex"))
    out_specs = P("ex", "ckpt")
    return jax.shard_map(local, mesh=mesh, in_specs=in_specs, out_specs=out_specs, check_vma=False)
```

profile of v0, /device:TPU:1, one launch (start us, length us, event | category | flops | bytes accessed | tf_op | source)
XLA Modules:
  0.0 727.1 jit_solution(14683547059490021606)
XLA Ops:
  6.5 3.6 copy.48
  12.8 3.9 multiply_convert_fusion
  16.8 498.5 %while.15 = (s32[]{:T(128)}, bf16[1,320,4096]{2,1,0:T(8,128)(2,1)}, f32[320,8,320]{2,0,1:T(8,128)}, f32[8]{0:T(128)S(1)}, bf16[1,320,4096]{2,1,0:T(8,128)(2,1)}, /*index=5*/s32[]{:T(128)}, f32[1]{0:T(128)}) while((s32[]{:T(128)}, bf16[1,320,4096]{2,1,0:T(8,128)(2,1)}, f32[320,8,320]{2,0,1:T(8,128)}, f32[8]{0:T(128)S(1)}, ...), condition=%wide.region_4.5_spmd, body=%wide.region_1.4_spmd.sunk | while | flops 838860800 | bytes 22282420 | solution.py:45
  16.8 8.9 %collective-permute-start = (bf16[1,320,4096]{2,1,0:T(8,128)(2,1)}, bf16[1,320,4096]{2,1,0:T(8,128)(2,1)S(1)}, u32[]{:S(2)}, u32[]{:S(2)}) collective-permute-start(bf16[1,320,4096]{2,1,0:T(8,128)(2,1)} %get-tuple-element.173), channel_id=1, source_target_pairs={{0,248},{8,0},{16,8},{24,16},{32,24},{40,32},{48,40},{56,48},{64,5... | collective-permute-start | bytes 7864328 | tf_op jit(solution)/shard_map/while/body/eval_jaxpr/ppermute | solution.py:11
  27.0 54.5 %collective-permute-done = bf16[1,320,4096]{2,1,0:T(8,128)(2,1)S(1)} collective-permute-done((bf16[1,320,4096]{2,1,0:T(8,128)(2,1)}, bf16[1,320,4096]{2,1,0:T(8,128)(2,1)S(1)}, u32[]{:S(2)}, u32[]{:S(2)}) %collective-permute-start) | collective-permute-done | bytes 2621472 | tf_op jit(solution)/shard_map/while/body/eval_jaxpr/ppermute | solution.py:11
  84.0 5.4 collective-permute-start
  90.7 53.7 %collective-permute-done = bf16[1,320,4096]{2,1,0:T(8,128)(2,1)S(1)} collective-permute-done((bf16[1,320,4096]{2,1,0:T(8,128)(2,1)}, bf16[1,320,4096]{2,1,0:T(8,128)(2,1)S(1)}, u32[]{:S(2)}, u32[]{:S(2)}) %collective-permute-start) | collective-permute-done | bytes 2621472 | tf_op jit(solution)/shard_map/while/body/eval_jaxpr/ppermute | solution.py:11
  144.4 3.3 conditional.2
  144.4 3.3 fusion.3
  153.5 52.8 %collective-permute-done = bf16[1,320,4096]{2,1,0:T(8,128)(2,1)S(1)} collective-permute-done((bf16[1,320,4096]{2,1,0:T(8,128)(2,1)}, bf16[1,320,4096]{2,1,0:T(8,128)(2,1)S(1)}, u32[]{:S(2)}, u32[]{:S(2)}) %collective-permute-start) | collective-permute-done | bytes 2621472 | tf_op jit(solution)/shard_map/while/body/eval_jaxpr/ppermute | solution.py:11
  208.7 8.6 %collective-permute-start = (bf16[1,320,4096]{2,1,0:T(8,128)(2,1)}, bf16[1,320,4096]{2,1,0:T(8,128)(2,1)S(1)}, u32[]{:S(2)}, u32[]{:S(2)}) collective-permute-start(bf16[1,320,4096]{2,1,0:T(8,128)(2,1)} %get-tuple-element.173), channel_id=1, source_target_pairs={{0,248},{8,0},{16,8},{24,16},{32,24},{40,32},{48,40},{56,48},{64,5... | collective-permute-start | bytes 7864328 | tf_op jit(solution)/shard_map/while/body/eval_jaxpr/ppermute | solution.py:11
  218.7 52.0 %collective-permute-done = bf16[1,320,4096]{2,1,0:T(8,128)(2,1)S(1)} collective-permute-done((bf16[1,320,4096]{2,1,0:T(8,128)(2,1)}, bf16[1,320,4096]{2,1,0:T(8,128)(2,1)S(1)}, u32[]{:S(2)}, u32[]{:S(2)}) %collective-permute-start) | collective-permute-done | bytes 2621472 | tf_op jit(solution)/shard_map/while/body/eval_jaxpr/ppermute | solution.py:11
  273.1 8.6 %collective-permute-start = (bf16[1,320,4096]{2,1,0:T(8,128)(2,1)}, bf16[1,320,4096]{2,1,0:T(8,128)(2,1)S(1)}, u32[]{:S(2)}, u32[]{:S(2)}) collective-permute-start(bf16[1,320,4096]{2,1,0:T(8,128)(2,1)} %get-tuple-element.173), channel_id=1, source_target_pairs={{0,248},{8,0},{16,8},{24,16},{32,24},{40,32},{48,40},{56,48},{64,5... | collective-permute-start | bytes 7864328 | tf_op jit(solution)/shard_map/while/body/eval_jaxpr/ppermute | solution.py:11
  283.0 51.1 %collective-permute-done = bf16[1,320,4096]{2,1,0:T(8,128)(2,1)S(1)} collective-permute-done((bf16[1,320,4096]{2,1,0:T(8,128)(2,1)}, bf16[1,320,4096]{2,1,0:T(8,128)(2,1)S(1)}, u32[]{:S(2)}, u32[]{:S(2)}) %collective-permute-start) | collective-permute-done | bytes 2621472 | tf_op jit(solution)/shard_map/while/body/eval_jaxpr/ppermute | solution.py:11
  334.1 3.3 conditional.2
  339.7 5.4 collective-permute-start
  346.5 50.3 %collective-permute-done = bf16[1,320,4096]{2,1,0:T(8,128)(2,1)S(1)} collective-permute-done((bf16[1,320,4096]{2,1,0:T(8,128)(2,1)}, bf16[1,320,4096]{2,1,0:T(8,128)(2,1)S(1)}, u32[]{:S(2)}, u32[]{:S(2)}) %collective-permute-start) | collective-permute-done | bytes 2621472 | tf_op jit(solution)/shard_map/while/body/eval_jaxpr/ppermute | solution.py:11
  396.7 3.3 conditional.2
  396.7 3.3 fusion.3
  405.9 49.4 %collective-permute-done = bf16[1,320,4096]{2,1,0:T(8,128)(2,1)S(1)} collective-permute-done((bf16[1,320,4096]{2,1,0:T(8,128)(2,1)}, bf16[1,320,4096]{2,1,0:T(8,128)(2,1)S(1)}, u32[]{:S(2)}, u32[]{:S(2)}) %collective-permute-start) | collective-permute-done | bytes 2621472 | tf_op jit(solution)/shard_map/while/body/eval_jaxpr/ppermute | solution.py:11
  455.3 3.3 conditional.2
  455.3 3.3 fusion.3
  464.4 48.5 %collective-permute-done = bf16[1,320,4096]{2,1,0:T(8,128)(2,1)S(1)} collective-permute-done((bf16[1,320,4096]{2,1,0:T(8,128)(2,1)}, bf16[1,320,4096]{2,1,0:T(8,128)(2,1)S(1)}, u32[]{:S(2)}, u32[]{:S(2)}) %collective-permute-start) | collective-permute-done | bytes 2621472 | tf_op jit(solution)/shard_map/while/body/eval_jaxpr/ppermute | solution.py:11
  515.3 5.5 copy.15
  523.6 7.8 %collective-permute-start.7 = (f32[320,320]{0,1:T(8,128)S(1)}, f32[320,320]{0,1:T(8,128)S(1)}, u32[]{:S(2)}, u32[]{:S(2)}) collective-permute-start(f32[320,320]{0,1:T(8,128)S(1)} %get-tuple-element.125), channel_id=1, source_target_pairs={{0,16},{8,24},{16,32},{24,40},{32,48},{40,56},{48,64},{56,72},{64,... | collective-permute-start | bytes 1228808 | tf_op jit(solution)/shard_map/ppermute | solution.py:11
  531.4 15.8 %collective-permute-done.1 = f32[320,320]{0,1:T(8,128)S(1)} collective-permute-done((f32[320,320]{0,1:T(8,128)S(1)}, f32[320,320]{0,1:T(8,128)S(1)}, u32[]{:S(2)}, u32[]{:S(2)}) %collective-permute-start.1) | collective-permute-done | bytes 409632 | tf_op jit(solution)/shard_map/ppermute | solution.py:11
  547.2 18.4 %collective-permute-done.2 = f32[320,320]{0,1:T(8,128)S(1)} collective-permute-done((f32[320,320]{0,1:T(8,128)S(1)}, f32[320,320]{0,1:T(8,128)S(1)}, u32[]{:S(2)}, u32[]{:S(2)}) %collective-permute-start.2) | collective-permute-done | bytes 409632 | tf_op jit(solution)/shard_map/ppermute | solution.py:11
  565.7 42.9 %collective-permute-done.3 = f32[320,320]{0,1:T(8,128)S(1)} collective-permute-done((f32[320,320]{0,1:T(8,128)S(1)}, f32[320,320]{0,1:T(8,128)S(1)}, u32[]{:S(2)}, u32[]{:S(2)}) %collective-permute-start.3) | collective-permute-done | bytes 409632 | tf_op jit(solution)/shard_map/ppermute | solution.py:11
  608.6 30.6 %collective-permute-done.4 = f32[320,320]{0,1:T(8,128)S(1)} collective-permute-done((f32[320,320]{0,1:T(8,128)S(1)}, f32[320,320]{0,1:T(8,128)S(1)}, u32[]{:S(2)}, u32[]{:S(2)}) %collective-permute-start.4) | collective-permute-done | bytes 409632 | tf_op jit(solution)/shard_map/ppermute | solution.py:11
  639.7 7.6 %copy.23 = f32[320,16,320]{2,1,0:T(8,128)} copy(f32[320,16,320]{2,0,1:T(8,128)S(1)} %constant_dynamic-update-slice_fusion.1) | data formatting | bytes 13107200 | tf_op jit(solution)/shard_map/concatenate | solution.py:50
  647.4 9.2 %reshape.45 = f32[320,5120]{1,0:T(8,128)} reshape(f32[320,16,320]{2,1,0:T(8,128)} %copy.23) | data formatting | bytes 13107200 | tf_op jit(solution)/shard_map/reshape | solution.py:51
  656.6 63.7 %reduce-scatter.2.cloned.1.call-done = f32[320,640]{1,0:T(8,128)} async-done(((f32[320,5120]{1,0:T(8,128)}), f32[320,640]{1,0:T(8,128)}) %reduce-scatter.2.cloned.1.call-update) | async-done | bytes 819216 | tf_op jit(solution)/shard_map/reduce_scatter | solution.py:52
  (66 shorter events, 38.8 us)
Async XLA Ops:
  6.5 713.7 %reduce-scatter.2.cloned.1.call-start = ((), (), s32[]{:S(2)}) async-start(), calls=%async_computation.1 | async-start | bytes 7372800 | tf_op jit(solution)/shard_map/reduce_scatter | solution.py:52
  16.8 64.8 %collective-permute-start = (bf16[1,320,4096]{2,1,0:T(8,128)(2,1)}, bf16[1,320,4096]{2,1,0:T(8,128)(2,1)S(1)}, u32[]{:S(2)}, u32[]{:S(2)}) collective-permute-start(bf16[1,320,4096]{2,1,0:T(8,128)(2,1)} %get-tuple-element.173), channel_id=1, source_target_pairs={{0,248},{8,0},{16,8},{24,16},{32,24},{40,32},{48,40},{56,48},{64,5... | collective-permute-start | bytes 7864328 | tf_op jit(solution)/shard_map/while/body/eval_jaxpr/ppermute | solution.py:11
  84.0 60.4 %collective-permute-start = (bf16[1,320,4096]{2,1,0:T(8,128)(2,1)}, bf16[1,320,4096]{2,1,0:T(8,128)(2,1)S(1)}, u32[]{:S(2)}, u32[]{:S(2)}) collective-permute-start(bf16[1,320,4096]{2,1,0:T(8,128)(2,1)} %get-tuple-element.173), channel_id=1, source_target_pairs={{0,248},{8,0},{16,8},{24,16},{32,24},{40,32},{48,40},{56,48},{64,5... | collective-permute-start | bytes 7864328 | tf_op jit(solution)/shard_map/while/body/eval_jaxpr/ppermute | solution.py:11
  150.0 56.3 %collective-permute-start = (bf16[1,320,4096]{2,1,0:T(8,128)(2,1)}, bf16[1,320,4096]{2,1,0:T(8,128)(2,1)S(1)}, u32[]{:S(2)}, u32[]{:S(2)}) collective-permute-start(bf16[1,320,4096]{2,1,0:T(8,128)(2,1)} %get-tuple-element.173), channel_id=1, source_target_pairs={{0,248},{8,0},{16,8},{24,16},{32,24},{40,32},{48,40},{56,48},{64,5... | collective-permute-start | bytes 7864328 | tf_op jit(solution)/shard_map/while/body/eval_jaxpr/ppermute | solution.py:11
  208.7 61.9 %collective-permute-start = (bf16[1,320,4096]{2,1,0:T(8,128)(2,1)}, bf16[1,320,4096]{2,1,0:T(8,128)(2,1)S(1)}, u32[]{:S(2)}, u32[]{:S(2)}) collective-permute-start(bf16[1,320,4096]{2,1,0:T(8,128)(2,1)} %get-tuple-element.173), channel_id=1, source_target_pairs={{0,248},{8,0},{16,8},{24,16},{32,24},{40,32},{48,40},{56,48},{64,5... | collective-permute-start | bytes 7864328 | tf_op jit(solution)/shard_map/while/body/eval_jaxpr/ppermute | solution.py:11
  273.1 61.1 %collective-permute-start = (bf16[1,320,4096]{2,1,0:T(8,128)(2,1)}, bf16[1,320,4096]{2,1,0:T(8,128)(2,1)S(1)}, u32[]{:S(2)}, u32[]{:S(2)}) collective-permute-start(bf16[1,320,4096]{2,1,0:T(8,128)(2,1)} %get-tuple-element.173), channel_id=1, source_target_pairs={{0,248},{8,0},{16,8},{24,16},{32,24},{40,32},{48,40},{56,48},{64,5... | collective-permute-start | bytes 7864328 | tf_op jit(solution)/shard_map/while/body/eval_jaxpr/ppermute | solution.py:11
  339.7 57.0 %collective-permute-start = (bf16[1,320,4096]{2,1,0:T(8,128)(2,1)}, bf16[1,320,4096]{2,1,0:T(8,128)(2,1)S(1)}, u32[]{:S(2)}, u32[]{:S(2)}) collective-permute-start(bf16[1,320,4096]{2,1,0:T(8,128)(2,1)} %get-tuple-element.173), channel_id=1, source_target_pairs={{0,248},{8,0},{16,8},{24,16},{32,24},{40,32},{48,40},{56,48},{64,5... | collective-permute-start | bytes 7864328 | tf_op jit(solution)/shard_map/while/body/eval_jaxpr/ppermute | solution.py:11
  402.4 52.9 %collective-permute-start = (bf16[1,320,4096]{2,1,0:T(8,128)(2,1)}, bf16[1,320,4096]{2,1,0:T(8,128)(2,1)S(1)}, u32[]{:S(2)}, u32[]{:S(2)}) collective-permute-start(bf16[1,320,4096]{2,1,0:T(8,128)(2,1)} %get-tuple-element.173), channel_id=1, source_target_pairs={{0,248},{8,0},{16,8},{24,16},{32,24},{40,32},{48,40},{56,48},{64,5... | collective-permute-start | bytes 7864328 | tf_op jit(solution)/shard_map/while/body/eval_jaxpr/ppermute | solution.py:11
  460.9 52.1 %collective-permute-start = (bf16[1,320,4096]{2,1,0:T(8,128)(2,1)}, bf16[1,320,4096]{2,1,0:T(8,128)(2,1)S(1)}, u32[]{:S(2)}, u32[]{:S(2)}) collective-permute-start(bf16[1,320,4096]{2,1,0:T(8,128)(2,1)} %get-tuple-element.173), channel_id=1, source_target_pairs={{0,248},{8,0},{16,8},{24,16},{32,24},{40,32},{48,40},{56,48},{64,5... | collective-permute-start | bytes 7864328 | tf_op jit(solution)/shard_map/while/body/eval_jaxpr/ppermute | solution.py:11
  520.8 118.7 %copy-start = (f32[320,8,320]{2,0,1:T(8,128)S(1)}, f32[320,8,320]{2,0,1:T(8,128)}, u32[]{:S(2)}) copy-start(f32[320,8,320]{2,0,1:T(8,128)} %get-tuple-element.113) | copy-start | bytes 9830404
  523.3 23.9 %collective-permute-start.1 = (f32[320,320]{0,1:T(8,128)S(1)}, f32[320,320]{0,1:T(8,128)S(1)}, u32[]{:S(2)}, u32[]{:S(2)}) collective-permute-start(f32[320,320]{0,1:T(8,128)S(1)} %get-tuple-element.131), channel_id=1, source_target_pairs={{0,64},{8,72},{16,80},{24,88},{32,96},{40,104},{48,112},{56,120},{... | collective-permute-start | bytes 1228808 | tf_op jit(solution)/shard_map/ppermute | solution.py:11
  523.4 42.2 %collective-permute-start.2 = (f32[320,320]{0,1:T(8,128)S(1)}, f32[320,320]{0,1:T(8,128)S(1)}, u32[]{:S(2)}, u32[]{:S(2)}) collective-permute-start(f32[320,320]{0,1:T(8,128)S(1)} %get-tuple-element.130), channel_id=1, source_target_pairs={{0,56},{8,64},{16,72},{24,80},{32,88},{40,96},{48,104},{56,112},{6... | collective-permute-start | bytes 1228808 | tf_op jit(solution)/shard_map/ppermute | solution.py:11
  523.5 115.9 %collective-permute-start.8 = (f32[320,320]{0,1:T(8,128)S(1)}, f32[320,320]{0,1:T(8,128)S(1)}, u32[]{:S(2)}, u32[]{:S(2)}) collective-permute-start(f32[320,320]{0,1:T(8,128)S(1)} %get-tuple-element.124), channel_id=1, source_target_pairs={{0,8},{8,16},{16,24},{24,32},{32,40},{40,48},{48,56},{56,64},{64,7... | collective-permute-start | bytes 1228808 | tf_op jit(solution)/shard_map/ppermute | solution.py:11
  523.6 115.8 %collective-permute-start.7 = (f32[320,320]{0,1:T(8,128)S(1)}, f32[320,320]{0,1:T(8,128)S(1)}, u32[]{:S(2)}, u32[]{:S(2)}) collective-permute-start(f32[320,320]{0,1:T(8,128)S(1)} %get-tuple-element.125), channel_id=1, source_target_pairs={{0,16},{8,24},{16,32},{24,40},{32,48},{40,56},{48,64},{56,72},{64,... | collective-permute-start | bytes 1228808 | tf_op jit(solution)/shard_map/ppermute | solution.py:11
  531.3 108.0 %collective-permute-start.6 = (f32[320,320]{0,1:T(8,128)S(1)}, f32[320,320]{0,1:T(8,128)S(1)}, u32[]{:S(2)}, u32[]{:S(2)}) collective-permute-start(f32[320,320]{0,1:T(8,128)S(1)} %get-tuple-element.126), channel_id=1, source_target_pairs={{0,24},{8,32},{16,40},{24,48},{32,56},{40,64},{48,72},{56,80},{64,... | collective-permute-start | bytes 1228808 | tf_op jit(solution)/shard_map/ppermute | solution.py:11
  547.2 61.4 %collective-permute-start.3 = (f32[320,320]{0,1:T(8,128)S(1)}, f32[320,320]{0,1:T(8,128)S(1)}, u32[]{:S(2)}, u32[]{:S(2)}) collective-permute-start(f32[320,320]{0,1:T(8,128)S(1)} %get-tuple-element.129), channel_id=1, source_target_pairs={{0,48},{8,56},{16,64},{24,72},{32,80},{40,88},{48,96},{56,104},{64... | collective-permute-start | bytes 1228808 | tf_op jit(solution)/shard_map/ppermute | solution.py:11
  565.6 73.6 %collective-permute-start.4 = (f32[320,320]{0,1:T(8,128)S(1)}, f32[320,320]{0,1:T(8,128)S(1)}, u32[]{:S(2)}, u32[]{:S(2)}) collective-permute-start(f32[320,320]{0,1:T(8,128)S(1)} %get-tuple-element.128), channel_id=1, source_target_pairs={{0,40},{8,48},{16,56},{24,64},{32,72},{40,80},{48,88},{56,96},{64,... | collective-permute-start | bytes 1228808 | tf_op jit(solution)/shard_map/ppermute | solution.py:11
  608.6 30.7 %collective-permute-start.5 = (f32[320,320]{0,1:T(8,128)S(1)}, f32[320,320]{0,1:T(8,128)S(1)}, u32[]{:S(2)}, u32[]{:S(2)}) collective-permute-start(f32[320,320]{0,1:T(8,128)S(1)} %get-tuple-element.127), channel_id=1, source_target_pairs={{0,32},{8,40},{16,48},{24,56},{32,64},{40,72},{48,80},{56,88},{64,... | collective-permute-start | bytes 1228808 | tf_op jit(solution)/shard_map/ppermute | solution.py:11
Sparse Core Ops, SparseCore 0:
  656.7 63.5 reduce-scatter.1
where the time goes:
time: 731 us; the launch traced here: 727 us
  waiting for transfers between devices  584 us (80%)
  local copies, waits for them, and re-layouts  52.9 us (7%)
  starting transfers between devices  51.6 us (7%)
  between operations  14.8 us (2%)
  matrix products  13.1 us (2%)
    ppermute x16, waiting for transfers between devices, passed_along(): lax.ppermute(value, axis, [(i, (i + by) % length) for i in range(length)])  520 us
    reduce_scatter x1, waiting for transfers between devices, local(): return lax.psum_scatter(panel, 'ckpt', scatter_dimension=1, tiled=True)  63.7 us
    ppermute x16, starting transfers between devices, passed_along(): lax.ppermute(value, axis, [(i, (i + by) % length) for i in range(length)])  51.6 us
  transfers between devices with their start and end apart: 17, of which 13 were waited for; matrix products, arithmetic and copies ran while one was open for 1% of the time, Pallas kernels for 0%

commit v1 on v0

v1 whole, which is shorter than its diff:
```python
import jax
import jax.numpy as jnp
from jax import lax
from jax.experimental import pallas as pl
from jax.experimental.pallas import tpu as pltpu
from jax.sharding import PartitionSpec as P


EPSILON = 1e-08
AXES = ("ex", "ckpt")
NY = 4
CHUNK = 32


def tiles_kernel(place_ref, factor_ref, *refs):
    here, above, below = refs[0:4], refs[4:8], refs[8:12]
    keep_ref, give_ref, left_ref, right_ref = refs[12:]
    rows = here[0].shape[0]
    half = rows // 2
    y = place_ref[0]
    c = place_ref[1]
    r = pl.program_id(0)

    @pl.when(r == 0)
    def _():
        for plane, group in enumerate((below, here, above)):
            for rel in range(NY):
                start = (plane * NY + lax.rem(y + rel, NY)) * rows

                @pl.loop(0, rows // CHUNK)
                def _(step, plane=plane, group=group, rel=rel, start=start):
                    source = pl.ds(pl.multiple_of(step * CHUNK, CHUNK), CHUNK)
                    target = pl.ds(pl.multiple_of(start + step * CHUNK, CHUNK), CHUNK)
                    piece = group[rel][source, :]
                    left_ref[target, :] = (piece.astype(jnp.float32) * factor_ref[...]).astype(jnp.bfloat16)
                    if plane == 2:
                        right_ref[rel, source, :] = piece

    b = lax.rem(y + r, NY)
    for far in range(2):
        for out_ref, core in ((keep_ref, c), (give_ref, 1 - c)):
            start = pl.multiple_of((b + 6 - 2 * (2 * far + core)) * rows, CHUNK)
            product = lax.dot_general(
                right_ref[r],
                left_ref[pl.ds(start, 2 * rows), :],
                (((1,), (1,)), ((), ())),
                preferred_element_type=jnp.float32,
            ).astype(out_ref.dtype)
            low, high = (0, 3) if far else (1, 2)
            for slot, first in ((high, 0), (low, rows)):
                out_ref[0, slot, :, 0:rows] = product[0:half, first : first + rows]
                out_ref[0, slot, :, rows : 2 * rows] = product[half:rows, first : first + rows]


def tiles(place, factor, here, above, below):
    rows, width = here[0].shape
    half = rows // 2
    vmem = pl.BlockSpec(memory_space=pltpu.VMEM)
    block = pl.BlockSpec((1, 4, half, 2 * rows), lambda r: (r, 0, 0, 0))
    return pl.pallas_call(
        tiles_kernel,
        grid=(NY,),
        in_specs=[pl.BlockSpec(memory_space=pltpu.SMEM), vmem] + [vmem] * 12,
        out_specs=[block, block],
        out_shape=[
            jax.ShapeDtypeStruct((NY, 4, half, 2 * rows), jnp.float32),
            jax.ShapeDtypeStruct((NY, 4, half, 2 * rows), jnp.bfloat16),
        ],
        scratch_shapes=[
            pltpu.VMEM((3 * NY * rows, width), jnp.bfloat16),
            pltpu.VMEM((NY, rows, width), jnp.bfloat16),
        ],
        compiler_params=pltpu.CompilerParams(vmem_limit_bytes=44 * 2**20),
        cost_estimate=pl.CostEstimate(
            flops=2 * 32 * rows * rows * width, bytes_accessed=24 * rows * width * 2, transcendentals=0
        ),
    )(place, factor, *here, *above, *below)


def local_fn(blocks):
    def flat(e, x, c):
        return (e % blocks) * 8 + (x % 4) * 2 + c

    def ring(e, by):
        return e - e % NY + (e + by) % NY

    def send(value, move):
        pairs = []
        for e in range(blocks):
            for x in range(4):
                for c in range(2):
                    target = move(e, x, c)
                    if target is not None:
                        pairs.append((flat(e, x, c), flat(*target)))
        return lax.ppermute(value, AXES, pairs)

    def offset_of(x, c):
        return (4 if x in (0, 3) else 0) + 2 * c + 1 + (1 if x >= 2 else 0)

    def local(grads, second_moment, step_size, partners, counts):
        width = grads.shape[2]
        rows = grads.shape[1]
        reach = partners.shape[1]
        quarter = width // NY
        part = rows // 4
        e = lax.axis_index("ex")
        k = lax.axis_index("ckpt")
        y = lax.rem(e, NY)
        x = k // 2
        c = lax.rem(k, 2)
        own = grads[0]

        def cut(index):
            return lax.dynamic_slice_in_dim(own, lax.rem(index, NY) * quarter, quarter, 1)

        here = [None] * NY
        above = [None] * NY
        below = [None] * NY
        here[0] = lax.optimization_barrier(cut(y))
        for s in (1, 3, 2):
            here[NY - s] = send(cut(y + s), lambda e, x, c, s=s: (ring(e, s), x, c))
        for r in (0, 3, 1, 2):
            above[r] = send(here[r], lambda e, x, c: (e - NY, x, c))
            below[r] = send(here[r], lambda e, x, c: (e + NY, x, c))

        offsets = jnp.mod(partners[0] - e, blocks)
        alive = jnp.arange(reach, dtype=jnp.int32) < counts[0]
        wanted = jnp.arange(1, reach + 1, dtype=jnp.int32)
        matched = jnp.logical_and(offsets[:, None] == wanted[None, :], alive[:, None])
        listed = jnp.sum(matched.astype(jnp.float32), axis=0)
        listed = send(listed, lambda e, x, c: (e + offset_of(x, c) - NY, x, c))
        is_far = jnp.logical_or(x == 0, x == 3)
        offset = jnp.where(is_far, NY, 0) + 2 * c + 1 + jnp.where(x >= 2, 1, 0)
        weight = lax.dynamic_slice_in_dim(listed, offset - 1, 1, 0)[0]

        factor = step_size[:, None] / (jnp.sqrt(second_moment) + EPSILON) * width ** (-0.5)
        factor = lax.dynamic_slice_in_dim(factor, y * quarter, quarter, 1)
        keep, give = tiles(jnp.stack([y, c]), factor, here, above, below)

        given = send(give, lambda e, x, c: (e, x, 1 - c))
        total = keep + given.astype(jnp.float32)

        def pick(array, index, axis):
            return lax.dynamic_index_in_dim(array, lax.rem(index, 4), axis, keepdims=False)

        upper, lower = total[:, :, :part], total[:, :, part:]
        near_x = pick(upper, x, 1)
        near_y = lower[0]
        arrived_x, arrived_y = [], []
        for t in (1, 3, 2):
            arrived_x.append(send(pick(upper, x + t, 1).astype(jnp.bfloat16), lambda e, x, c, t=t: (e, x + t, c)))
            arrived_y.append(send(lower[t].astype(jnp.bfloat16), lambda e, x, c, t=t: (ring(e, t), x, c)))
        for value in arrived_x:
            near_x = near_x + value.astype(jnp.float32)
        for value in arrived_y:
            near_y = near_y + value.astype(jnp.float32)
        first = near_x[0]
        last = pick(near_y, x, 0)
        arrived_x, arrived_y = [], []
        for t in (1, 3, 2):
            arrived_y.append(send(near_x[t].astype(jnp.bfloat16), lambda e, x, c, t=t: (ring(e, t), x, c)))
            arrived_x.append(send(pick(near_y, x + t, 0).astype(jnp.bfloat16), lambda e, x, c, t=t: (e, x + t, c)))
        for value in arrived_y:
            first = first + value.astype(jnp.float32)
        for value in arrived_x:
            last = last + value.astype(jnp.float32)
        final = jnp.concatenate([first, last], axis=0)
        final = jnp.where(weight > 0, final, 0.0)

        def back(low):
            def move(e, x, c):
                if (x < 2) != low:
                    return None
                return (e + NY, 0 if x in (0, 3) else 1, 1 - c)

            return move

        def ahead(low):
            def move(e, x, c):
                if (x < 2) != low:
                    return None
                return (e + NY - offset_of(x, c), 3 if x in (0, 3) else 2, c)

            return move

        back_low = send(final, back(True))
        back_high = send(final, back(False))
        ahead_low = send(final, ahead(True))
        ahead_high = send(final, ahead(False))

        def later(tile):
            return jnp.concatenate([tile[:, :rows], tile[:, rows:]], axis=0)

        backward = jnp.concatenate([later(back_high), later(back_low)], axis=1)
        forward = jnp.concatenate([later(ahead_low), later(ahead_high)], axis=0)
        forward = jnp.concatenate([forward[:rows].T, forward[rows:].T], axis=1)
        return jnp.where(x >= 2, forward, backward)

    return local


def build(mesh):
    local = local_fn(mesh.shape["ex"])
    in_specs = (P("ckpt", "ex", None), P("ckpt", None), P("ckpt"), P("ex", None), P("ex"))
    return jax.shard_map(local, mesh=mesh, in_specs=in_specs, out_specs=P("ex", "ckpt"), check_vma=False)


def solution(mesh):
    return build(mesh)
```

time: 731 us -> 192 us (0.26)
  waiting for transfers between devices: 584 us -> 80.2 us
  local copies, waits for them, and re-layouts: 52.9 us -> 9.98 us
  starting transfers between devices: 51.6 us -> 72.6 us
  Pallas kernels: 0 us -> 14.6 us
  matrix products: 13.1 us -> 0 us
  between operations: 14.8 us -> 2.27 us
    ppermute x16 -> x29, waiting for transfers between devices: 520 us -> 80.2 us  [send(): return lax.ppermute(value, AXES, pairs)]
    reduce_scatter x1 -> x0, waiting for transfers between devices: 63.7 us -> none  [local(): return lax.psum_scatter(panel, 'ckpt', scatter_dimension=1, tiled=True)]
    ppermute x16 -> x29, starting transfers between devices: 51.6 us -> 72.6 us  [send(): return lax.ppermute(value, AXES, pairs)]
    while x9 -> x0, local copies, waits for them, and re-layouts: 17.6 us -> none
    pallas_call x0 -> x1, Pallas kernels: none -> 14.6 us  [tiles(): pl.pallas_call(tiles_kernel, grid=(NY,), in_specs=[pl.BlockSpec(memory_sp...]
    dot_general x4 -> x0, matrix products: 13.1 us -> none  [product(): lax.dot_general(scaled, visitor, (((0, 2), (0, 2)), ((), ())), preferred_...]
    reshape x1 -> x0, local copies, waits for them, and re-layouts: 9.19 us -> none  [local(): panel = panel.reshape(block_rows, 2 * reach * block_rows)]
    concatenate x2 -> x0, local copies, waits for them, and re-layouts: 7.87 us -> none  [local(): panel = jnp.concatenate([jnp.stack(returned, axis=1), stacked], axis=1)]
  transfers between devices with their start and end apart: 17 -> 29, of which waited for: 13 -> 13; matrix products, arithmetic and copies ran while one was open for 1% -> 4% of each run, Pallas kernels for 0% -> 0%
where the time goes in v1:
time: 192 us; the launch traced here: 191 us
  waiting for transfers between devices  80.2 us (42%)
  starting transfers between devices  72.6 us (38%)
  Pallas kernels  14.6 us (8%)
  other arithmetic  11 us (6%)
  local copies, waits for them, and re-layouts  9.98 us (5%)
  between operations  2.27 us (1%)
    ppermute x29, waiting for transfers between devices, send(): return lax.ppermute(value, AXES, pairs)  80.2 us
    ppermute x29, starting transfers between devices, send(): return lax.ppermute(value, AXES, pairs)  72.6 us
    pallas_call x1, Pallas kernels, tiles(): pl.pallas_call(tiles_kernel, grid=(NY,), in_specs=[pl.BlockSpec(memory_sp...  14.6 us
    another operation x2, other arithmetic  7.1 us
    unnamed x14, local copies, waits for them, and re-layouts  4.44 us
  transfers between devices with their start and end apart: 29, of which 13 were waited for; matrix products, arithmetic and copies ran while one was open for 4% of the time, Pallas kernels for 0%

profile of v1, /device:TPU:1, one launch (start us, length us, event | category | flops | bytes accessed | tf_op | source)
XLA Modules:
  0.0 190.7 jit_solution(17092347340486956634)
XLA Ops:
  0.0 1.9 %dynamic-slice_bitcast_fusion = (bf16[320,1024]{1,0:T(8,128)(2,1)S(1)}, bf16[320,1024]{1,0:T(8,128)(2,1)S(1)}, bf16[320,1024]{1,0:T(8,128)(2,1)S(1)}, bf16[320,1024]{1,0:T(8,128)(2,1)S(1)}) fusion(bf16[1,320,4096]{2,1,0:T(8,128)(2,1)} %param.5, s32[]{:T(128)S(6)} %select_n.85, s32[]{:T(128)S(6)} %select_n.83, s32[]{:T(128)S(6)} %select_n.82, s32[]{:T(128)S(6)} %select_n.84), kind=kLoop, calls=%fused_computation.12 | loop fusion | bytes 5242896 | tf_op jit(solution)/shard_map/dynamic_slice | solution.py:114
  1.9 3.8 %collective-permute-start.2 = (bf16[320,1024]{1,0:T(8,128)(2,1)S(1)}, bf16[320,1024]{1,0:T(8,128)(2,1)S(1)}, u32[]{:S(2)}, u32[]{:S(2)}) collective-permute-start(bf16[320,1024]{1,0:T(8,128)(2,1)S(1)} %get-tuple-element.22), channel_id=1, source_target_pairs={{0,16},{1,17},{2,18},{3,19},{4,20},{5,21},{6,22},{7,23},{8,24},{9,... | collective-permute-start | bytes 1966088 | tf_op jit(solution)/shard_map/ppermute | solution.py:95
  6.1 2.3 %collective-permute-start.1 = (bf16[320,1024]{1,0:T(8,128)(2,1)S(1)}, bf16[320,1024]{1,0:T(8,128)(2,1)S(1)}, u32[]{:S(2)}, u32[]{:S(2)}) collective-permute-start(bf16[320,1024]{1,0:T(8,128)(2,1)S(1)} %get-tuple-element.20), channel_id=1, source_target_pairs={{0,24},{1,25},{2,26},{3,27},{4,28},{5,29},{6,30},{7,31},{8,0},{9,1... | collective-permute-start | bytes 1966088 | tf_op jit(solution)/shard_map/ppermute | solution.py:95
  8.4 5.6 %collective-permute-start.4 = (bf16[320,1024]{1,0:T(8,128)(2,1)S(1)}, bf16[320,1024]{1,0:T(8,128)(2,1)S(1)}, u32[]{:S(2)}, u32[]{:S(2)}) collective-permute-start(bf16[320,1024]{1,0:T(8,128)(2,1)S(1)} %get-tuple-element.21.refs_0_), channel_id=1, source_target_pairs={{0,224},{1,225},{2,226},{3,227},{4,228},{5,229},{6,230},{7,231},{8... | collective-permute-start | bytes 1966088 | tf_op jit(solution)/shard_map/ppermute | solution.py:95
  14.0 5.2 %collective-permute-done.2.refs_2_ = bf16[320,1024]{1,0:T(8,128)(2,1)S(1)} collective-permute-done((bf16[320,1024]{1,0:T(8,128)(2,1)S(1)}, bf16[320,1024]{1,0:T(8,128)(2,1)S(1)}, u32[]{:S(2)}, u32[]{:S(2)}) %collective-permute-start.2) | collective-permute-done | bytes 655392 | tf_op jit(solution)/shard_map/ppermute | solution.py:95
  19.3 2.4 %collective-permute-start.10 = (bf16[320,1024]{1,0:T(8,128)(2,1)S(1)}, bf16[320,1024]{1,0:T(8,128)(2,1)S(1)}, u32[]{:S(2)}, u32[]{:S(2)}) collective-permute-start(bf16[320,1024]{1,0:T(8,128)(2,1)S(1)} %collective-permute-done.2.refs_2_), channel_id=1, source_target_pairs={{0,32},{1,33},{2,34},{3,35},{4,36},{5,37},{6,38},{7,39},{8,40},{9,... | collective-permute-start | bytes 1966088 | tf_op jit(solution)/shard_map/ppermute | solution.py:95
  21.6 13.3 %collective-permute-done.3.refs_3_ = bf16[320,1024]{1,0:T(8,128)(2,1)S(1)} collective-permute-done((bf16[320,1024]{1,0:T(8,128)(2,1)S(1)}, bf16[320,1024]{1,0:T(8,128)(2,1)S(1)}, u32[]{:S(2)}, u32[]{:S(2)}) %collective-permute-start.3) | collective-permute-done | bytes 655392 | tf_op jit(solution)/shard_map/ppermute | solution.py:95
  35.0 5.6 %collective-permute-start.6 = (bf16[320,1024]{1,0:T(8,128)(2,1)S(1)}, bf16[320,1024]{1,0:T(8,128)(2,1)}, u32[]{:S(2)}, u32[]{:S(2)}) collective-permute-start(bf16[320,1024]{1,0:T(8,128)(2,1)S(1)} %collective-permute-done.2.refs_2_), channel_id=1, source_target_pairs={{0,224},{1,225},{2,226},{3,227},{4,228},{5,229},{6,230},{7,231},{8... | collective-permute-start | bytes 1966088 | tf_op jit(solution)/shard_map/ppermute | solution.py:95
  40.6 2.7 %collective-permute-start.5 = (bf16[320,1024]{1,0:T(8,128)(2,1)S(1)}, bf16[320,1024]{1,0:T(8,128)(2,1)}, u32[]{:S(2)}, u32[]{:S(2)}) collective-permute-start(bf16[320,1024]{1,0:T(8,128)(2,1)S(1)} %collective-permute-done.1.refs_1_), channel_id=1, source_target_pairs={{0,224},{1,225},{2,226},{3,227},{4,228},{5,229},{6,230},{7,231},{8... | collective-permute-start | bytes 1966088 | tf_op jit(solution)/shard_map/ppermute | solution.py:95
  45.0 1.5 collective-permute-start.9
  47.9 10.8 %collective-permute-done.11.refs_11_ = bf16[320,1024]{1,0:T(8,128)(2,1)} collective-permute-done((bf16[320,1024]{1,0:T(8,128)(2,1)S(1)}, bf16[320,1024]{1,0:T(8,128)(2,1)}, u32[]{:S(2)}, u32[]{:S(2)}) %collective-permute-start.11) | collective-permute-done | bytes 655392 | tf_op jit(solution)/shard_map/ppermute | solution.py:95
  58.7 9.6 %collective-permute-done.5.refs_5_ = bf16[320,1024]{1,0:T(8,128)(2,1)} collective-permute-done((bf16[320,1024]{1,0:T(8,128)(2,1)S(1)}, bf16[320,1024]{1,0:T(8,128)(2,1)}, u32[]{:S(2)}, u32[]{:S(2)}) %collective-permute-start.5) | collective-permute-done | bytes 655392 | tf_op jit(solution)/shard_map/ppermute | solution.py:95
  68.3 14.0 %collective-permute-done.7.refs_7_ = bf16[320,1024]{1,0:T(8,128)(2,1)} collective-permute-done((bf16[320,1024]{1,0:T(8,128)(2,1)S(1)}, bf16[320,1024]{1,0:T(8,128)(2,1)}, u32[]{:S(2)}, u32[]{:S(2)}) %collective-permute-start.7) | collective-permute-done | bytes 655392 | tf_op jit(solution)/shard_map/ppermute | solution.py:95
  84.5 14.6 %shard_map.55 = (f32[4,4,160,640]{3,2,1,0:T(8,128)}, bf16[4,4,160,640]{3,2,1,0:T(8,128)(2,1)}) custom-call(s32[2]{0:T(128)S(1)} %pad_add_fusion.place_ref, f32[1,1024]{1,0:T(1,128)S(1)} %divide_multiply_fusion.factor_ref, bf16[320,1024]{1,0:T(8,128)(2,1)S(1)} %get-tuple-element.21.refs_0_, bf16[320,1024]{1,0:T(8,128)(2,1)S(1)} %collective-permute-done.1.refs_1_, ...), custom_call_target="tpu_custom_call" | custom-call | flops 6710886400 | bytes 15728640 | tf_op jit(solution)/shard_map/pallas_call | solution.py:60
  100.5 5.7 %collective-permute-done.12 = bf16[4,4,160,640]{3,2,1,0:T(8,128)(2,1)S(1)} collective-permute-done((bf16[4,4,160,640]{3,2,1,0:T(8,128)(2,1)}, bf16[4,4,160,640]{3,2,1,0:T(8,128)(2,1)S(1)}, u32[]{:S(2)}, u32[]{:S(2)}) %collective-permute-start.12) | collective-permute-done | bytes 3276832 | tf_op jit(solution)/shard_map/ppermute | solution.py:95
  106.2 6.9 %fusion.20 = (bf16[4,4,160,640]{3,2,1,0:T(8,128)(2,1)S(1)}, f32[4,4,160,640]{3,2,1,0:T(8,128)}) fusion(f32[4,4,160,640]{3,2,1,0:T(8,128)} %get-tuple-element.7, bf16[4,4,160,640]{3,2,1,0:T(8,128)(2,1)S(1)} %collective-permute-done.12), kind=kLoop, calls=%fused_computation.53 | loop fusion | flops 4915200 | bytes 19660800 | tf_op jit(solution)/shard_map/convert.2
  113.7 2.2 %collective-permute-start.20 = (bf16[4,80,640]{2,1,0:T(8,128)(2,1)S(1)}, bf16[4,80,640]{2,1,0:T(8,128)(2,1)S(1)}, u32[]{:S(2)}, u32[]{:S(2)}) collective-permute-start(bf16[4,80,640]{2,1,0:T(8,128)(2,1)S(1)} %get-tuple-element.18), channel_id=1, source_target_pairs={{0,24},{1,25},{2,26},{3,27},{4,28},{5,29},{6,30},{7,31},{8,0},{9,1... | collective-permute-start | bytes 1228808 | tf_op jit(solution)/shard_map/ppermute | solution.py:95
  116.8 3.4 %collective-permute-start = (f32[8]{0:T(128)S(1)}, f32[8]{0:T(128)S(1)}, u32[]{:S(2)}, u32[]{:S(2)}) collective-permute-start(f32[8]{0:T(128)S(1)} %convert_reduce_fusion), channel_id=1, source_target_pairs={{0,8},{1,25},{2,234},{3,251},{4,244},{5,5},{6,22},{7,39},{8,16},{9... | collective-permute-start | bytes 104 | tf_op jit(solution)/shard_map/ppermute | solution.py:95
  120.3 4.3 %collective-permute-done = f32[8]{0:T(128)S(1)} collective-permute-done((f32[8]{0:T(128)S(1)}, f32[8]{0:T(128)S(1)}, u32[]{:S(2)}, u32[]{:S(2)}) %collective-permute-start) | collective-permute-done | bytes 64 | tf_op jit(solution)/shard_map/ppermute | solution.py:95
  125.8 2.2 %slice.79 = f32[4,4,80,640]{3,2,1,0:T(8,128)S(1)} slice(f32[4,4,160,640]{3,2,1,0:T(8,128)} %get-tuple-element.12), slice={[0:4], [0:4], [0:80], [0:640]} | slice | bytes 6553600 | tf_op jit(solution)/shard_map/slice | solution.py:146
  128.2 9.6 %collective-permute-start.13 = (bf16[4,80,640]{2,1,0:T(8,128)(2,1)S(1)}, bf16[4,80,640]{2,1,0:T(8,128)(2,1)S(1)}, u32[]{:S(2)}, u32[]{:S(2)}) collective-permute-start(bf16[4,80,640]{2,1,0:T(8,128)(2,1)S(1)} %get-tuple-element.13), channel_id=1, source_target_pairs={{0,2},{1,3},{2,4},{3,5},{4,6},{5,7},{6,0},{7,1},{8,10},{9,11},{10,... | collective-permute-start | bytes 1228808 | tf_op jit(solution)/shard_map/ppermute | solution.py:95
  137.8 1.9 collective-permute-start.15
  141.1 2.7 %collective-permute-start.23 = (bf16[80,640]{1,0:T(8,128)(2,1)S(1)}, bf16[80,640]{1,0:T(8,128)(2,1)S(1)}, u32[]{:S(2)}, u32[]{:S(2)}) collective-permute-start(bf16[80,640]{1,0:T(8,128)(2,1)S(1)} %get-tuple-element.25), channel_id=1, source_target_pairs={{0,6},{1,7},{2,0},{3,1},{4,2},{5,3},{6,4},{7,5},{8,14},{9,15},{10,... | collective-permute-start | bytes 307208 | tf_op jit(solution)/shard_map/ppermute | solution.py:95
  144.3 2.5 %collective-permute-start.24 = (bf16[80,640]{1,0:T(8,128)(2,1)S(1)}, bf16[80,640]{1,0:T(8,128)(2,1)S(1)}, u32[]{:S(2)}, u32[]{:S(2)}) collective-permute-start(bf16[80,640]{1,0:T(8,128)(2,1)S(1)} %get-tuple-element.24), channel_id=1, source_target_pairs={{0,4},{1,5},{2,6},{3,7},{4,0},{5,1},{6,2},{7,3},{8,12},{9,13},{10,... | collective-permute-start | bytes 307208 | tf_op jit(solution)/shard_map/ppermute | solution.py:95
  146.9 6.3 %collective-permute-done.15 = bf16[4,80,640]{2,1,0:T(8,128)(2,1)S(1)} collective-permute-done((bf16[4,80,640]{2,1,0:T(8,128)(2,1)S(1)}, bf16[4,80,640]{2,1,0:T(8,128)(2,1)S(1)}, u32[]{:S(2)}, u32[]{:S(2)}) %collective-permute-start.15) | collective-permute-done | bytes 409632 | tf_op jit(solution)/shard_map/ppermute | solution.py:95
  154.4 1.8 collective-permute-start.17
  156.2 6.2 %collective-permute-start.18 = (bf16[80,640]{1,0:T(8,128)(2,1)S(1)}, bf16[80,640]{1,0:T(8,128)(2,1)S(1)}, u32[]{:S(2)}, u32[]{:S(2)}) collective-permute-start(bf16[80,640]{1,0:T(8,128)(2,1)S(1)} %get-tuple-element.35), channel_id=1, source_target_pairs={{0,16},{1,17},{2,18},{3,19},{4,20},{5,21},{6,22},{7,23},{8,24},{9,... | collective-permute-start | bytes 307208 | tf_op jit(solution)/shard_map/ppermute | solution.py:95
  163.4 1.7 collective-permute-done.18
  165.2 7.5 %collective-permute-start.25 = (f32[160,640]{1,0:T(8,128)S(1)}, f32[160,640]{1,0:T(8,128)S(1)}, u32[]{:S(2)}, u32[]{:S(2)}) collective-permute-start(f32[160,640]{1,0:T(8,128)S(1)} %maximum_select_fusion.1), channel_id=1, source_target_pairs={{0,254},{1,239},{2,28},{3,13},{8,6},{9,247},{10,36},{11,21},{16,14... | collective-permute-start | bytes 1228808 | tf_op jit(solution)/shard_map/ppermute | solution.py:95
  174.7 5.6 %collective-permute-start.28 = (f32[160,640]{1,0:T(8,128)S(1)}, f32[160,640]{1,0:T(8,128)S(1)}, u32[]{:S(2)}, u32[]{:S(2)}) collective-permute-start(f32[160,640]{1,0:T(8,128)S(1)} %maximum_select_fusion.1), channel_id=1, source_target_pairs={{0,33},{1,32},{2,35},{3,34},{8,41},{9,40},{10,43},{11,42},{16,49},... | collective-permute-start | bytes 1228808 | tf_op jit(solution)/shard_map/ppermute | solution.py:95
  181.5 4.6 %collective-permute-done.27 = f32[160,640]{1,0:T(8,128)S(1)} collective-permute-done((f32[160,640]{1,0:T(8,128)S(1)}, f32[160,640]{1,0:T(8,128)S(1)}, u32[]{:S(2)}, u32[]{:S(2)}) %collective-permute-start.27) | collective-permute-done | bytes 409632 | tf_op jit(solution)/shard_map/ppermute | solution.py:95
  186.3 3.1 %collective-permute-done.28 = f32[160,640]{1,0:T(8,128)S(1)} collective-permute-done((f32[160,640]{1,0:T(8,128)S(1)}, f32[160,640]{1,0:T(8,128)S(1)}, u32[]{:S(2)}, u32[]{:S(2)}) %collective-permute-start.28) | collective-permute-done | bytes 409632 | tf_op jit(solution)/shard_map/ppermute | solution.py:95
  (66 shorter events, 17.0 us)
Async XLA Ops:
  1.9 17.3 %collective-permute-start.2 = (bf16[320,1024]{1,0:T(8,128)(2,1)S(1)}, bf16[320,1024]{1,0:T(8,128)(2,1)S(1)}, u32[]{:S(2)}, u32[]{:S(2)}) collective-permute-start(bf16[320,1024]{1,0:T(8,128)(2,1)S(1)} %get-tuple-element.22), channel_id=1, source_target_pairs={{0,16},{1,17},{2,18},{3,19},{4,20},{5,21},{6,22},{7,23},{8,24},{9,... | collective-permute-start | bytes 1966088 | tf_op jit(solution)/shard_map/ppermute | solution.py:95
  5.7 29.2 %collective-permute-start.3 = (bf16[320,1024]{1,0:T(8,128)(2,1)S(1)}, bf16[320,1024]{1,0:T(8,128)(2,1)S(1)}, u32[]{:S(2)}, u32[]{:S(2)}) collective-permute-start(bf16[320,1024]{1,0:T(8,128)(2,1)S(1)} %get-tuple-element.19), channel_id=1, source_target_pairs={{0,8},{1,9},{2,10},{3,11},{4,12},{5,13},{6,14},{7,15},{8,16},{9,17... | collective-permute-start | bytes 1966088 | tf_op jit(solution)/shard_map/ppermute | solution.py:95
  6.1 34.5 %collective-permute-start.1 = (bf16[320,1024]{1,0:T(8,128)(2,1)S(1)}, bf16[320,1024]{1,0:T(8,128)(2,1)S(1)}, u32[]{:S(2)}, u32[]{:S(2)}) collective-permute-start(bf16[320,1024]{1,0:T(8,128)(2,1)S(1)} %get-tuple-element.20), channel_id=1, source_target_pairs={{0,24},{1,25},{2,26},{3,27},{4,28},{5,29},{6,30},{7,31},{8,0},{9,1... | collective-permute-start | bytes 1966088 | tf_op jit(solution)/shard_map/ppermute | solution.py:95
  8.4 32.2 %collective-permute-start.4 = (bf16[320,1024]{1,0:T(8,128)(2,1)S(1)}, bf16[320,1024]{1,0:T(8,128)(2,1)S(1)}, u32[]{:S(2)}, u32[]{:S(2)}) collective-permute-start(bf16[320,1024]{1,0:T(8,128)(2,1)S(1)} %get-tuple-element.21.refs_0_), channel_id=1, source_target_pairs={{0,224},{1,225},{2,226},{3,227},{4,228},{5,229},{6,230},{7,231},{8... | collective-permute-start | bytes 1966088 | tf_op jit(solution)/shard_map/ppermute | solution.py:95
  14.0 29.3 %collective-permute-start.8 = (bf16[320,1024]{1,0:T(8,128)(2,1)S(1)}, bf16[320,1024]{1,0:T(8,128)(2,1)S(1)}, u32[]{:S(2)}, u32[]{:S(2)}) collective-permute-start(bf16[320,1024]{1,0:T(8,128)(2,1)S(1)} %get-tuple-element.21.refs_0_), channel_id=1, source_target_pairs={{0,32},{1,33},{2,34},{3,35},{4,36},{5,37},{6,38},{7,39},{8,40},{9,... | collective-permute-start | bytes 1966088 | tf_op jit(solution)/shard_map/ppermute | solution.py:95
  19.3 24.9 %collective-permute-start.10 = (bf16[320,1024]{1,0:T(8,128)(2,1)S(1)}, bf16[320,1024]{1,0:T(8,128)(2,1)S(1)}, u32[]{:S(2)}, u32[]{:S(2)}) collective-permute-start(bf16[320,1024]{1,0:T(8,128)(2,1)S(1)} %collective-permute-done.2.refs_2_), channel_id=1, source_target_pairs={{0,32},{1,33},{2,34},{3,35},{4,36},{5,37},{6,38},{7,39},{8,40},{9,... | collective-permute-start | bytes 1966088 | tf_op jit(solution)/shard_map/ppermute | solution.py:95
  35.0 33.3 %collective-permute-start.6 = (bf16[320,1024]{1,0:T(8,128)(2,1)S(1)}, bf16[320,1024]{1,0:T(8,128)(2,1)}, u32[]{:S(2)}, u32[]{:S(2)}) collective-permute-start(bf16[320,1024]{1,0:T(8,128)(2,1)S(1)} %collective-permute-done.2.refs_2_), channel_id=1, source_target_pairs={{0,224},{1,225},{2,226},{3,227},{4,228},{5,229},{6,230},{7,231},{8... | collective-permute-start | bytes 1966088 | tf_op jit(solution)/shard_map/ppermute | solution.py:95
  40.6 18.1 %collective-permute-start.11 = (bf16[320,1024]{1,0:T(8,128)(2,1)S(1)}, bf16[320,1024]{1,0:T(8,128)(2,1)}, u32[]{:S(2)}, u32[]{:S(2)}) collective-permute-start(bf16[320,1024]{1,0:T(8,128)(2,1)S(1)} %collective-permute-done.3.refs_3_), channel_id=1, source_target_pairs={{0,32},{1,33},{2,34},{3,35},{4,36},{5,37},{6,38},{7,39},{8,40},{9,... | collective-permute-start | bytes 1966088 | tf_op jit(solution)/shard_map/ppermute | solution.py:95
  40.6 27.6 %collective-permute-start.5 = (bf16[320,1024]{1,0:T(8,128)(2,1)S(1)}, bf16[320,1024]{1,0:T(8,128)(2,1)}, u32[]{:S(2)}, u32[]{:S(2)}) collective-permute-start(bf16[320,1024]{1,0:T(8,128)(2,1)S(1)} %collective-permute-done.1.refs_1_), channel_id=1, source_target_pairs={{0,224},{1,225},{2,226},{3,227},{4,228},{5,229},{6,230},{7,231},{8... | collective-permute-start | bytes 1966088 | tf_op jit(solution)/shard_map/ppermute | solution.py:95
  44.1 38.2 %collective-permute-start.7 = (bf16[320,1024]{1,0:T(8,128)(2,1)S(1)}, bf16[320,1024]{1,0:T(8,128)(2,1)}, u32[]{:S(2)}, u32[]{:S(2)}) collective-permute-start(bf16[320,1024]{1,0:T(8,128)(2,1)S(1)} %collective-permute-done.3.refs_3_), channel_id=1, source_target_pairs={{0,224},{1,225},{2,226},{3,227},{4,228},{5,229},{6,230},{7,231},{8... | collective-permute-start | bytes 1966088 | tf_op jit(solution)/shard_map/ppermute | solution.py:95
  45.0 37.3 %collective-permute-start.9 = (bf16[320,1024]{1,0:T(8,128)(2,1)S(1)}, bf16[320,1024]{1,0:T(8,128)(2,1)}, u32[]{:S(2)}, u32[]{:S(2)}) collective-permute-start(bf16[320,1024]{1,0:T(8,128)(2,1)S(1)} %collective-permute-done.1.refs_1_), channel_id=1, source_target_pairs={{0,32},{1,33},{2,34},{3,35},{4,36},{5,37},{6,38},{7,39},{8,40},{9,... | collective-permute-start | bytes 1966088 | tf_op jit(solution)/shard_map/ppermute | solution.py:95
  82.3 1.1 copy-start.1
  83.4 1.1 copy-start.3
  99.1 7.0 %collective-permute-start.12 = (bf16[4,4,160,640]{3,2,1,0:T(8,128)(2,1)}, bf16[4,4,160,640]{3,2,1,0:T(8,128)(2,1)S(1)}, u32[]{:S(2)}, u32[]{:S(2)}) collective-permute-start(bf16[4,4,160,640]{3,2,1,0:T(8,128)(2,1)} %get-tuple-element.8), channel_id=1, source_target_pairs={{0,1},{1,0},{2,3},{3,2},{4,5},{5,4},{6,7},{7,6},{8,9},{9,8},{10,11... | collective-permute-start | bytes 9830408 | tf_op jit(solution)/shard_map/ppermute | solution.py:95
  106.2 9.9 %copy-start.4 = (s32[1,8]{1,0:T(1,128)S(1)}, s32[1,8]{1,0:T(1,128)}, u32[]{:S(2)}) copy-start(s32[1,8]{1,0:T(1,128)} %param.8) | copy-start | bytes 100
  113.1 24.6 %collective-permute-start.19 = (bf16[4,80,640]{2,1,0:T(8,128)(2,1)S(1)}, bf16[4,80,640]{2,1,0:T(8,128)(2,1)S(1)}, u32[]{:S(2)}, u32[]{:S(2)}) collective-permute-start(bf16[4,80,640]{2,1,0:T(8,128)(2,1)S(1)} %get-tuple-element.16), channel_id=1, source_target_pairs={{0,8},{1,9},{2,10},{3,11},{4,12},{5,13},{6,14},{7,15},{8,16},{9,17... | collective-permute-start | bytes 1228808 | tf_op jit(solution)/shard_map/ppermute | solution.py:95
  113.7 26.0 %collective-permute-start.20 = (bf16[4,80,640]{2,1,0:T(8,128)(2,1)S(1)}, bf16[4,80,640]{2,1,0:T(8,128)(2,1)S(1)}, u32[]{:S(2)}, u32[]{:S(2)}) collective-permute-start(bf16[4,80,640]{2,1,0:T(8,128)(2,1)S(1)} %get-tuple-element.18), channel_id=1, source_target_pairs={{0,24},{1,25},{2,26},{3,27},{4,28},{5,29},{6,30},{7,31},{8,0},{9,1... | collective-permute-start | bytes 1228808 | tf_op jit(solution)/shard_map/ppermute | solution.py:95
  115.9 23.8 %collective-permute-start.21 = (bf16[4,80,640]{2,1,0:T(8,128)(2,1)S(1)}, bf16[4,80,640]{2,1,0:T(8,128)(2,1)S(1)}, u32[]{:S(2)}, u32[]{:S(2)}) collective-permute-start(bf16[4,80,640]{2,1,0:T(8,128)(2,1)S(1)} %get-tuple-element.17), channel_id=1, source_target_pairs={{0,16},{1,17},{2,18},{3,19},{4,20},{5,21},{6,22},{7,23},{8,24},{9,... | collective-permute-start | bytes 1228808 | tf_op jit(solution)/shard_map/ppermute | solution.py:95
  116.8 7.8 %collective-permute-start = (f32[8]{0:T(128)S(1)}, f32[8]{0:T(128)S(1)}, u32[]{:S(2)}, u32[]{:S(2)}) collective-permute-start(f32[8]{0:T(128)S(1)} %convert_reduce_fusion), channel_id=1, source_target_pairs={{0,8},{1,25},{2,234},{3,251},{4,244},{5,5},{6,22},{7,39},{8,16},{9... | collective-permute-start | bytes 104 | tf_op jit(solution)/shard_map/ppermute | solution.py:95
  128.2 16.1 %collective-permute-start.13 = (bf16[4,80,640]{2,1,0:T(8,128)(2,1)S(1)}, bf16[4,80,640]{2,1,0:T(8,128)(2,1)S(1)}, u32[]{:S(2)}, u32[]{:S(2)}) collective-permute-start(bf16[4,80,640]{2,1,0:T(8,128)(2,1)S(1)} %get-tuple-element.13), channel_id=1, source_target_pairs={{0,2},{1,3},{2,4},{3,5},{4,6},{5,7},{6,0},{7,1},{8,10},{9,11},{10,... | collective-permute-start | bytes 1228808 | tf_op jit(solution)/shard_map/ppermute | solution.py:95
  137.8 9.1 %collective-permute-start.14 = (bf16[4,80,640]{2,1,0:T(8,128)(2,1)S(1)}, bf16[4,80,640]{2,1,0:T(8,128)(2,1)S(1)}, u32[]{:S(2)}, u32[]{:S(2)}) collective-permute-start(bf16[4,80,640]{2,1,0:T(8,128)(2,1)S(1)} %get-tuple-element.14), channel_id=1, source_target_pairs={{0,6},{1,7},{2,0},{3,1},{4,2},{5,3},{6,4},{7,5},{8,14},{9,15},{10,... | collective-permute-start | bytes 1228808 | tf_op jit(solution)/shard_map/ppermute | solution.py:95
  137.8 15.4 %collective-permute-start.15 = (bf16[4,80,640]{2,1,0:T(8,128)(2,1)S(1)}, bf16[4,80,640]{2,1,0:T(8,128)(2,1)S(1)}, u32[]{:S(2)}, u32[]{:S(2)}) collective-permute-start(bf16[4,80,640]{2,1,0:T(8,128)(2,1)S(1)} %get-tuple-element.15), channel_id=1, source_target_pairs={{0,4},{1,5},{2,6},{3,7},{4,0},{5,1},{6,2},{7,3},{8,12},{9,13},{10,... | collective-permute-start | bytes 1228808 | tf_op jit(solution)/shard_map/ppermute | solution.py:95
  141.0 15.1 %collective-permute-start.22 = (bf16[80,640]{1,0:T(8,128)(2,1)S(1)}, bf16[80,640]{1,0:T(8,128)(2,1)S(1)}, u32[]{:S(2)}, u32[]{:S(2)}) collective-permute-start(bf16[80,640]{1,0:T(8,128)(2,1)S(1)} %get-tuple-element.23), channel_id=1, source_target_pairs={{0,2},{1,3},{2,4},{3,5},{4,6},{5,7},{6,0},{7,1},{8,10},{9,11},{10,... | collective-permute-start | bytes 307208 | tf_op jit(solution)/shard_map/ppermute | solution.py:95
  141.1 21.2 %collective-permute-start.23 = (bf16[80,640]{1,0:T(8,128)(2,1)S(1)}, bf16[80,640]{1,0:T(8,128)(2,1)S(1)}, u32[]{:S(2)}, u32[]{:S(2)}) collective-permute-start(bf16[80,640]{1,0:T(8,128)(2,1)S(1)} %get-tuple-element.25), channel_id=1, source_target_pairs={{0,6},{1,7},{2,0},{3,1},{4,2},{5,3},{6,4},{7,5},{8,14},{9,15},{10,... | collective-permute-start | bytes 307208 | tf_op jit(solution)/shard_map/ppermute | solution.py:95
  144.3 18.0 %collective-permute-start.24 = (bf16[80,640]{1,0:T(8,128)(2,1)S(1)}, bf16[80,640]{1,0:T(8,128)(2,1)S(1)}, u32[]{:S(2)}, u32[]{:S(2)}) collective-permute-start(bf16[80,640]{1,0:T(8,128)(2,1)S(1)} %get-tuple-element.24), channel_id=1, source_target_pairs={{0,4},{1,5},{2,6},{3,7},{4,0},{5,1},{6,2},{7,3},{8,12},{9,13},{10,... | collective-permute-start | bytes 307208 | tf_op jit(solution)/shard_map/ppermute | solution.py:95
  153.4 9.0 %collective-permute-start.16 = (bf16[80,640]{1,0:T(8,128)(2,1)S(1)}, bf16[80,640]{1,0:T(8,128)(2,1)S(1)}, u32[]{:S(2)}, u32[]{:S(2)}) collective-permute-start(bf16[80,640]{1,0:T(8,128)(2,1)S(1)} %get-tuple-element.34), channel_id=1, source_target_pairs={{0,8},{1,9},{2,10},{3,11},{4,12},{5,13},{6,14},{7,15},{8,16},{9,17... | collective-permute-start | bytes 307208 | tf_op jit(solution)/shard_map/ppermute | solution.py:95
  154.4 9.0 %collective-permute-start.17 = (bf16[80,640]{1,0:T(8,128)(2,1)S(1)}, bf16[80,640]{1,0:T(8,128)(2,1)S(1)}, u32[]{:S(2)}, u32[]{:S(2)}) collective-permute-start(bf16[80,640]{1,0:T(8,128)(2,1)S(1)} %get-tuple-element.36), channel_id=1, source_target_pairs={{0,24},{1,25},{2,26},{3,27},{4,28},{5,29},{6,30},{7,31},{8,0},{9,1... | collective-permute-start | bytes 307208 | tf_op jit(solution)/shard_map/ppermute | solution.py:95
  156.2 9.0 %collective-permute-start.18 = (bf16[80,640]{1,0:T(8,128)(2,1)S(1)}, bf16[80,640]{1,0:T(8,128)(2,1)S(1)}, u32[]{:S(2)}, u32[]{:S(2)}) collective-permute-start(bf16[80,640]{1,0:T(8,128)(2,1)S(1)} %get-tuple-element.35), channel_id=1, source_target_pairs={{0,16},{1,17},{2,18},{3,19},{4,20},{5,21},{6,22},{7,23},{8,24},{9,... | collective-permute-start | bytes 307208 | tf_op jit(solution)/shard_map/ppermute | solution.py:95
  165.2 15.1 %collective-permute-start.25 = (f32[160,640]{1,0:T(8,128)S(1)}, f32[160,640]{1,0:T(8,128)S(1)}, u32[]{:S(2)}, u32[]{:S(2)}) collective-permute-start(f32[160,640]{1,0:T(8,128)S(1)} %maximum_select_fusion.1), channel_id=1, source_target_pairs={{0,254},{1,239},{2,28},{3,13},{8,6},{9,247},{10,36},{11,21},{16,14... | collective-permute-start | bytes 1228808 | tf_op jit(solution)/shard_map/ppermute | solution.py:95
  172.7 8.1 %collective-permute-start.26 = (f32[160,640]{1,0:T(8,128)S(1)}, f32[160,640]{1,0:T(8,128)S(1)}, u32[]{:S(2)}, u32[]{:S(2)}) collective-permute-start(f32[160,640]{1,0:T(8,128)S(1)} %maximum_select_fusion.1), channel_id=1, source_target_pairs={{4,20},{5,5},{6,246},{7,231},{12,28},{13,13},{14,254},{15,239},{20... | collective-permute-start | bytes 1228808 | tf_op jit(solution)/shard_map/ppermute | solution.py:95
  173.4 12.7 %collective-permute-start.27 = (f32[160,640]{1,0:T(8,128)S(1)}, f32[160,640]{1,0:T(8,128)S(1)}, u32[]{:S(2)}, u32[]{:S(2)}) collective-permute-start(f32[160,640]{1,0:T(8,128)S(1)} %maximum_select_fusion.1), channel_id=1, source_target_pairs={{4,35},{5,34},{6,33},{7,32},{12,43},{13,42},{14,41},{15,40},{20,51... | collective-permute-start | bytes 1228808 | tf_op jit(solution)/shard_map/ppermute | solution.py:95
  174.7 14.6 %collective-permute-start.28 = (f32[160,640]{1,0:T(8,128)S(1)}, f32[160,640]{1,0:T(8,128)S(1)}, u32[]{:S(2)}, u32[]{:S(2)}) collective-permute-start(f32[160,640]{1,0:T(8,128)S(1)} %maximum_select_fusion.1), channel_id=1, source_target_pairs={{0,33},{1,32},{2,35},{3,34},{8,41},{9,40},{10,43},{11,42},{16,49},... | collective-permute-start | bytes 1228808 | tf_op jit(solution)/shard_map/ppermute | solution.py:95
  (2 other events, 1.7 us)

commit v2 on v1

v2 whole, which is shorter than its diff:
```python
import functools

import jax
import jax.numpy as jnp
from jax import lax
from jax.experimental import pallas as pl
from jax.experimental.pallas import tpu as pltpu
from jax.sharding import PartitionSpec as P


EPSILON = 1e-08
AXES = ("ex", "ckpt")
NY = 4
CHUNK = 32


def scale_into(left_ref, piece_ref, factor_ref, start):
    @pl.loop(0, piece_ref.shape[0] // CHUNK)
    def _(step):
        source = pl.ds(pl.multiple_of(step * CHUNK, CHUNK), CHUNK)
        target = pl.ds(pl.multiple_of(start + step * CHUNK, CHUNK), CHUNK)
        piece = piece_ref[source, :].astype(jnp.float32)
        left_ref[target, :] = (piece * factor_ref[...]).astype(jnp.bfloat16)


def fill(out_ref, index, tile):
    half = tile.shape[0] // 2
    rows = tile.shape[1]
    out_ref[index, :, 0:rows] = tile[:half].astype(out_ref.dtype)
    out_ref[index, :, rows : 2 * rows] = tile[half:].astype(out_ref.dtype)


def product_of(right, left):
    return lax.dot_general(right, left, (((1,), (1,)), ((), ())), preferred_element_type=jnp.float32)


def owner(far, p):
    return jnp.where(far == 1, 3 * p, 1 + p)


def tiles_kernel(late, place_ref, factor_ref, *refs):
    if late:
        right_in, last_below, left_in = refs[0:4], refs[4], refs[5]
        keep_ref, give_ref, right_ref, left_ref, piece_ref, sems = refs[6:]
        loads = [(right_in[rel], right_ref.at[rel]) for rel in (2, 0, 1, 3)]
        loads += [(last_below, piece_ref.at[0]), (left_in, left_ref)]
    else:
        right_in, rest = refs[0:3], refs[3:10]
        left_out, keep_ref, give_ref, right_ref, left_ref, piece_ref, sems = refs[10:]
        loads = [(ref, right_ref.at[rel]) for rel, ref in zip((0, 1, 3), right_in)]
        loads += [(ref, piece_ref.at[i]) for i, ref in enumerate(rest)]
    rows = right_ref.shape[1]
    y = place_ref[0]
    c = place_ref[1]
    copies = [pltpu.make_async_copy(source, target, sems.at[i]) for i, (source, target) in enumerate(loads)]
    for copy in copies:
        copy.start()
    for copy in copies:
        copy.wait()
    if late:
        groups = ((0, 2, piece_ref.at[0]), (2, 2, right_ref.at[2]))
    else:
        groups = tuple((2, rel, right_ref.at[rel]) for rel in (0, 1, 3))
        groups += tuple((1, rel, piece_ref.at[rel]) for rel in range(NY))
        groups += tuple((0, rel, piece_ref.at[NY + i]) for i, rel in enumerate((0, 1, 3)))
    for plane, rel, ref in groups:
        scale_into(left_ref, ref, factor_ref, (plane * NY + lax.rem(y + rel, NY)) * rows)
    if not late:
        store = pltpu.make_async_copy(left_ref, left_out, sems.at[len(loads)])
        store.start()

    def start_of(r, offset):
        return pl.multiple_of((lax.rem(y + r, NY) + 2 * NY - offset) * rows, CHUNK)

    @pl.loop(0, 4)
    def _(turn):
        far = turn // 2
        given = lax.rem(turn, 2)
        core = jnp.where(given == 1, 1 - c, c)
        lowest = 4 * far + 2 * core + 1

        def one(slot, r, p):
            tile = product_of(right_ref[r], left_ref[pl.ds(start_of(r, lowest + p), rows), :])
            place(slot, p, tile)

        def place(slot, p, tile):
            index = slot * 4 + owner(far, p) if late else owner(far, p) * 2 + slot

            @pl.when(given == 0)
            def _():
                fill(keep_ref, index, tile)

            @pl.when(given == 1)
            def _():
                fill(give_ref, index, tile)

        if late:
            pair = product_of(right_ref[2], left_ref[pl.ds(start_of(2, lowest + 1), 2 * rows), :])
            place(0, 1, pair[:, :rows])
            place(0, 0, pair[:, rows:])
            one(1, jnp.where(core == 0, 3, 1), 0)
            one(1, 0, 1)
        else:
            one(0, 0, 0)
            one(0, 3, 1)
            one(1, jnp.where(core == 0, 1, 3), 0)
            one(1, 1, 1)

    if not late:
        store.wait()


def tiles(late, place, factor, *arrays):
    rows, width = arrays[0].shape
    half = rows // 2
    vmem = pl.BlockSpec(memory_space=pltpu.VMEM)
    hbm = pl.BlockSpec(memory_space=pltpu.HBM)
    left = [] if late else [jax.ShapeDtypeStruct((3 * NY * rows, width), jnp.bfloat16)]
    shapes = left + [
        jax.ShapeDtypeStruct((8, half, 2 * rows), jnp.float32),
        jax.ShapeDtypeStruct((8, half, 2 * rows), jnp.bfloat16),
    ]
    *left, keep, give = pl.pallas_call(
        functools.partial(tiles_kernel, late),
        in_specs=[pl.BlockSpec(memory_space=pltpu.SMEM), vmem] + [hbm] * len(arrays),
        out_specs=[hbm] * len(left) + [vmem] * 2,
        out_shape=shapes,
        scratch_shapes=[
            pltpu.VMEM((NY, rows, width), jnp.bfloat16),
            pltpu.VMEM((3 * NY * rows, width), jnp.bfloat16),
            pltpu.VMEM((1 if late else 7, rows, width), jnp.bfloat16),
            pltpu.SemaphoreType.DMA((11,)),
        ],
        compiler_params=pltpu.CompilerParams(vmem_limit_bytes=26 * 2**20),
        cost_estimate=pl.CostEstimate(
            flops=32 * rows * rows * width, bytes_accessed=12 * rows * width * 2, transcendentals=0
        ),
    )(place, factor, *arrays)
    shape = (2, 4, half, 2 * rows) if late else (4, 2, half, 2 * rows)
    return (*left, keep.reshape(shape), give.reshape(shape))


def local_fn(blocks):
    def flat(e, x, c):
        return (e % blocks) * 8 + (x % 4) * 2 + c

    def ring(e, by):
        return e - e % NY + (e + by) % NY

    def send(value, move):
        pairs = []
        for e in range(blocks):
            for x in range(4):
                for c in range(2):
                    target = move(e, x, c)
                    if target is not None:
                        pairs.append((flat(e, x, c), flat(*target)))
        return lax.ppermute(value, AXES, pairs)

    def offset_of(x, c):
        return (4 if x in (0, 3) else 0) + 2 * c + 1 + (1 if x >= 2 else 0)

    def local(grads, second_moment, step_size, partners, counts):
        width = grads.shape[2]
        rows = grads.shape[1]
        reach = partners.shape[1]
        quarter = width // NY
        part = rows // 4
        e = lax.axis_index("ex")
        k = lax.axis_index("ckpt")
        y = lax.rem(e, NY)
        x = k // 2
        c = lax.rem(k, 2)
        own = grads[0]

        def cut(index):
            return lax.dynamic_slice_in_dim(own, lax.rem(index, NY) * quarter, quarter, 1)

        here = [None] * NY
        above = [None] * NY
        below = [None] * NY
        here[0] = lax.optimization_barrier(cut(y))
        for s in (1, 3, 2):
            here[NY - s] = send(cut(y + s), lambda e, x, c, s=s: (ring(e, s), x, c))
        for r in (0, 3, 1, 2):
            above[r] = send(here[r], lambda e, x, c: (e - NY, x, c))
            below[r] = send(here[r], lambda e, x, c: (e + NY, x, c))

        offsets = jnp.mod(partners[0] - e, blocks)
        alive = jnp.arange(reach, dtype=jnp.int32) < counts[0]
        wanted = jnp.arange(1, reach + 1, dtype=jnp.int32)
        matched = jnp.logical_and(offsets[:, None] == wanted[None, :], alive[:, None])
        listed = jnp.sum(matched.astype(jnp.float32), axis=0)
        listed = send(listed, lambda e, x, c: (e + offset_of(x, c) - NY, x, c))
        is_far = jnp.logical_or(x == 0, x == 3)
        offset = jnp.where(is_far, NY, 0) + 2 * c + 1 + jnp.where(x >= 2, 1, 0)
        weight = lax.dynamic_slice_in_dim(listed, offset - 1, 1, 0)[0]

        factor = step_size[:, None] / (jnp.sqrt(second_moment) + EPSILON) * width ** (-0.5)
        factor = lax.dynamic_slice_in_dim(factor, y * quarter, quarter, 1)
        place = jnp.stack([y, c])
        left, keep, give = tiles(
            False, place, factor, above[0], above[1], above[3], *here, below[0], below[1], below[3]
        )

        def low_of(x):
            return x < 2

        def pick(array, index, axis):
            return lax.dynamic_index_in_dim(array, lax.rem(index, 4), axis, keepdims=False)

        def narrow(value):
            return value.astype(jnp.bfloat16)

        def wide(value):
            return value.astype(jnp.float32)

        given = send(give, lambda e, x, c: (e, x, 1 - c))
        total = keep + wide(given)
        early = pick(total, x, 0)
        arrived_early = [send(narrow(pick(total, x + t, 0)), lambda e, x, c, t=t: (e, x + t, c)) for t in (1, 3, 2)]
        keep, give = tiles(True, place, factor, *above, below[2], left)
        given = send(give, lambda e, x, c: (e, x, 1 - c))
        total = keep + wide(given)

        def rest(e, c):
            return ring(e, 3 if c == 0 else 1)

        upper, lower = total[:, :, :part], total[:, :, part:]
        by2 = send(narrow(lower[0]), lambda e, x, c: (ring(e, 2), x, c))
        by1 = send(narrow(lower[1, :2]), lambda e, x, c: (rest(e, c), x, c))
        upper_own = pick(upper, x, 1)
        arrived = [send(narrow(pick(upper, x + t, 1)), lambda e, x, c, t=t: (e, x + t, c)) for t in (1, 3, 2)]
        arrived_early, arrived[0] = lax.optimization_barrier((arrived_early, arrived[0]))
        for value in arrived_early:
            early = early + wide(value)
        low = low_of(x)
        final = jnp.where(low, early[0], 0.0)
        final = final + wide(send(narrow(early[1]), lambda e, x, c: (ring(e, 3 if low_of(x) and c == 1 else 1), x, c)))
        final = final + wide(send(narrow(early[0]), lambda e, x, c: None if low_of(x) else (ring(e, 3), x, c)))
        lower_own = wide(by2) + jnp.concatenate([wide(by1), lower[1, 2:]], axis=0)
        bottom = pick(lower_own, x, 0)
        bottom_arrived = [
            send(narrow(pick(lower_own, x + t, 0)), lambda e, x, c, t=t: (e, x + t, c)) for t in (1, 3, 2)
        ]
        for value in arrived:
            upper_own = upper_own + wide(value)
        ay2 = send(narrow(upper_own[0]), lambda e, x, c: (ring(e, 2), x, c))
        ay1 = send(narrow(upper_own[1]), lambda e, x, c: (rest(e, c), x, c) if low_of(x) else None)
        top = jnp.where(low, 0.0, upper_own[1]) + wide(ay2) + wide(ay1)
        for value in bottom_arrived:
            bottom = bottom + wide(value)
        final = final + jnp.concatenate([top, bottom], axis=0)
        final = jnp.where(weight > 0, final, 0.0)

        def back(low):
            def move(e, x, c):
                if (x < 2) != low:
                    return None
                return (e + NY, 0 if x in (0, 3) else 1, 1 - c)

            return move

        def ahead(low):
            def move(e, x, c):
                if (x < 2) != low:
                    return None
                return (e + NY - offset_of(x, c), 3 if x in (0, 3) else 2, c)

            return move

        back_low = send(final, back(True))
        back_high = send(final, back(False))
        ahead_low = send(final, ahead(True))
        ahead_high = send(final, ahead(False))

        def later(tile):
            return jnp.concatenate([tile[:, :rows], tile[:, rows:]], axis=0)

        backward = jnp.concatenate([later(back_high), later(back_low)], axis=1)
        forward = jnp.concatenate([later(ahead_low), later(ahead_high)], axis=0)
        forward = jnp.concatenate([forward[:rows].T, forward[rows:].T], axis=1)
        return jnp.where(x >= 2, forward, backward)

    return local


def build(mesh):
    local = local_fn(mesh.shape["ex"])
    in_specs = (P("ckpt", "ex", None), P("ckpt", None), P("ckpt"), P("ex", None), P("ex"))
    return jax.shard_map(local, mesh=mesh, in_specs=in_specs, out_specs=P("ex", "ckpt"), check_vma=False)


def solution(mesh):
    return build(mesh)
```

time: 192 us -> 193 us (level)
  Pallas kernels: 14.6 us -> 29.8 us
  waiting for transfers between devices: 80.2 us -> 69.8 us
  starting transfers between devices: 72.6 us -> 76.7 us
  other arithmetic: 11 us -> 7.32 us
  local copies, waits for them, and re-layouts: 9.98 us -> 6.61 us
    pallas_call x1 -> x2, Pallas kernels: 14.6 us -> 29.8 us  [tiles(): pl.pallas_call(functools.partial(tiles_kernel, late), in_specs=[pl.BlockS...]
    ppermute x29 -> x33, waiting for transfers between devices: 80.2 us -> 69.8 us  [send(): return lax.ppermute(value, AXES, pairs)]
    another operation x3 -> x2, other arithmetic: 7.17 us -> 1.98 us
    ppermute x29 -> x33, starting transfers between devices: 72.6 us -> 76.7 us  [send(): return lax.ppermute(value, AXES, pairs)]
    slice x1, local copies, waits for them, and re-layouts: 2.19 us -> 0.11 us  [local(): upper, lower = (total[:, :, :part], total[:, :, part:])]
    unnamed x14 -> x8, local copies, waits for them, and re-layouts: 4.44 us -> 2.75 us
  transfers between devices with their start and end apart: 29 -> 33, of which waited for: 13 -> 11; matrix products, arithmetic and copies ran while one was open for 4% -> 4% of each run, Pallas kernels for 0% -> 15%
where the time goes in v2:
time: 193 us
  starting transfers between devices  76.7 us (40%)
  waiting for transfers between devices  69.8 us (36%)
  Pallas kernels  29.8 us (15%)
  other arithmetic  7.32 us (4%)
  local copies, waits for them, and re-layouts  6.61 us (3%)
  between operations  2.43 us (1%)
    ppermute x33, starting transfers between devices, send(): return lax.ppermute(value, AXES, pairs)  76.7 us
    ppermute x33, waiting for transfers between devices, send(): return lax.ppermute(value, AXES, pairs)  69.8 us
    pallas_call x2, Pallas kernels, tiles(): pl.pallas_call(functools.partial(tiles_kernel, late), in_specs=[pl.BlockS...  29.8 us
  transfers between devices with their start and end apart: 33, of which 11 were waited for; matrix products, arithmetic and copies ran while one was open for 4% of the time, Pallas kernels for 15%

profile of v2, /device:TPU:1, one launch (start us, length us, event | category | flops | bytes accessed | tf_op | source)
XLA Modules:
  0.0 192.7 jit_solution(18024969079491784299)
XLA Ops:
  0.0 1.9 dynamic-slice_bitcast_fusion.1
  1.9 3.6 %collective-permute-start.2 = (bf16[320,1024]{1,0:T(8,128)(2,1)S(1)}, bf16[320,1024]{1,0:T(8,128)(2,1)S(1)}, u32[]{:S(2)}, u32[]{:S(2)}) collective-permute-start(bf16[320,1024]{1,0:T(8,128)(2,1)S(1)} %get-tuple-element.29), channel_id=1, source_target_pairs={{0,24},{1,25},{2,26},{3,27},{4,28},{5,29},{6,30},{7,31},{8,0},{9,1... | collective-permute-start | bytes 1966088 | tf_op jit(solution)/shard_map/ppermute | solution.py:158
  5.6 5.6 %collective-permute-start.1 = (bf16[320,1024]{1,0:T(8,128)(2,1)S(1)}, bf16[320,1024]{1,0:T(8,128)(2,1)S(1)}, u32[]{:S(2)}, u32[]{:S(2)}) collective-permute-start(bf16[320,1024]{1,0:T(8,128)(2,1)S(1)} %get-tuple-element.30.refs_3_), channel_id=1, source_target_pairs={{0,224},{1,225},{2,226},{3,227},{4,228},{5,229},{6,230},{7,231},{8... | collective-permute-start | bytes 1966088 | tf_op jit(solution)/shard_map/ppermute | solution.py:158
  11.1 1.6 collective-permute-start.6
  12.8 20.1 %collective-permute-done.2.refs_4_ = bf16[320,1024]{1,0:T(8,128)(2,1)S(1)} collective-permute-done((bf16[320,1024]{1,0:T(8,128)(2,1)S(1)}, bf16[320,1024]{1,0:T(8,128)(2,1)S(1)}, u32[]{:S(2)}, u32[]{:S(2)}) %collective-permute-start.2) | collective-permute-done | bytes 655392 | tf_op jit(solution)/shard_map/ppermute | solution.py:158
  32.9 1.5 collective-permute-start.8
  38.2 4.0 %collective-permute-start.14 = (bf16[320,1024]{1,0:T(8,128)(2,1)S(1)}, bf16[320,1024]{1,0:T(8,128)(2,1)S(1)}, u32[]{:S(2)}, u32[]{:S(2)}) collective-permute-start(bf16[320,1024]{1,0:T(8,128)(2,1)S(1)} %collective-permute-done.6.refs_5_), channel_id=1, source_target_pairs={{0,224},{1,225},{2,226},{3,227},{4,228},{5,229},{6,230},{7,231},{8... | collective-permute-start | bytes 1966088 | tf_op jit(solution)/shard_map/ppermute | solution.py:158
  42.2 5.4 %collective-permute-done.3.refs_1_ = bf16[320,1024]{1,0:T(8,128)(2,1)} collective-permute-done((bf16[320,1024]{1,0:T(8,128)(2,1)S(1)}, bf16[320,1024]{1,0:T(8,128)(2,1)}, u32[]{:S(2)}, u32[]{:S(2)}) %collective-permute-start.3) | collective-permute-done | bytes 655392 | tf_op jit(solution)/shard_map/ppermute | solution.py:158
  47.7 14.0 %collective-permute-done.5.refs_2_.refs_3_ = bf16[320,1024]{1,0:T(8,128)(2,1)} collective-permute-done((bf16[320,1024]{1,0:T(8,128)(2,1)S(1)}, bf16[320,1024]{1,0:T(8,128)(2,1)}, u32[]{:S(2)}, u32[]{:S(2)}) %collective-permute-start.5) | collective-permute-done | bytes 655392 | tf_op jit(solution)/shard_map/ppermute | solution.py:158
  61.7 17.0 %shard_map.55 = (bf16[3840,1024]{1,0:T(8,128)(2,1)S(1)}, f32[8,160,640]{2,1,0:T(8,128)S(1)}, bf16[8,160,640]{2,1,0:T(8,128)(2,1)}) custom-call(s32[2]{0:T(128)S(1)} %pad_add_fusion.place_ref, f32[1,1024]{1,0:T(1,128)S(1)} %divide_multiply_fusion.factor_ref, bf16[320,1024]{1,0:T(8,128)(2,1)S(1)} %collective-permute-done.1.refs_0_, ...), custom_call_target="tpu_custom_call" | custom-call | flops 3355443200 | bytes 7864320 | tf_op jit(solution)/shard_map/pallas_call | solution.py:123
  78.7 1.7 copy-done
  80.3 10.8 %collective-permute-start.10 = (bf16[4,2,160,640]{3,2,1,0:T(8,128)(2,1)}, bf16[4,2,160,640]{3,2,1,0:T(8,128)(2,1)}, u32[]{:S(2)}, u32[]{:S(2)}) collective-permute-start(bf16[4,2,160,640]{3,2,1,0:T(8,128)(2,1)} %bitcast.11), channel_id=1, source_target_pairs={{0,1},{1,0},{2,3},{3,2},{4,5},{5,4},{6,7},{7,6},{8,9},{9,8},{10,11... | collective-permute-start | bytes 4915208 | tf_op jit(solution)/shard_map/ppermute | solution.py:158
  92.2 12.9 %shard_map.56 = (f32[8,160,640]{2,1,0:T(8,128)S(1)}, bf16[8,160,640]{2,1,0:T(8,128)(2,1)}) custom-call(s32[2]{0:T(128)S(1)} %pad_add_fusion.place_ref, f32[1,1024]{1,0:T(1,128)S(1)} %divide_multiply_fusion.factor_ref, bf16[320,1024]{1,0:T(8,128)(2,1)S(1)} %copy-done.2, bf16[320,1024]{1,0:T(8,128)(2,1)} %collective-permute-done.3.refs_1_, ...), custom_call_target="tpu_custom_call" | custom-call | flops 3355443200 | bytes 7864320 | tf_op jit(solution)/shard_map/pallas_call | solution.py:123
  105.9 6.3 %collective-permute-start = (f32[8]{0:T(128)S(1)}, f32[8]{0:T(128)S(1)}, u32[]{:S(2)}, u32[]{:S(2)}) collective-permute-start(f32[8]{0:T(128)S(1)} %convert_reduce_fusion), channel_id=1, source_target_pairs={{0,8},{1,25},{2,234},{3,251},{4,244},{5,5},{6,22},{7,39},{8,16},{9... | collective-permute-start | bytes 104 | tf_op jit(solution)/shard_map/ppermute | solution.py:158
  114.1 2.7 %convert_add_fusion.1 = f32[4,2,160,640]{3,2,1,0:T(8,128)S(1)} fusion(f32[4,2,160,640]{3,2,1,0:T(8,128)} %bitcast.94, bf16[4,2,160,640]{3,2,1,0:T(8,128)(2,1)} %collective-permute-done.10), kind=kLoop, calls=%fused_computation.1 | loop fusion | flops 1638400 | bytes 8192000 | tf_op jit(solution)/shard_map/add | solution.py:219
  117.7 2.0 %collective-permute-start.12 = (bf16[2,160,640]{2,1,0:T(8,128)(2,1)S(1)}, bf16[2,160,640]{2,1,0:T(8,128)(2,1)S(1)}, u32[]{:S(2)}, u32[]{:S(2)}) collective-permute-start(bf16[2,160,640]{2,1,0:T(8,128)(2,1)S(1)} %get-tuple-element.26), channel_id=1, source_target_pairs={{0,6},{1,7},{2,0},{3,1},{4,2},{5,3},{6,4},{7,5},{8,14},{9,15},{10,... | collective-permute-start | bytes 1228808 | tf_op jit(solution)/shard_map/ppermute | solution.py:158
  119.8 1.9 fusion.25
  122.7 7.5 %collective-permute-done.25 = bf16[2,80,640]{2,1,0:T(8,128)(2,1)S(1)} collective-permute-done((bf16[2,80,640]{2,1,0:T(8,128)(2,1)S(1)}, bf16[2,80,640]{2,1,0:T(8,128)(2,1)S(1)}, u32[]{:S(2)}, u32[]{:S(2)}) %collective-permute-start.25) | collective-permute-done | bytes 204832 | tf_op jit(solution)/shard_map/ppermute | solution.py:158
  130.2 2.1 %collective-permute-start.20 = (bf16[2,80,640]{2,1,0:T(8,128)(2,1)S(1)}, bf16[2,80,640]{2,1,0:T(8,128)(2,1)S(1)}, u32[]{:S(2)}, u32[]{:S(2)}) collective-permute-start(bf16[2,80,640]{2,1,0:T(8,128)(2,1)S(1)} %get-tuple-element.34), channel_id=1, source_target_pairs={{0,6},{1,7},{2,0},{3,1},{4,2},{5,3},{6,4},{7,5},{8,14},{9,15},{10,... | collective-permute-start | bytes 614408 | tf_op jit(solution)/shard_map/ppermute | solution.py:158
  132.4 7.7 %collective-permute-done.17 = bf16[2,80,640]{2,1,0:T(8,128)(2,1)S(1)} collective-permute-done((bf16[2,80,640]{2,1,0:T(8,128)(2,1)S(1)}, bf16[2,80,640]{2,1,0:T(8,128)(2,1)S(1)}, u32[]{:S(2)}, u32[]{:S(2)}) %collective-permute-start.17) | collective-permute-done | bytes 204832 | tf_op jit(solution)/shard_map/ppermute | solution.py:158
  140.2 3.8 %collective-permute-start.24 = (bf16[4,80,640]{2,1,0:T(8,128)(2,1)S(1)}, bf16[4,80,640]{2,1,0:T(8,128)(2,1)S(1)}, u32[]{:S(2)}, u32[]{:S(2)}) collective-permute-start(bf16[4,80,640]{2,1,0:T(8,128)(2,1)S(1)} %slice_bitcast_fusion.1), channel_id=1, source_target_pairs={{0,16},{1,17},{2,18},{3,19},{4,20},{5,21},{6,22},{7,23},{8,24},{9,... | collective-permute-start | bytes 1228808 | tf_op jit(solution)/shard_map/ppermute | solution.py:158
  145.0 1.3 collective-permute-done.21
  146.4 1.6 collective-permute-start.22
  148.0 4.5 %collective-permute-start.23 = (bf16[80,640]{1,0:T(8,128)(2,1)S(1)}, bf16[80,640]{1,0:T(8,128)(2,1)S(1)}, u32[]{:S(2)}, u32[]{:S(2)}) collective-permute-start(bf16[80,640]{1,0:T(8,128)(2,1)S(1)} %get-tuple-element.49), channel_id=1, source_target_pairs={{0,24},{1,9},{2,26},{3,11},{8,0},{9,17},{10,2},{11,19},{16,8},{17,... | collective-permute-start | bytes 307208 | tf_op jit(solution)/shard_map/ppermute | solution.py:158
  152.7 2.7 %collective-permute-start.26 = (bf16[80,640]{1,0:T(8,128)(2,1)S(1)}, bf16[80,640]{1,0:T(8,128)(2,1)S(1)}, u32[]{:S(2)}, u32[]{:S(2)}) collective-permute-start(bf16[80,640]{1,0:T(8,128)(2,1)S(1)} %get-tuple-element.37), channel_id=1, source_target_pairs={{0,2},{1,3},{2,4},{3,5},{4,6},{5,7},{6,0},{7,1},{8,10},{9,11},{10,... | collective-permute-start | bytes 307208 | tf_op jit(solution)/shard_map/ppermute | solution.py:158
  155.3 4.2 %collective-permute-start.27 = (bf16[80,640]{1,0:T(8,128)(2,1)S(1)}, bf16[80,640]{1,0:T(8,128)(2,1)S(1)}, u32[]{:S(2)}, u32[]{:S(2)}) collective-permute-start(bf16[80,640]{1,0:T(8,128)(2,1)S(1)} %get-tuple-element.39), channel_id=1, source_target_pairs={{0,6},{1,7},{2,0},{3,1},{4,2},{5,3},{6,4},{7,5},{8,14},{9,15},{10,... | collective-permute-start | bytes 307208 | tf_op jit(solution)/shard_map/ppermute | solution.py:158
  159.6 2.6 %collective-permute-done.27 = bf16[80,640]{1,0:T(8,128)(2,1)S(1)} collective-permute-done((bf16[80,640]{1,0:T(8,128)(2,1)S(1)}, bf16[80,640]{1,0:T(8,128)(2,1)S(1)}, u32[]{:S(2)}, u32[]{:S(2)}) %collective-permute-start.27) | collective-permute-done | bytes 102432 | tf_op jit(solution)/shard_map/ppermute | solution.py:158
  162.3 2.3 %collective-permute-done.28 = bf16[80,640]{1,0:T(8,128)(2,1)S(1)} collective-permute-done((bf16[80,640]{1,0:T(8,128)(2,1)S(1)}, bf16[80,640]{1,0:T(8,128)(2,1)S(1)}, u32[]{:S(2)}, u32[]{:S(2)}) %collective-permute-start.28) | collective-permute-done | bytes 102432 | tf_op jit(solution)/shard_map/ppermute | solution.py:158
  164.8 6.6 %collective-permute-start.29 = (f32[160,640]{1,0:T(8,128)S(1)}, f32[160,640]{1,0:T(8,128)S(1)}, u32[]{:S(2)}, u32[]{:S(2)}) collective-permute-start(f32[160,640]{1,0:T(8,128)S(1)} %fusion.5), channel_id=1, source_target_pairs={{0,254},{1,239},{2,28},{3,13},{8,6},{9,247},{10,36},{11,21},{16,14... | collective-permute-start | bytes 1228808 | tf_op jit(solution)/shard_map/ppermute | solution.py:158
  173.4 9.0 %collective-permute-start.32 = (f32[160,640]{1,0:T(8,128)S(1)}, f32[160,640]{1,0:T(8,128)S(1)}, u32[]{:S(2)}, u32[]{:S(2)}) collective-permute-start(f32[160,640]{1,0:T(8,128)S(1)} %fusion.5), channel_id=1, source_target_pairs={{0,33},{1,32},{2,35},{3,34},{8,41},{9,40},{10,43},{11,42},{16,49},... | collective-permute-start | bytes 1228808 | tf_op jit(solution)/shard_map/ppermute | solution.py:158
  183.1 1.6 collective-permute-done.31
  184.8 6.6 %collective-permute-done.32 = f32[160,640]{1,0:T(8,128)S(1)} collective-permute-done((f32[160,640]{1,0:T(8,128)S(1)}, f32[160,640]{1,0:T(8,128)S(1)}, u32[]{:S(2)}, u32[]{:S(2)}) %collective-permute-start.32) | collective-permute-done | bytes 409632 | tf_op jit(solution)/shard_map/ppermute | solution.py:158
  (78 shorter events, 13.2 us)
Async XLA Ops:
  1.9 30.9 %collective-permute-start.2 = (bf16[320,1024]{1,0:T(8,128)(2,1)S(1)}, bf16[320,1024]{1,0:T(8,128)(2,1)S(1)}, u32[]{:S(2)}, u32[]{:S(2)}) collective-permute-start(bf16[320,1024]{1,0:T(8,128)(2,1)S(1)} %get-tuple-element.29), channel_id=1, source_target_pairs={{0,24},{1,25},{2,26},{3,27},{4,28},{5,29},{6,30},{7,31},{8,0},{9,1... | collective-permute-start | bytes 1966088 | tf_op jit(solution)/shard_map/ppermute | solution.py:158
  5.6 27.3 %collective-permute-start.4 = (bf16[320,1024]{1,0:T(8,128)(2,1)S(1)}, bf16[320,1024]{1,0:T(8,128)(2,1)S(1)}, u32[]{:S(2)}, u32[]{:S(2)}) collective-permute-start(bf16[320,1024]{1,0:T(8,128)(2,1)S(1)} %get-tuple-element.28), channel_id=1, source_target_pairs={{0,8},{1,9},{2,10},{3,11},{4,12},{5,13},{6,14},{7,15},{8,16},{9,17... | collective-permute-start | bytes 1966088 | tf_op jit(solution)/shard_map/ppermute | solution.py:158
  5.6 28.8 %collective-permute-start.1 = (bf16[320,1024]{1,0:T(8,128)(2,1)S(1)}, bf16[320,1024]{1,0:T(8,128)(2,1)S(1)}, u32[]{:S(2)}, u32[]{:S(2)}) collective-permute-start(bf16[320,1024]{1,0:T(8,128)(2,1)S(1)} %get-tuple-element.30.refs_3_), channel_id=1, source_target_pairs={{0,224},{1,225},{2,226},{3,227},{4,228},{5,229},{6,230},{7,231},{8... | collective-permute-start | bytes 1966088 | tf_op jit(solution)/shard_map/ppermute | solution.py:158
  11.1 24.4 %collective-permute-start.6 = (bf16[320,1024]{1,0:T(8,128)(2,1)S(1)}, bf16[320,1024]{1,0:T(8,128)(2,1)S(1)}, u32[]{:S(2)}, u32[]{:S(2)}) collective-permute-start(bf16[320,1024]{1,0:T(8,128)(2,1)S(1)} %get-tuple-element.31), channel_id=1, source_target_pairs={{0,16},{1,17},{2,18},{3,19},{4,20},{5,21},{6,22},{7,23},{8,24},{9,... | collective-permute-start | bytes 1966088 | tf_op jit(solution)/shard_map/ppermute | solution.py:158
  12.8 25.4 %collective-permute-start.7 = (bf16[320,1024]{1,0:T(8,128)(2,1)S(1)}, bf16[320,1024]{1,0:T(8,128)(2,1)}, u32[]{:S(2)}, u32[]{:S(2)}) collective-permute-start(bf16[320,1024]{1,0:T(8,128)(2,1)S(1)} %get-tuple-element.30.refs_3_), channel_id=1, source_target_pairs={{0,32},{1,33},{2,34},{3,35},{4,36},{5,37},{6,38},{7,39},{8,40},{9,... | collective-permute-start | bytes 1966088 | tf_op jit(solution)/shard_map/ppermute | solution.py:158
  32.9 14.7 %collective-permute-start.3 = (bf16[320,1024]{1,0:T(8,128)(2,1)S(1)}, bf16[320,1024]{1,0:T(8,128)(2,1)}, u32[]{:S(2)}, u32[]{:S(2)}) collective-permute-start(bf16[320,1024]{1,0:T(8,128)(2,1)S(1)} %collective-permute-done.2.refs_4_), channel_id=1, source_target_pairs={{0,224},{1,225},{2,226},{3,227},{4,228},{5,229},{6,230},{7,231},{8... | collective-permute-start | bytes 1966088 | tf_op jit(solution)/shard_map/ppermute | solution.py:158
  32.9 28.8 %collective-permute-start.8 = (bf16[320,1024]{1,0:T(8,128)(2,1)S(1)}, bf16[320,1024]{1,0:T(8,128)(2,1)}, u32[]{:S(2)}, u32[]{:S(2)}) collective-permute-start(bf16[320,1024]{1,0:T(8,128)(2,1)S(1)} %collective-permute-done.2.refs_4_), channel_id=1, source_target_pairs={{0,32},{1,33},{2,34},{3,35},{4,36},{5,37},{6,38},{7,39},{8,40},{9,... | collective-permute-start | bytes 1966088 | tf_op jit(solution)/shard_map/ppermute | solution.py:158
  34.4 27.3 %collective-permute-start.5 = (bf16[320,1024]{1,0:T(8,128)(2,1)S(1)}, bf16[320,1024]{1,0:T(8,128)(2,1)}, u32[]{:S(2)}, u32[]{:S(2)}) collective-permute-start(bf16[320,1024]{1,0:T(8,128)(2,1)S(1)} %collective-permute-done.4.refs_6_), channel_id=1, source_target_pairs={{0,224},{1,225},{2,226},{3,227},{4,228},{5,229},{6,230},{7,231},{8... | collective-permute-start | bytes 1966088 | tf_op jit(solution)/shard_map/ppermute | solution.py:158
  35.6 26.1 %collective-permute-start.9 = (bf16[320,1024]{1,0:T(8,128)(2,1)S(1)}, bf16[320,1024]{1,0:T(8,128)(2,1)}, u32[]{:S(2)}, u32[]{:S(2)}) collective-permute-start(bf16[320,1024]{1,0:T(8,128)(2,1)S(1)} %collective-permute-done.4.refs_6_), channel_id=1, source_target_pairs={{0,32},{1,33},{2,34},{3,35},{4,36},{5,37},{6,38},{7,39},{8,40},{9,... | collective-permute-start | bytes 1966088 | tf_op jit(solution)/shard_map/ppermute | solution.py:158
  38.2 52.9 %collective-permute-start.14 = (bf16[320,1024]{1,0:T(8,128)(2,1)S(1)}, bf16[320,1024]{1,0:T(8,128)(2,1)S(1)}, u32[]{:S(2)}, u32[]{:S(2)}) collective-permute-start(bf16[320,1024]{1,0:T(8,128)(2,1)S(1)} %collective-permute-done.6.refs_5_), channel_id=1, source_target_pairs={{0,224},{1,225},{2,226},{3,227},{4,228},{5,229},{6,230},{7,231},{8... | collective-permute-start | bytes 1966088 | tf_op jit(solution)/shard_map/ppermute | solution.py:158
  47.6 43.5 %collective-permute-start.15 = (bf16[320,1024]{1,0:T(8,128)(2,1)S(1)}, bf16[320,1024]{1,0:T(8,128)(2,1)S(1)}, u32[]{:S(2)}, u32[]{:S(2)}) collective-permute-start(bf16[320,1024]{1,0:T(8,128)(2,1)S(1)} %collective-permute-done.6.refs_5_), channel_id=1, source_target_pairs={{0,32},{1,33},{2,34},{3,35},{4,36},{5,37},{6,38},{7,39},{8,40},{9,... | collective-permute-start | bytes 1966088 | tf_op jit(solution)/shard_map/ppermute | solution.py:158
  80.3 33.8 %collective-permute-start.10 = (bf16[4,2,160,640]{3,2,1,0:T(8,128)(2,1)}, bf16[4,2,160,640]{3,2,1,0:T(8,128)(2,1)}, u32[]{:S(2)}, u32[]{:S(2)}) collective-permute-start(bf16[4,2,160,640]{3,2,1,0:T(8,128)(2,1)} %bitcast.11), channel_id=1, source_target_pairs={{0,1},{1,0},{2,3},{3,2},{4,5},{5,4},{6,7},{7,6},{8,9},{9,8},{10,11... | collective-permute-start | bytes 4915208 | tf_op jit(solution)/shard_map/ppermute | solution.py:158
  105.0 14.7 %collective-permute-start.16 = (bf16[2,4,160,640]{3,2,1,0:T(8,128)(2,1)}, bf16[2,4,160,640]{3,2,1,0:T(8,128)(2,1)}, u32[]{:S(2)}, u32[]{:S(2)}) collective-permute-start(bf16[2,4,160,640]{3,2,1,0:T(8,128)(2,1)} %bitcast.17), channel_id=1, source_target_pairs={{0,1},{1,0},{2,3},{3,2},{4,5},{5,4},{6,7},{7,6},{8,9},{9,8},{10,11... | collective-permute-start | bytes 4915208 | tf_op jit(solution)/shard_map/ppermute | solution.py:158
  105.9 7.0 %collective-permute-start = (f32[8]{0:T(128)S(1)}, f32[8]{0:T(128)S(1)}, u32[]{:S(2)}, u32[]{:S(2)}) collective-permute-start(f32[8]{0:T(128)S(1)} %convert_reduce_fusion), channel_id=1, source_target_pairs={{0,8},{1,25},{2,234},{3,251},{4,244},{5,5},{6,22},{7,39},{8,16},{9... | collective-permute-start | bytes 104 | tf_op jit(solution)/shard_map/ppermute | solution.py:158
  117.0 23.2 %collective-permute-start.11 = (bf16[2,160,640]{2,1,0:T(8,128)(2,1)S(1)}, bf16[2,160,640]{2,1,0:T(8,128)(2,1)S(1)}, u32[]{:S(2)}, u32[]{:S(2)}) collective-permute-start(bf16[2,160,640]{2,1,0:T(8,128)(2,1)S(1)} %get-tuple-element.27), channel_id=1, source_target_pairs={{0,2},{1,3},{2,4},{3,5},{4,6},{5,7},{6,0},{7,1},{8,10},{9,11},{10,... | collective-permute-start | bytes 1228808 | tf_op jit(solution)/shard_map/ppermute | solution.py:158
  117.7 26.2 %collective-permute-start.12 = (bf16[2,160,640]{2,1,0:T(8,128)(2,1)S(1)}, bf16[2,160,640]{2,1,0:T(8,128)(2,1)S(1)}, u32[]{:S(2)}, u32[]{:S(2)}) collective-permute-start(bf16[2,160,640]{2,1,0:T(8,128)(2,1)S(1)} %get-tuple-element.26), channel_id=1, source_target_pairs={{0,6},{1,7},{2,0},{3,1},{4,2},{5,3},{6,4},{7,5},{8,14},{9,15},{10,... | collective-permute-start | bytes 1228808 | tf_op jit(solution)/shard_map/ppermute | solution.py:158
  119.7 24.2 %collective-permute-start.13 = (bf16[2,160,640]{2,1,0:T(8,128)(2,1)S(1)}, bf16[2,160,640]{2,1,0:T(8,128)(2,1)S(1)}, u32[]{:S(2)}, u32[]{:S(2)}) collective-permute-start(bf16[2,160,640]{2,1,0:T(8,128)(2,1)S(1)} %get-tuple-element.25), channel_id=1, source_target_pairs={{0,4},{1,5},{2,6},{3,7},{4,0},{5,1},{6,2},{7,3},{8,12},{9,13},{10,... | collective-permute-start | bytes 1228808 | tf_op jit(solution)/shard_map/ppermute | solution.py:158
  121.9 18.3 %collective-permute-start.17 = (bf16[2,80,640]{2,1,0:T(8,128)(2,1)S(1)}, bf16[2,80,640]{2,1,0:T(8,128)(2,1)S(1)}, u32[]{:S(2)}, u32[]{:S(2)}) collective-permute-start(bf16[2,80,640]{2,1,0:T(8,128)(2,1)S(1)} %get-tuple-element.32), channel_id=1, source_target_pairs={{0,2},{1,3},{2,4},{3,5},{4,6},{5,7},{6,0},{7,1},{8,10},{9,11},{10,... | collective-permute-start | bytes 614408 | tf_op jit(solution)/shard_map/ppermute | solution.py:158
  122.5 7.7 %collective-permute-start.25 = (bf16[2,80,640]{2,1,0:T(8,128)(2,1)S(1)}, bf16[2,80,640]{2,1,0:T(8,128)(2,1)S(1)}, u32[]{:S(2)}, u32[]{:S(2)}) collective-permute-start(bf16[2,80,640]{2,1,0:T(8,128)(2,1)S(1)} %slice_bitcast_fusion.2), channel_id=1, source_target_pairs={{0,24},{1,9},{2,26},{3,11},{4,28},{5,13},{6,30},{7,15},{8,0},{9,17... | collective-permute-start | bytes 614408 | tf_op jit(solution)/shard_map/ppermute | solution.py:158
  130.2 14.7 %collective-permute-start.20 = (bf16[2,80,640]{2,1,0:T(8,128)(2,1)S(1)}, bf16[2,80,640]{2,1,0:T(8,128)(2,1)S(1)}, u32[]{:S(2)}, u32[]{:S(2)}) collective-permute-start(bf16[2,80,640]{2,1,0:T(8,128)(2,1)S(1)} %get-tuple-element.34), channel_id=1, source_target_pairs={{0,6},{1,7},{2,0},{3,1},{4,2},{5,3},{6,4},{7,5},{8,14},{9,15},{10,... | collective-permute-start | bytes 614408 | tf_op jit(solution)/shard_map/ppermute | solution.py:158
  140.2 6.1 %collective-permute-start.21 = (bf16[2,80,640]{2,1,0:T(8,128)(2,1)S(1)}, bf16[2,80,640]{2,1,0:T(8,128)(2,1)S(1)}, u32[]{:S(2)}, u32[]{:S(2)}) collective-permute-start(bf16[2,80,640]{2,1,0:T(8,128)(2,1)S(1)} %get-tuple-element.33), channel_id=1, source_target_pairs={{0,4},{1,5},{2,6},{3,7},{4,0},{5,1},{6,2},{7,3},{8,12},{9,13},{10,... | collective-permute-start | bytes 614408 | tf_op jit(solution)/shard_map/ppermute | solution.py:158
  140.2 12.3 %collective-permute-start.24 = (bf16[4,80,640]{2,1,0:T(8,128)(2,1)S(1)}, bf16[4,80,640]{2,1,0:T(8,128)(2,1)S(1)}, u32[]{:S(2)}, u32[]{:S(2)}) collective-permute-start(bf16[4,80,640]{2,1,0:T(8,128)(2,1)S(1)} %slice_bitcast_fusion.1), channel_id=1, source_target_pairs={{0,16},{1,17},{2,18},{3,19},{4,20},{5,21},{6,22},{7,23},{8,24},{9,... | collective-permute-start | bytes 1228808 | tf_op jit(solution)/shard_map/ppermute | solution.py:158
  144.2 20.4 %collective-permute-start.18 = (bf16[160,640]{1,0:T(8,128)(2,1)S(1)}, bf16[160,640]{1,0:T(8,128)(2,1)S(1)}, u32[]{:S(2)}, u32[]{:S(2)}) collective-permute-start(bf16[160,640]{1,0:T(8,128)(2,1)S(1)} %get-tuple-element.35), channel_id=1, source_target_pairs={{0,8},{1,25},{2,10},{3,27},{4,12},{5,13},{6,14},{7,15},{8,16},{9,1... | collective-permute-start | bytes 614408 | tf_op jit(solution)/shard_map/ppermute | solution.py:158
  144.3 20.4 %collective-permute-start.19 = (bf16[160,640]{1,0:T(8,128)(2,1)S(1)}, bf16[160,640]{1,0:T(8,128)(2,1)S(1)}, u32[]{:S(2)}, u32[]{:S(2)}) collective-permute-start(bf16[160,640]{1,0:T(8,128)(2,1)S(1)} %get-tuple-element.36), channel_id=1, source_target_pairs={{4,28},{5,29},{6,30},{7,31},{12,4},{13,5},{14,6},{15,7},{20,12},{2... | collective-permute-start | bytes 614408 | tf_op jit(solution)/shard_map/ppermute | solution.py:158
  146.4 8.9 %collective-permute-start.22 = (bf16[80,640]{1,0:T(8,128)(2,1)S(1)}, bf16[80,640]{1,0:T(8,128)(2,1)S(1)}, u32[]{:S(2)}, u32[]{:S(2)}) collective-permute-start(bf16[80,640]{1,0:T(8,128)(2,1)S(1)} %get-tuple-element.48), channel_id=1, source_target_pairs={{0,16},{1,17},{2,18},{3,19},{4,20},{5,21},{6,22},{7,23},{8,24},{9,... | collective-permute-start | bytes 307208 | tf_op jit(solution)/shard_map/ppermute | solution.py:158
  148.0 11.6 %collective-permute-start.23 = (bf16[80,640]{1,0:T(8,128)(2,1)S(1)}, bf16[80,640]{1,0:T(8,128)(2,1)S(1)}, u32[]{:S(2)}, u32[]{:S(2)}) collective-permute-start(bf16[80,640]{1,0:T(8,128)(2,1)S(1)} %get-tuple-element.49), channel_id=1, source_target_pairs={{0,24},{1,9},{2,26},{3,11},{8,0},{9,17},{10,2},{11,19},{16,8},{17,... | collective-permute-start | bytes 307208 | tf_op jit(solution)/shard_map/ppermute | solution.py:158
  152.7 7.0 %collective-permute-start.26 = (bf16[80,640]{1,0:T(8,128)(2,1)S(1)}, bf16[80,640]{1,0:T(8,128)(2,1)S(1)}, u32[]{:S(2)}, u32[]{:S(2)}) collective-permute-start(bf16[80,640]{1,0:T(8,128)(2,1)S(1)} %get-tuple-element.37), channel_id=1, source_target_pairs={{0,2},{1,3},{2,4},{3,5},{4,6},{5,7},{6,0},{7,1},{8,10},{9,11},{10,... | collective-permute-start | bytes 307208 | tf_op jit(solution)/shard_map/ppermute | solution.py:158
  155.3 6.9 %collective-permute-start.27 = (bf16[80,640]{1,0:T(8,128)(2,1)S(1)}, bf16[80,640]{1,0:T(8,128)(2,1)S(1)}, u32[]{:S(2)}, u32[]{:S(2)}) collective-permute-start(bf16[80,640]{1,0:T(8,128)(2,1)S(1)} %get-tuple-element.39), channel_id=1, source_target_pairs={{0,6},{1,7},{2,0},{3,1},{4,2},{5,3},{6,4},{7,5},{8,14},{9,15},{10,... | collective-permute-start | bytes 307208 | tf_op jit(solution)/shard_map/ppermute | solution.py:158
  164.8 17.6 %collective-permute-start.29 = (f32[160,640]{1,0:T(8,128)S(1)}, f32[160,640]{1,0:T(8,128)S(1)}, u32[]{:S(2)}, u32[]{:S(2)}) collective-permute-start(f32[160,640]{1,0:T(8,128)S(1)} %fusion.5), channel_id=1, source_target_pairs={{0,254},{1,239},{2,28},{3,13},{8,6},{9,247},{10,36},{11,21},{16,14... | collective-permute-start | bytes 1228808 | tf_op jit(solution)/shard_map/ppermute | solution.py:158
  171.4 11.1 %collective-permute-start.30 = (f32[160,640]{1,0:T(8,128)S(1)}, f32[160,640]{1,0:T(8,128)S(1)}, u32[]{:S(2)}, u32[]{:S(2)}) collective-permute-start(f32[160,640]{1,0:T(8,128)S(1)} %fusion.5), channel_id=1, source_target_pairs={{4,20},{5,5},{6,246},{7,231},{12,28},{13,13},{14,254},{15,239},{20... | collective-permute-start | bytes 1228808 | tf_op jit(solution)/shard_map/ppermute | solution.py:158
  172.1 12.6 %collective-permute-start.31 = (f32[160,640]{1,0:T(8,128)S(1)}, f32[160,640]{1,0:T(8,128)S(1)}, u32[]{:S(2)}, u32[]{:S(2)}) collective-permute-start(f32[160,640]{1,0:T(8,128)S(1)} %fusion.5), channel_id=1, source_target_pairs={{4,35},{5,34},{6,33},{7,32},{12,43},{13,42},{14,41},{15,40},{20,51... | collective-permute-start | bytes 1228808 | tf_op jit(solution)/shard_map/ppermute | solution.py:158
  173.4 18.0 %collective-permute-start.32 = (f32[160,640]{1,0:T(8,128)S(1)}, f32[160,640]{1,0:T(8,128)S(1)}, u32[]{:S(2)}, u32[]{:S(2)}) collective-permute-start(f32[160,640]{1,0:T(8,128)S(1)} %fusion.5), channel_id=1, source_target_pairs={{0,33},{1,32},{2,35},{3,34},{8,41},{9,40},{10,43},{11,42},{16,49},... | collective-permute-start | bytes 1228808 | tf_op jit(solution)/shard_map/ppermute | solution.py:158
  (5 other events, 65.7 us)

commit v3 on v2

v3 whole, which is shorter than its diff:
```python
import functools

import jax
import jax.numpy as jnp
from jax import lax
from jax.experimental import pallas as pl
from jax.experimental.pallas import tpu as pltpu
from jax.sharding import PartitionSpec as P


EPSILON = 1e-08
AXES = ("ex", "ckpt")
NY = 4
CHUNK = 32


def scale_into(left_ref, piece_ref, factor_ref, start):
    @pl.loop(0, piece_ref.shape[0] // CHUNK)
    def _(step):
        source = pl.ds(pl.multiple_of(step * CHUNK, CHUNK), CHUNK)
        target = pl.ds(pl.multiple_of(start + step * CHUNK, CHUNK), CHUNK)
        piece = piece_ref[source, :].astype(jnp.float32)
        left_ref[target, :] = (piece * factor_ref[...]).astype(jnp.bfloat16)


def fill(out_ref, index, tile):
    half = tile.shape[0] // 2
    rows = tile.shape[1]
    out_ref[index, :, 0:rows] = tile[:half].astype(out_ref.dtype)
    out_ref[index, :, rows : 2 * rows] = tile[half:].astype(out_ref.dtype)


def product_of(right, left):
    return lax.dot_general(right, left, (((1,), (1,)), ((), ())), preferred_element_type=jnp.float32)


def owner(far, p):
    return jnp.where(far == 1, 3 * p, 1 + p)


def tiles_kernel(late, place_ref, factor_ref, *refs):
    keep_ref, give_ref, left_ref = refs[-3:]
    pieces = refs[:-3]
    order = (0, 3, 1, 2) if late else (0, 3, 1)
    here = dict(zip((0, 3, 1, 2), pieces[:NY]))
    above = dict(zip(order, pieces[NY : NY + len(order)]))
    below = dict(zip(order, pieces[NY + len(order) :]))
    rows = pieces[0].shape[0]
    y = place_ref[0]
    c = place_ref[1]
    for plane, group in enumerate((below, here, above)):
        for rel, ref in group.items():
            scale_into(left_ref, ref, factor_ref, (plane * NY + lax.rem(y + rel, NY)) * rows)

    def left_of(r, offset, count):
        start = (lax.rem(y + r, NY) + 2 * NY - offset) * rows
        return left_ref[pl.ds(pl.multiple_of(start, CHUNK), count * rows), :]

    @pl.loop(0, 4)
    def _(turn):
        far = turn // 2
        given = lax.rem(turn, 2)
        core = jnp.where(given == 1, 1 - c, c)
        lowest = 4 * far + 2 * core + 1

        def place(slot, p, tile):
            index = slot * 4 + owner(far, p) if late else owner(far, p) * 2 + slot

            @pl.when(given == 0)
            def _():
                fill(keep_ref, index, tile)

            @pl.when(given == 1)
            def _():
                fill(give_ref, index, tile)

        first = core == 0
        if late:
            pair = product_of(above[2][...], left_of(2, lowest + 1, 2))
            place(0, 1, pair[:, :rows])
            place(0, 0, pair[:, rows:])
            right = jnp.where(first, above[3][...], above[1][...])
            place(1, 0, product_of(right, left_of(jnp.where(first, 3, 1), lowest, 1)))
            place(1, 1, product_of(above[0][...], left_of(0, lowest + 1, 1)))
        else:
            right = jnp.where(first, above[1][...], above[3][...])
            pair = product_of(right, left_of(jnp.where(first, 1, 3), lowest + 1, 2))
            place(jnp.where(first, 1, 0), 1, pair[:, :rows])
            place(1, 0, pair[:, rows:])
            right = jnp.where(first, above[3][...], above[1][...])
            place(jnp.where(first, 0, 1), 1, product_of(right, left_of(jnp.where(first, 3, 1), lowest + 1, 1)))
            place(0, 0, product_of(above[0][...], left_of(0, lowest, 1)))


def tiles(late, place, factor, here, above, below):
    order = (0, 3, 1, 2) if late else (0, 3, 1)
    arrays = [here[r] for r in (0, 3, 1, 2)] + [above[r] for r in order] + [below[r] for r in order]
    rows, width = arrays[0].shape
    half = rows // 2
    vmem = pl.BlockSpec(memory_space=pltpu.VMEM)
    keep, give = pl.pallas_call(
        functools.partial(tiles_kernel, late),
        in_specs=[pl.BlockSpec(memory_space=pltpu.SMEM)] + [vmem] * (1 + len(arrays)),
        out_specs=[vmem] * 2,
        out_shape=[
            jax.ShapeDtypeStruct((8, half, 2 * rows), jnp.float32),
            jax.ShapeDtypeStruct((8, half, 2 * rows), jnp.bfloat16),
        ],
        scratch_shapes=[pltpu.VMEM((3 * NY * rows, width), jnp.bfloat16)],
        compiler_params=pltpu.CompilerParams(vmem_limit_bytes=28 * 2**20),
        cost_estimate=pl.CostEstimate(
            flops=32 * rows * rows * width, bytes_accessed=12 * rows * width * 2, transcendentals=0
        ),
    )(place, factor, *arrays)
    shape = (2, 4, half, 2 * rows) if late else (4, 2, half, 2 * rows)
    return keep.reshape(shape), give.reshape(shape)


def local_fn(blocks):
    def flat(e, x, c):
        return (e % blocks) * 8 + (x % 4) * 2 + c

    def ring(e, by):
        return e - e % NY + (e + by) % NY

    def send(value, move):
        pairs = []
        for e in range(blocks):
            for x in range(4):
                for c in range(2):
                    target = move(e, x, c)
                    if target is not None:
                        pairs.append((flat(e, x, c), flat(*target)))
        return lax.ppermute(value, AXES, pairs)

    def offset_of(x, c):
        return (4 if x in (0, 3) else 0) + 2 * c + 1 + (1 if x >= 2 else 0)

    def local(grads, second_moment, step_size, partners, counts):
        width = grads.shape[2]
        rows = grads.shape[1]
        reach = partners.shape[1]
        quarter = width // NY
        part = rows // 4
        own = grads[0]
        e = lax.axis_index("ex")
        k = lax.axis_index("ckpt")
        y = lax.bitwise_and(e, NY - 1)
        x = lax.shift_right_logical(k, 1)
        c = lax.bitwise_and(k, 1)
        starts = [lax.bitwise_and(y + i, NY - 1) * quarter for i in range(NY)]
        spots = [lax.bitwise_and(x + i, 3) for i in range(4)]
        low = x < 2
        is_far = jnp.logical_or(x == 0, x == 3)
        offset = jnp.where(is_far, NY, 0) + 2 * c + 1 + jnp.where(low, 0, 1)
        later_block = x >= 2
        own, starts, spots, low, offset, later_block, y, c, e, zero = lax.optimization_barrier(
            (own, starts, spots, low, offset - 1, later_block, y, c, e, e - e)
        )

        def cut(block, i):
            return lax.dynamic_slice(block, (zero, starts[i]), (rows, quarter), allow_negative_indices=False)

        def pick(array, i, axis):
            at = [zero] * array.ndim
            at[axis] = spots[i % 4]
            sizes = list(array.shape)
            sizes[axis] = 1
            return lax.dynamic_slice(array, at, sizes, allow_negative_indices=False).squeeze(axis)

        here = [None] * NY
        above = [None] * NY
        below = [None] * NY
        ahead, behind = cut(own, 1), cut(own, 3)
        own, ahead, behind = lax.optimization_barrier((own, ahead, behind))
        here[0] = cut(own, 0)
        here[3] = send(ahead, lambda e, x, c: (ring(e, 1), x, c))
        here[1] = send(behind, lambda e, x, c: (ring(e, 3), x, c))
        here[2] = send(cut(own, 2), lambda e, x, c: (ring(e, 2), x, c))
        for r in (0, 3, 1, 2):
            above[r] = send(here[r], lambda e, x, c: (e - NY, x, c))
            below[r] = send(here[r], lambda e, x, c: (e + NY, x, c))

        offsets = jnp.mod(partners[0] - e, blocks)
        alive = jnp.arange(reach, dtype=jnp.int32) < counts[0]
        wanted = jnp.arange(1, reach + 1, dtype=jnp.int32)
        matched = jnp.logical_and(offsets[:, None] == wanted[None, :], alive[:, None])
        listed = jnp.sum(matched.astype(jnp.float32), axis=0)
        listed = send(listed, lambda e, x, c: (e + offset_of(x, c) - NY, x, c))
        weight = lax.dynamic_slice(listed, (offset,), (1,), allow_negative_indices=False)[0]

        factor = step_size[:, None] / (jnp.sqrt(second_moment) + EPSILON) * width ** (-0.5)
        factor = lax.dynamic_slice(factor, (zero, starts[0]), (1, quarter), allow_negative_indices=False)
        place = jnp.stack([y, c])
        keep, give = tiles(False, place, factor, here, above, below)

        def low_of(x):
            return x < 2

        def narrow(value):
            return value.astype(jnp.bfloat16)

        def wide(value):
            return value.astype(jnp.float32)

        given = send(give, lambda e, x, c: (e, x, 1 - c))
        total = keep + wide(given)
        early = pick(total, 0, 0)
        arrived_early = [send(narrow(pick(total, t, 0)), lambda e, x, c, t=t: (e, x + t, c)) for t in (1, 3, 2)]
        keep, give = tiles(True, place, factor, here, above, below)
        given = send(give, lambda e, x, c: (e, x, 1 - c))
        total = keep + wide(given)

        def rest(e, c):
            return ring(e, 3 if c == 0 else 1)

        upper, lower = total[:, :, :part], total[:, :, part:]
        by2 = send(narrow(lower[0]), lambda e, x, c: (ring(e, 2), x, c))
        by1 = send(narrow(lower[1, :2]), lambda e, x, c: (rest(e, c), x, c))
        upper_own = pick(upper, 0, 1)
        arrived = [send(narrow(pick(upper, t, 1)), lambda e, x, c, t=t: (e, x + t, c)) for t in (1, 3, 2)]
        lower_own = wide(by2) + jnp.concatenate([wide(by1), lower[1, 2:]], axis=0)
        bottom = pick(lower_own, 0, 0)
        bottom_arrived = [send(narrow(pick(lower_own, t, 0)), lambda e, x, c, t=t: (e, x + t, c)) for t in (1, 3, 2)]
        arrived_early, arrived[0] = lax.optimization_barrier((arrived_early, arrived[0]))
        for value in arrived_early:
            early = early + wide(value)
        for value in arrived:
            upper_own = upper_own + wide(value)
        ay2 = send(narrow(upper_own[0]), lambda e, x, c: (ring(e, 2), x, c))
        ey1 = send(narrow(early[1]), lambda e, x, c: (ring(e, 3 if low_of(x) and c == 1 else 1), x, c))
        padded = jnp.concatenate([upper_own[1], jnp.zeros_like(upper_own[1])], axis=0)
        mixed = send(
            narrow(jnp.where(low, padded, early[0])), lambda e, x, c: (rest(e, c) if low_of(x) else ring(e, 3), x, c)
        )
        for value in bottom_arrived:
            bottom = bottom + wide(value)
        top = wide(ay2) + jnp.where(low, 0.0, upper_own[1])
        final = jnp.concatenate([top, bottom], axis=0) + wide(ey1) + wide(mixed) + jnp.where(low, early[0], 0.0)
        final = jnp.where(weight > 0, final, 0.0)

        def deliver(first):
            def move(e, x, c):
                far = x in (0, 3)
                if (x < 2) == first:
                    return (e + NY, 0 if far else 1, 1 - c)
                return (e + NY - offset_of(x, c), 3 if far else 2, c)

            return move

        one = send(final, deliver(True))
        two = send(final, deliver(False))

        def later(tile):
            return jnp.concatenate([tile[:, :rows], tile[:, rows:]], axis=0)

        one, two = later(one), later(two)
        backward = jnp.concatenate([two, one], axis=1)
        forward = jnp.concatenate([two.T, one.T], axis=1)
        return jnp.where(later_block, forward, backward)

    return local


def build(mesh):
    local = local_fn(mesh.shape["ex"])
    in_specs = (P("ckpt", "ex", None), P("ckpt", None), P("ckpt"), P("ex", None), P("ex"))
    return jax.shard_map(local, mesh=mesh, in_specs=in_specs, out_specs=P("ex", "ckpt"), check_vma=False)


def solution(mesh):
    return build(mesh)
```

time: 193 us -> 184 us (0.953)
  the two profiles are of different devices: /device:TPU:1 before, /device:TPU:5 now
where the time goes in v3:
time: 184 us
  waiting for transfers between devices  75.8 us (41%)
  starting transfers between devices  75 us (41%)
  Pallas kernels  22.7 us (12%)
  local copies, waits for them, and re-layouts  4.44 us (2%)
  other arithmetic  3.65 us (2%)
  between operations  2.29 us (1%)
    ppermute x30, waiting for transfers between devices, send(): return lax.ppermute(value, AXES, pairs)  75.8 us
    ppermute x30, starting transfers between devices, send(): return lax.ppermute(value, AXES, pairs)  75 us
    pallas_call x2, Pallas kernels, tiles(): pl.pallas_call(functools.partial(tiles_kernel, late), in_specs=[pl.BlockS...  22.7 us
  transfers between devices with their start and end apart: 30, of which 10 were waited for; matrix products, arithmetic and copies ran while one was open for 2% of the time, Pallas kernels for 6%

profile of v3, /device:TPU:5, one launch (start us, length us, event | category | flops | bytes accessed | tf_op | source)
XLA Modules:
  0.0 183.9 jit_solution(3637159021923282752)
XLA Ops:
  0.0 2.1 %constant_dynamic-slice_fusion.2 = (bf16[320,1024]{1,0:T(8,128)(2,1)S(1)}, bf16[320,1024]{1,0:T(8,128)(2,1)S(1)}) fusion(bf16[320,4096]{1,0:T(8,128)(2,1)} %bitcast.86, s32[]{:T(128)S(6)} %mul.24, s32[]{:T(128)S(6)} %mul.22), kind=kLoop, calls=%fused_computation.51 | loop fusion | bytes 2621448 | tf_op jit(solution)/shard_map/dynamic_slice | solution.py:162
  2.1 1.4 collective-permute-start.1
  3.5 1.5 collective-permute-start.2
  5.7 1.6 collective-permute-start.3
  7.3 1.6 collective-permute-start.8
  9.0 3.9 %collective-permute-start.4 = (bf16[320,1024]{1,0:T(8,128)(2,1)S(1)}, bf16[320,1024]{1,0:T(8,128)(2,1)S(1)}, u32[]{:S(2)}, u32[]{:S(2)}) collective-permute-start(bf16[320,1024]{1,0:T(8,128)(2,1)S(1)} %get-tuple-element.63.refs_0_), channel_id=1, source_target_pairs={{0,224},{1,225},{2,226},{3,227},{4,228},{5,229},{6,230},{7,231},{8... | collective-permute-start | bytes 1966088 | tf_op jit(solution)/shard_map/ppermute | solution.py:134
  12.9 6.3 %collective-permute-done.1.refs_1_ = bf16[320,1024]{1,0:T(8,128)(2,1)S(1)} collective-permute-done((bf16[320,1024]{1,0:T(8,128)(2,1)S(1)}, bf16[320,1024]{1,0:T(8,128)(2,1)S(1)}, u32[]{:S(2)}, u32[]{:S(2)}) %collective-permute-start.1) | collective-permute-done | bytes 655392 | tf_op jit(solution)/shard_map/ppermute | solution.py:134
  19.2 1.6 collective-permute-start.9
  20.8 3.9 %collective-permute-start.5 = (bf16[320,1024]{1,0:T(8,128)(2,1)S(1)}, bf16[320,1024]{1,0:T(8,128)(2,1)S(1)}, u32[]{:S(2)}, u32[]{:S(2)}) collective-permute-start(bf16[320,1024]{1,0:T(8,128)(2,1)S(1)} %collective-permute-done.1.refs_1_), channel_id=1, source_target_pairs={{0,224},{1,225},{2,226},{3,227},{4,228},{5,229},{6,230},{7,231},{8... | collective-permute-start | bytes 1966088 | tf_op jit(solution)/shard_map/ppermute | solution.py:134
  24.7 9.5 %collective-permute-done.3.refs_3_ = bf16[320,1024]{1,0:T(8,128)(2,1)S(1)} collective-permute-done((bf16[320,1024]{1,0:T(8,128)(2,1)S(1)}, bf16[320,1024]{1,0:T(8,128)(2,1)S(1)}, u32[]{:S(2)}, u32[]{:S(2)}) %collective-permute-start.3) | collective-permute-done | bytes 655392 | tf_op jit(solution)/shard_map/ppermute | solution.py:134
  34.3 1.6 collective-permute-start.10
  35.9 3.9 %collective-permute-start.6 = (bf16[320,1024]{1,0:T(8,128)(2,1)S(1)}, bf16[320,1024]{1,0:T(8,128)(2,1)S(1)}, u32[]{:S(2)}, u32[]{:S(2)}) collective-permute-start(bf16[320,1024]{1,0:T(8,128)(2,1)S(1)} %collective-permute-done.2.refs_2_), channel_id=1, source_target_pairs={{0,224},{1,225},{2,226},{3,227},{4,228},{5,229},{6,230},{7,231},{8... | collective-permute-start | bytes 1966088 | tf_op jit(solution)/shard_map/ppermute | solution.py:134
  40.5 2.0 %collective-permute-start.7 = (bf16[320,1024]{1,0:T(8,128)(2,1)S(1)}, bf16[320,1024]{1,0:T(8,128)(2,1)S(1)}, u32[]{:S(2)}, u32[]{:S(2)}) collective-permute-start(bf16[320,1024]{1,0:T(8,128)(2,1)S(1)} %collective-permute-done.3.refs_3_), channel_id=1, source_target_pairs={{0,224},{1,225},{2,226},{3,227},{4,228},{5,229},{6,230},{7,231},{8... | collective-permute-start | bytes 1966088 | tf_op jit(solution)/shard_map/ppermute | solution.py:134
  44.1 10.2 %collective-permute-done.10.refs_10_.refs_9_ = bf16[320,1024]{1,0:T(8,128)(2,1)S(1)} collective-permute-done((bf16[320,1024]{1,0:T(8,128)(2,1)S(1)}, bf16[320,1024]{1,0:T(8,128)(2,1)S(1)}, u32[]{:S(2)}, u32[]{:S(2)}) %collective-permute-start.10) | collective-permute-done | bytes 655392 | tf_op jit(solution)/shard_map/ppermute | solution.py:134
  54.3 14.0 %collective-permute-done.11.refs_11_ = bf16[320,1024]{1,0:T(8,128)(2,1)S(1)} collective-permute-done((bf16[320,1024]{1,0:T(8,128)(2,1)S(1)}, bf16[320,1024]{1,0:T(8,128)(2,1)S(1)}, u32[]{:S(2)}, u32[]{:S(2)}) %collective-permute-start.11) | collective-permute-done | bytes 655392 | tf_op jit(solution)/shard_map/ppermute | solution.py:134
  68.3 11.4 %shard_map.55 = (f32[8,160,640]{2,1,0:T(8,128)S(1)}, bf16[8,160,640]{2,1,0:T(8,128)(2,1)S(1)}) custom-call(s32[2]{0:T(128)S(1)} %pad_add_fusion.place_ref, f32[1,1024]{1,0:T(1,128)S(1)} %divide_multiply_fusion.factor_ref, bf16[320,1024]{1,0:T(8,128)(2,1)S(1)} %get-tuple-element.63.refs_0_, bf16[320,1024]{1,0:T(8,128)(2,1)S(1)} %collective-permute-done.1.refs_1_, ...), custom_call_target="tpu_custom_call" | custom-call | flops 3355443200 | bytes 7864320 | tf_op jit(solution)/shard_map/pallas_call | solution.py:101
  79.8 7.9 %collective-permute-start.12 = (bf16[2,4,160,640]{3,2,1,0:T(8,128)(2,1)S(1)}, bf16[2,4,160,640]{3,2,1,0:T(8,128)(2,1)S(1)}, u32[]{:S(2)}, u32[]{:S(2)}) collective-permute-start(bf16[2,4,160,640]{3,2,1,0:T(8,128)(2,1)S(1)} %bitcast.85), channel_id=1, source_target_pairs={{0,1},{1,0},{2,3},{3,2},{4,5},{5,4},{6,7},{7,6},{8,9},{9,8},{10,11... | collective-permute-start | bytes 4915208 | tf_op jit(solution)/shard_map/ppermute | solution.py:134
  87.6 11.2 %shard_map.56 = (f32[8,160,640]{2,1,0:T(8,128)S(1)}, bf16[8,160,640]{2,1,0:T(8,128)(2,1)S(1)}) custom-call(s32[2]{0:T(128)S(1)} %pad_add_fusion.place_ref, f32[1,1024]{1,0:T(1,128)S(1)} %divide_multiply_fusion.factor_ref, bf16[320,1024]{1,0:T(8,128)(2,1)S(1)} %get-tuple-element.63.refs_0_, bf16[320,1024]{1,0:T(8,128)(2,1)S(1)} %collective-permute-done.1.refs_1_, ...), custom_call_target="tpu_custom_call" | custom-call | flops 3355443200 | bytes 7864320 | tf_op jit(solution)/shard_map/pallas_call | solution.py:101
  102.4 2.3 %collective-permute-start.21 = (bf16[4,80,640]{2,1,0:T(8,128)(2,1)S(1)}, bf16[4,80,640]{2,1,0:T(8,128)(2,1)S(1)}, u32[]{:S(2)}, u32[]{:S(2)}) collective-permute-start(bf16[4,80,640]{2,1,0:T(8,128)(2,1)S(1)} %slice_bitcast_fusion.2), channel_id=1, source_target_pairs={{0,16},{1,17},{2,18},{3,19},{4,20},{5,21},{6,22},{7,23},{8,24},{9,... | collective-permute-start | bytes 1228808 | tf_op jit(solution)/shard_map/ppermute | solution.py:134
  105.2 5.6 %collective-permute-start.16 = (bf16[2,160,640]{2,1,0:T(8,128)(2,1)S(1)}, bf16[2,160,640]{2,1,0:T(8,128)(2,1)S(1)}, u32[]{:S(2)}, u32[]{:S(2)}) collective-permute-start(bf16[2,160,640]{2,1,0:T(8,128)(2,1)S(1)} %get-tuple-element.59), channel_id=1, source_target_pairs={{0,4},{1,5},{2,6},{3,7},{4,0},{5,1},{6,2},{7,3},{8,12},{9,13},{10,... | collective-permute-start | bytes 1228808 | tf_op jit(solution)/shard_map/ppermute | solution.py:134
  110.8 2.1 %collective-permute-start.15 = (bf16[2,160,640]{2,1,0:T(8,128)(2,1)S(1)}, bf16[2,160,640]{2,1,0:T(8,128)(2,1)S(1)}, u32[]{:S(2)}, u32[]{:S(2)}) collective-permute-start(bf16[2,160,640]{2,1,0:T(8,128)(2,1)S(1)} %get-tuple-element.60), channel_id=1, source_target_pairs={{0,6},{1,7},{2,0},{3,1},{4,2},{5,3},{6,4},{7,5},{8,14},{9,15},{10,... | collective-permute-start | bytes 1228808 | tf_op jit(solution)/shard_map/ppermute | solution.py:134
  113.1 10.5 %collective-permute-start.17 = (bf16[2,80,640]{2,1,0:T(8,128)(2,1)S(1)}, bf16[2,80,640]{2,1,0:T(8,128)(2,1)S(1)}, u32[]{:S(2)}, u32[]{:S(2)}) collective-permute-start(bf16[2,80,640]{2,1,0:T(8,128)(2,1)S(1)} %get-tuple-element.66), channel_id=1, source_target_pairs={{0,2},{1,3},{2,4},{3,5},{4,6},{5,7},{6,0},{7,1},{8,10},{9,11},{10,... | collective-permute-start | bytes 614408 | tf_op jit(solution)/shard_map/ppermute | solution.py:134
  124.8 8.4 %collective-permute-done.17 = bf16[2,80,640]{2,1,0:T(8,128)(2,1)S(1)} collective-permute-done((bf16[2,80,640]{2,1,0:T(8,128)(2,1)S(1)}, bf16[2,80,640]{2,1,0:T(8,128)(2,1)S(1)}, u32[]{:S(2)}, u32[]{:S(2)}) %collective-permute-start.17) | collective-permute-done | bytes 204832 | tf_op jit(solution)/shard_map/ppermute | solution.py:134
  133.2 3.2 %collective-permute-start.23 = (bf16[80,640]{1,0:T(8,128)(2,1)S(1)}, bf16[80,640]{1,0:T(8,128)(2,1)S(1)}, u32[]{:S(2)}, u32[]{:S(2)}) collective-permute-start(bf16[80,640]{1,0:T(8,128)(2,1)S(1)} %get-tuple-element.69), channel_id=1, source_target_pairs={{0,2},{1,3},{2,4},{3,5},{4,6},{5,7},{6,0},{7,1},{8,10},{9,11},{10,... | collective-permute-start | bytes 307208 | tf_op jit(solution)/shard_map/ppermute | solution.py:134
  136.4 4.1 %collective-permute-start.25 = (bf16[80,640]{1,0:T(8,128)(2,1)S(1)}, bf16[80,640]{1,0:T(8,128)(2,1)S(1)}, u32[]{:S(2)}, u32[]{:S(2)}) collective-permute-start(bf16[80,640]{1,0:T(8,128)(2,1)S(1)} %get-tuple-element.70), channel_id=1, source_target_pairs={{0,4},{1,5},{2,6},{3,7},{4,0},{5,1},{6,2},{7,3},{8,12},{9,13},{10,... | collective-permute-start | bytes 307208 | tf_op jit(solution)/shard_map/ppermute | solution.py:134
  142.4 3.4 %collective-permute-start.27 = (bf16[160,640]{1,0:T(8,128)(2,1)S(1)}, bf16[160,640]{1,0:T(8,128)(2,1)S(1)}, u32[]{:S(2)}, u32[]{:S(2)}) collective-permute-start(bf16[160,640]{1,0:T(8,128)(2,1)S(1)} %select_convert_fusion), channel_id=1, source_target_pairs={{0,24},{1,9},{2,26},{3,11},{4,28},{5,29},{6,30},{7,31},{8,0},{9,17... | collective-permute-start | bytes 614408 | tf_op jit(solution)/shard_map/ppermute | solution.py:134
  146.9 1.5 collective-permute-start.26
  148.5 1.1 collective-permute-done.27
  149.6 3.1 %collective-permute-done.26 = bf16[160,640]{1,0:T(8,128)(2,1)S(1)} collective-permute-done((bf16[160,640]{1,0:T(8,128)(2,1)S(1)}, bf16[160,640]{1,0:T(8,128)(2,1)S(1)}, u32[]{:S(2)}, u32[]{:S(2)}) %collective-permute-start.26) | collective-permute-done | bytes 204832 | tf_op jit(solution)/shard_map/ppermute | solution.py:134
  153.5 7.1 %collective-permute-start.28 = (f32[160,640]{1,0:T(8,128)S(1)}, f32[160,640]{1,0:T(8,128)S(1)}, u32[]{:S(2)}, u32[]{:S(2)}) collective-permute-start(f32[160,640]{1,0:T(8,128)S(1)} %fusion.7), channel_id=1, source_target_pairs={{0,254},{1,239},{2,28},{3,13},{4,35},{5,34},{6,33},{7,32},{8,6},{9... | collective-permute-start | bytes 1228808 | tf_op jit(solution)/shard_map/ppermute | solution.py:134
  160.7 21.5 %collective-permute-done.28 = f32[160,640]{1,0:T(8,128)S(1)} collective-permute-done((f32[160,640]{1,0:T(8,128)S(1)}, f32[160,640]{1,0:T(8,128)S(1)}, u32[]{:S(2)}, u32[]{:S(2)}) %collective-permute-start.28) | collective-permute-done | bytes 409632 | tf_op jit(solution)/shard_map/ppermute | solution.py:134
  182.8 1.1 maximum_select_fusion
  (68 shorter events, 10.7 us)
Async XLA Ops:
  0.0 5.0 %copy-start = (bf16[1,320,4096]{2,1,0:T(8,128)(2,1)S(1)}, bf16[1,320,4096]{2,1,0:T(8,128)(2,1)}, u32[]{:S(2)}) copy-start(bf16[1,320,4096]{2,1,0:T(8,128)(2,1)} %param.5) | copy-start | bytes 7864324
  2.1 17.1 %collective-permute-start.1 = (bf16[320,1024]{1,0:T(8,128)(2,1)S(1)}, bf16[320,1024]{1,0:T(8,128)(2,1)S(1)}, u32[]{:S(2)}, u32[]{:S(2)}) collective-permute-start(bf16[320,1024]{1,0:T(8,128)(2,1)S(1)} %get-tuple-element.41), channel_id=1, source_target_pairs={{0,8},{1,9},{2,10},{3,11},{4,12},{5,13},{6,14},{7,15},{8,16},{9,17... | collective-permute-start | bytes 1966088 | tf_op jit(solution)/shard_map/ppermute | solution.py:134
  3.5 17.3 %collective-permute-start.2 = (bf16[320,1024]{1,0:T(8,128)(2,1)S(1)}, bf16[320,1024]{1,0:T(8,128)(2,1)S(1)}, u32[]{:S(2)}, u32[]{:S(2)}) collective-permute-start(bf16[320,1024]{1,0:T(8,128)(2,1)S(1)} %get-tuple-element.42), channel_id=1, source_target_pairs={{0,24},{1,25},{2,26},{3,27},{4,28},{5,29},{6,30},{7,31},{8,0},{9,1... | collective-permute-start | bytes 1966088 | tf_op jit(solution)/shard_map/ppermute | solution.py:134
  5.7 28.6 %collective-permute-start.3 = (bf16[320,1024]{1,0:T(8,128)(2,1)S(1)}, bf16[320,1024]{1,0:T(8,128)(2,1)S(1)}, u32[]{:S(2)}, u32[]{:S(2)}) collective-permute-start(bf16[320,1024]{1,0:T(8,128)(2,1)S(1)} %get-tuple-element.62), channel_id=1, source_target_pairs={{0,16},{1,17},{2,18},{3,19},{4,20},{5,21},{6,22},{7,23},{8,24},{9,... | collective-permute-start | bytes 1966088 | tf_op jit(solution)/shard_map/ppermute | solution.py:134
  7.3 28.6 %collective-permute-start.8 = (bf16[320,1024]{1,0:T(8,128)(2,1)S(1)}, bf16[320,1024]{1,0:T(8,128)(2,1)S(1)}, u32[]{:S(2)}, u32[]{:S(2)}) collective-permute-start(bf16[320,1024]{1,0:T(8,128)(2,1)S(1)} %get-tuple-element.63.refs_0_), channel_id=1, source_target_pairs={{0,32},{1,33},{2,34},{3,35},{4,36},{5,37},{6,38},{7,39},{8,40},{9,... | collective-permute-start | bytes 1966088 | tf_op jit(solution)/shard_map/ppermute | solution.py:134
  9.0 30.9 %collective-permute-start.4 = (bf16[320,1024]{1,0:T(8,128)(2,1)S(1)}, bf16[320,1024]{1,0:T(8,128)(2,1)S(1)}, u32[]{:S(2)}, u32[]{:S(2)}) collective-permute-start(bf16[320,1024]{1,0:T(8,128)(2,1)S(1)} %get-tuple-element.63.refs_0_), channel_id=1, source_target_pairs={{0,224},{1,225},{2,226},{3,227},{4,228},{5,229},{6,230},{7,231},{8... | collective-permute-start | bytes 1966088 | tf_op jit(solution)/shard_map/ppermute | solution.py:134
  19.2 21.4 %collective-permute-start.9 = (bf16[320,1024]{1,0:T(8,128)(2,1)S(1)}, bf16[320,1024]{1,0:T(8,128)(2,1)S(1)}, u32[]{:S(2)}, u32[]{:S(2)}) collective-permute-start(bf16[320,1024]{1,0:T(8,128)(2,1)S(1)} %collective-permute-done.1.refs_1_), channel_id=1, source_target_pairs={{0,32},{1,33},{2,34},{3,35},{4,36},{5,37},{6,38},{7,39},{8,40},{9,... | collective-permute-start | bytes 1966088 | tf_op jit(solution)/shard_map/ppermute | solution.py:134
  20.8 23.3 %collective-permute-start.5 = (bf16[320,1024]{1,0:T(8,128)(2,1)S(1)}, bf16[320,1024]{1,0:T(8,128)(2,1)S(1)}, u32[]{:S(2)}, u32[]{:S(2)}) collective-permute-start(bf16[320,1024]{1,0:T(8,128)(2,1)S(1)} %collective-permute-done.1.refs_1_), channel_id=1, source_target_pairs={{0,224},{1,225},{2,226},{3,227},{4,228},{5,229},{6,230},{7,231},{8... | collective-permute-start | bytes 1966088 | tf_op jit(solution)/shard_map/ppermute | solution.py:134
  34.3 20.0 %collective-permute-start.10 = (bf16[320,1024]{1,0:T(8,128)(2,1)S(1)}, bf16[320,1024]{1,0:T(8,128)(2,1)S(1)}, u32[]{:S(2)}, u32[]{:S(2)}) collective-permute-start(bf16[320,1024]{1,0:T(8,128)(2,1)S(1)} %collective-permute-done.2.refs_2_), channel_id=1, source_target_pairs={{0,32},{1,33},{2,34},{3,35},{4,36},{5,37},{6,38},{7,39},{8,40},{9,... | collective-permute-start | bytes 1966088 | tf_op jit(solution)/shard_map/ppermute | solution.py:134
  35.9 18.3 %collective-permute-start.6 = (bf16[320,1024]{1,0:T(8,128)(2,1)S(1)}, bf16[320,1024]{1,0:T(8,128)(2,1)S(1)}, u32[]{:S(2)}, u32[]{:S(2)}) collective-permute-start(bf16[320,1024]{1,0:T(8,128)(2,1)S(1)} %collective-permute-done.2.refs_2_), channel_id=1, source_target_pairs={{0,224},{1,225},{2,226},{3,227},{4,228},{5,229},{6,230},{7,231},{8... | collective-permute-start | bytes 1966088 | tf_op jit(solution)/shard_map/ppermute | solution.py:134
  39.9 28.4 %collective-permute-start.11 = (bf16[320,1024]{1,0:T(8,128)(2,1)S(1)}, bf16[320,1024]{1,0:T(8,128)(2,1)S(1)}, u32[]{:S(2)}, u32[]{:S(2)}) collective-permute-start(bf16[320,1024]{1,0:T(8,128)(2,1)S(1)} %collective-permute-done.3.refs_3_), channel_id=1, source_target_pairs={{0,32},{1,33},{2,34},{3,35},{4,36},{5,37},{6,38},{7,39},{8,40},{9,... | collective-permute-start | bytes 1966088 | tf_op jit(solution)/shard_map/ppermute | solution.py:134
  40.5 27.8 %collective-permute-start.7 = (bf16[320,1024]{1,0:T(8,128)(2,1)S(1)}, bf16[320,1024]{1,0:T(8,128)(2,1)S(1)}, u32[]{:S(2)}, u32[]{:S(2)}) collective-permute-start(bf16[320,1024]{1,0:T(8,128)(2,1)S(1)} %collective-permute-done.3.refs_3_), channel_id=1, source_target_pairs={{0,224},{1,225},{2,226},{3,227},{4,228},{5,229},{6,230},{7,231},{8... | collective-permute-start | bytes 1966088 | tf_op jit(solution)/shard_map/ppermute | solution.py:134
  79.8 19.9 %copy-start.1 = (s32[1,8]{1,0:T(1,128)S(1)}, s32[1,8]{1,0:T(1,128)}, u32[]{:S(2)}) copy-start(s32[1,8]{1,0:T(1,128)} %param.8) | copy-start | bytes 100
  79.8 21.9 %collective-permute-start.12 = (bf16[2,4,160,640]{3,2,1,0:T(8,128)(2,1)S(1)}, bf16[2,4,160,640]{3,2,1,0:T(8,128)(2,1)S(1)}, u32[]{:S(2)}, u32[]{:S(2)}) collective-permute-start(bf16[2,4,160,640]{3,2,1,0:T(8,128)(2,1)S(1)} %bitcast.85), channel_id=1, source_target_pairs={{0,1},{1,0},{2,3},{3,2},{4,5},{5,4},{6,7},{7,6},{8,9},{9,8},{10,11... | collective-permute-start | bytes 4915208 | tf_op jit(solution)/shard_map/ppermute | solution.py:134
  98.8 5.9 %collective-permute-start.13 = (bf16[4,2,160,640]{3,2,1,0:T(8,128)(2,1)S(1)}, bf16[4,2,160,640]{3,2,1,0:T(8,128)(2,1)S(1)}, u32[]{:S(2)}, u32[]{:S(2)}) collective-permute-start(bf16[4,2,160,640]{3,2,1,0:T(8,128)(2,1)S(1)} %bitcast.84), channel_id=1, source_target_pairs={{0,1},{1,0},{2,3},{3,2},{4,5},{5,4},{6,7},{7,6},{8,9},{9,8},{10,11... | collective-permute-start | bytes 4915208 | tf_op jit(solution)/shard_map/ppermute | solution.py:134
  99.7 0.7 collective-permute-start
  102.2 10.9 %collective-permute-start.22 = (bf16[2,80,640]{2,1,0:T(8,128)(2,1)S(1)}, bf16[2,80,640]{2,1,0:T(8,128)(2,1)S(1)}, u32[]{:S(2)}, u32[]{:S(2)}) collective-permute-start(bf16[2,80,640]{2,1,0:T(8,128)(2,1)S(1)} %slice_bitcast_fusion.3), channel_id=1, source_target_pairs={{0,24},{1,9},{2,26},{3,11},{4,28},{5,13},{6,30},{7,15},{8,0},{9,17... | collective-permute-start | bytes 614408 | tf_op jit(solution)/shard_map/ppermute | solution.py:134
  102.4 21.2 %collective-permute-start.21 = (bf16[4,80,640]{2,1,0:T(8,128)(2,1)S(1)}, bf16[4,80,640]{2,1,0:T(8,128)(2,1)S(1)}, u32[]{:S(2)}, u32[]{:S(2)}) collective-permute-start(bf16[4,80,640]{2,1,0:T(8,128)(2,1)S(1)} %slice_bitcast_fusion.2), channel_id=1, source_target_pairs={{0,16},{1,17},{2,18},{3,19},{4,20},{5,21},{6,22},{7,23},{8,24},{9,... | collective-permute-start | bytes 1228808 | tf_op jit(solution)/shard_map/ppermute | solution.py:134
  105.2 28.0 %collective-permute-start.16 = (bf16[2,160,640]{2,1,0:T(8,128)(2,1)S(1)}, bf16[2,160,640]{2,1,0:T(8,128)(2,1)S(1)}, u32[]{:S(2)}, u32[]{:S(2)}) collective-permute-start(bf16[2,160,640]{2,1,0:T(8,128)(2,1)S(1)} %get-tuple-element.59), channel_id=1, source_target_pairs={{0,4},{1,5},{2,6},{3,7},{4,0},{5,1},{6,2},{7,3},{8,12},{9,13},{10,... | collective-permute-start | bytes 1228808 | tf_op jit(solution)/shard_map/ppermute | solution.py:134
  110.8 25.6 %collective-permute-start.15 = (bf16[2,160,640]{2,1,0:T(8,128)(2,1)S(1)}, bf16[2,160,640]{2,1,0:T(8,128)(2,1)S(1)}, u32[]{:S(2)}, u32[]{:S(2)}) collective-permute-start(bf16[2,160,640]{2,1,0:T(8,128)(2,1)S(1)} %get-tuple-element.60), channel_id=1, source_target_pairs={{0,6},{1,7},{2,0},{3,1},{4,2},{5,3},{6,4},{7,5},{8,14},{9,15},{10,... | collective-permute-start | bytes 1228808 | tf_op jit(solution)/shard_map/ppermute | solution.py:134
  112.9 27.6 %collective-permute-start.14 = (bf16[2,160,640]{2,1,0:T(8,128)(2,1)S(1)}, bf16[2,160,640]{2,1,0:T(8,128)(2,1)S(1)}, u32[]{:S(2)}, u32[]{:S(2)}) collective-permute-start(bf16[2,160,640]{2,1,0:T(8,128)(2,1)S(1)} %get-tuple-element.61), channel_id=1, source_target_pairs={{0,2},{1,3},{2,4},{3,5},{4,6},{5,7},{6,0},{7,1},{8,10},{9,11},{10,... | collective-permute-start | bytes 1228808 | tf_op jit(solution)/shard_map/ppermute | solution.py:134
  113.1 20.0 %collective-permute-start.17 = (bf16[2,80,640]{2,1,0:T(8,128)(2,1)S(1)}, bf16[2,80,640]{2,1,0:T(8,128)(2,1)S(1)}, u32[]{:S(2)}, u32[]{:S(2)}) collective-permute-start(bf16[2,80,640]{2,1,0:T(8,128)(2,1)S(1)} %get-tuple-element.66), channel_id=1, source_target_pairs={{0,2},{1,3},{2,4},{3,5},{4,6},{5,7},{6,0},{7,1},{8,10},{9,11},{10,... | collective-permute-start | bytes 614408 | tf_op jit(solution)/shard_map/ppermute | solution.py:134
  123.7 17.7 %collective-permute-start.19 = (bf16[2,80,640]{2,1,0:T(8,128)(2,1)S(1)}, bf16[2,80,640]{2,1,0:T(8,128)(2,1)S(1)}, u32[]{:S(2)}, u32[]{:S(2)}) collective-permute-start(bf16[2,80,640]{2,1,0:T(8,128)(2,1)S(1)} %get-tuple-element.67), channel_id=1, source_target_pairs={{0,4},{1,5},{2,6},{3,7},{4,0},{5,1},{6,2},{7,3},{8,12},{9,13},{10,... | collective-permute-start | bytes 614408 | tf_op jit(solution)/shard_map/ppermute | solution.py:134
  133.2 8.2 %collective-permute-start.18 = (bf16[2,80,640]{2,1,0:T(8,128)(2,1)S(1)}, bf16[2,80,640]{2,1,0:T(8,128)(2,1)S(1)}, u32[]{:S(2)}, u32[]{:S(2)}) collective-permute-start(bf16[2,80,640]{2,1,0:T(8,128)(2,1)S(1)} %get-tuple-element.68), channel_id=1, source_target_pairs={{0,6},{1,7},{2,0},{3,1},{4,2},{5,3},{6,4},{7,5},{8,14},{9,15},{10,... | collective-permute-start | bytes 614408 | tf_op jit(solution)/shard_map/ppermute | solution.py:134
  133.2 15.3 %collective-permute-start.23 = (bf16[80,640]{1,0:T(8,128)(2,1)S(1)}, bf16[80,640]{1,0:T(8,128)(2,1)S(1)}, u32[]{:S(2)}, u32[]{:S(2)}) collective-permute-start(bf16[80,640]{1,0:T(8,128)(2,1)S(1)} %get-tuple-element.69), channel_id=1, source_target_pairs={{0,2},{1,3},{2,4},{3,5},{4,6},{5,7},{6,0},{7,1},{8,10},{9,11},{10,... | collective-permute-start | bytes 307208 | tf_op jit(solution)/shard_map/ppermute | solution.py:134
  136.4 12.1 %collective-permute-start.25 = (bf16[80,640]{1,0:T(8,128)(2,1)S(1)}, bf16[80,640]{1,0:T(8,128)(2,1)S(1)}, u32[]{:S(2)}, u32[]{:S(2)}) collective-permute-start(bf16[80,640]{1,0:T(8,128)(2,1)S(1)} %get-tuple-element.70), channel_id=1, source_target_pairs={{0,4},{1,5},{2,6},{3,7},{4,0},{5,1},{6,2},{7,3},{8,12},{9,13},{10,... | collective-permute-start | bytes 307208 | tf_op jit(solution)/shard_map/ppermute | solution.py:134
  140.5 7.9 %collective-permute-start.24 = (bf16[80,640]{1,0:T(8,128)(2,1)S(1)}, bf16[80,640]{1,0:T(8,128)(2,1)S(1)}, u32[]{:S(2)}, u32[]{:S(2)}) collective-permute-start(bf16[80,640]{1,0:T(8,128)(2,1)S(1)} %get-tuple-element.71), channel_id=1, source_target_pairs={{0,6},{1,7},{2,0},{3,1},{4,2},{5,3},{6,4},{7,5},{8,14},{9,15},{10,... | collective-permute-start | bytes 307208 | tf_op jit(solution)/shard_map/ppermute | solution.py:134
  141.5 5.3 %collective-permute-start.20 = (bf16[80,640]{1,0:T(8,128)(2,1)S(1)}, bf16[80,640]{1,0:T(8,128)(2,1)S(1)}, u32[]{:S(2)}, u32[]{:S(2)}) collective-permute-start(bf16[80,640]{1,0:T(8,128)(2,1)S(1)} %get-tuple-element.77), channel_id=1, source_target_pairs={{0,16},{1,17},{2,18},{3,19},{4,20},{5,21},{6,22},{7,23},{8,24},{9,... | collective-permute-start | bytes 307208 | tf_op jit(solution)/shard_map/ppermute | solution.py:134
  142.4 7.2 %collective-permute-start.27 = (bf16[160,640]{1,0:T(8,128)(2,1)S(1)}, bf16[160,640]{1,0:T(8,128)(2,1)S(1)}, u32[]{:S(2)}, u32[]{:S(2)}) collective-permute-start(bf16[160,640]{1,0:T(8,128)(2,1)S(1)} %select_convert_fusion), channel_id=1, source_target_pairs={{0,24},{1,9},{2,26},{3,11},{4,28},{5,29},{6,30},{7,31},{8,0},{9,17... | collective-permute-start | bytes 614408 | tf_op jit(solution)/shard_map/ppermute | solution.py:134
  146.9 5.8 %collective-permute-start.26 = (bf16[160,640]{1,0:T(8,128)(2,1)S(1)}, bf16[160,640]{1,0:T(8,128)(2,1)S(1)}, u32[]{:S(2)}, u32[]{:S(2)}) collective-permute-start(bf16[160,640]{1,0:T(8,128)(2,1)S(1)} %fusion.13), channel_id=1, source_target_pairs={{0,8},{1,25},{2,10},{3,27},{4,12},{5,13},{6,14},{7,15},{8,16},{9,1... | collective-permute-start | bytes 614408 | tf_op jit(solution)/shard_map/ppermute | solution.py:134
  152.8 7.8 %collective-permute-start.29 = (f32[160,640]{1,0:T(8,128)S(1)}, f32[160,640]{1,0:T(8,128)S(1)}, u32[]{:S(2)}, u32[]{:S(2)}) collective-permute-start(f32[160,640]{1,0:T(8,128)S(1)} %fusion.7), channel_id=1, source_target_pairs={{0,33},{1,32},{2,35},{3,34},{4,20},{5,5},{6,246},{7,231},{8,41},{9... | collective-permute-start | bytes 1228808 | tf_op jit(solution)/shard_map/ppermute | solution.py:134
  153.5 28.7 %collective-permute-start.28 = (f32[160,640]{1,0:T(8,128)S(1)}, f32[160,640]{1,0:T(8,128)S(1)}, u32[]{:S(2)}, u32[]{:S(2)}) collective-permute-start(f32[160,640]{1,0:T(8,128)S(1)} %fusion.7), channel_id=1, source_target_pairs={{0,254},{1,239},{2,28},{3,13},{4,35},{5,34},{6,33},{7,32},{8,6},{9... | collective-permute-start | bytes 1228808 | tf_op jit(solution)/shard_map/ppermute | solution.py:134

commit v4 on v3

--- a/solution.py
+++ b/solution.py
@@ -30,90 +30,91 @@
     out_ref[index, :, rows : 2 * rows] = tile[half:].astype(out_ref.dtype)
 
 
-def product_of(right, left):
-    return lax.dot_general(right, left, (((1,), (1,)), ((), ())), preferred_element_type=jnp.float32)
-
-
 def owner(far, p):
     return jnp.where(far == 1, 3 * p, 1 + p)
 
 
-def tiles_kernel(late, place_ref, factor_ref, *refs):
-    keep_ref, give_ref, left_ref = refs[-3:]
-    pieces = refs[:-3]
-    order = (0, 3, 1, 2) if late else (0, 3, 1)
-    here = dict(zip((0, 3, 1, 2), pieces[:NY]))
-    above = dict(zip(order, pieces[NY : NY + len(order)]))
-    below = dict(zip(order, pieces[NY + len(order) :]))
-    rows = pieces[0].shape[0]
+SCALED = {
+    "prep": tuple((plane, r) for plane in (0, 1, 2) for r in (0, 3)) + ((1, 1), (1, 2)),
+    "early": ((0, 1), (2, 1)),
+    "late": ((0, 2), (2, 2)),
+}
+RIGHT = {"prep": (0, 3), "early": (0, 3, 1), "late": (0, 3, 1, 2)}
+
+
+def tiles_kernel(stage, place_ref, factor_ref, *refs):
+    count = len(SCALED[stage])
+    scaled, refs = refs[:count], refs[count:]
+    above, refs = dict(zip(RIGHT[stage], refs)), refs[len(RIGHT[stage]) :]
+    left_ref, keep_ref, give_ref = refs[-3:]
+    rows = scaled[0].shape[0]
     y = place_ref[0]
     c = place_ref[1]
-    for plane, group in enumerate((below, here, above)):
-        for rel, ref in group.items():
-            scale_into(left_ref, ref, factor_ref, (plane * NY + lax.rem(y + rel, NY)) * rows)
-
-    def left_of(r, offset, count):
-        start = (lax.rem(y + r, NY) + 2 * NY - offset) * rows
-        return left_ref[pl.ds(pl.multiple_of(start, CHUNK), count * rows), :]
-
-    @pl.loop(0, 4)
-    def _(turn):
-        far = turn // 2
-        given = lax.rem(turn, 2)
-        core = jnp.where(given == 1, 1 - c, c)
-        lowest = 4 * far + 2 * core + 1
-
-        def place(slot, p, tile):
-            index = slot * 4 + owner(far, p) if late else owner(far, p) * 2 + slot
-
-            @pl.when(given == 0)
+    for (plane, rel), ref in zip(SCALED[stage], scaled):
+        scale_into(left_ref, ref, factor_ref, (plane * NY + lax.rem(y + rel, NY)) * rows)
+
+    @pl.loop(0, 2)
+    def _(far):
+        def product(r, offset, blocks):
+            start = (lax.rem(y + r, NY) + 2 * NY - 4 * far - offset) * rows
+            left = left_ref[pl.ds(pl.multiple_of(start, CHUNK), blocks * rows), :]
+            return lax.dot_general(
+                above[r][...], left, (((1,), (1,)), ((), ())), preferred_element_type=jnp.float32
+            )
+
+        def place(core, slot, p, tile):
+            spot = owner(far, p)
+            index = slot * 4 + spot if stage == "late" else spot * 2 + slot
+
+            @pl.when(c == core)
             def _():
                 fill(keep_ref, index, tile)
 
-            @pl.when(given == 1)
+            @pl.when(c != core)
             def _():
                 fill(give_ref, index, tile)
 
-        first = core == 0
-        if late:
-            pair = product_of(above[2][...], left_of(2, lowest + 1, 2))
-            place(0, 1, pair[:, :rows])
-            place(0, 0, pair[:, rows:])
-            right = jnp.where(first, above[3][...], above[1][...])
-            place(1, 0, product_of(right, left_of(jnp.where(first, 3, 1), lowest, 1)))
-            place(1, 1, product_of(above[0][...], left_of(0, lowest + 1, 1)))
+        if stage == "prep":
+            place(0, 0, 0, product(0, 1, 1))
+            pair = product(3, 4, 2)
+            place(1, 0, 1, pair[:, :rows])
+            place(1, 1, 0, pair[:, rows:])
+        elif stage == "early":
+            pair = product(1, 2, 2)
+            place(0, 1, 1, pair[:, :rows])
+            place(0, 1, 0, pair[:, rows:])
+            place(0, 0, 1, product(3, 2, 1))
+            place(1, 1, 1, product(1, 4, 1))
+            place(1, 0, 0, product(0, 3, 1))
         else:
-            right = jnp.where(first, above[1][...], above[3][...])
-            pair = product_of(right, left_of(jnp.where(first, 1, 3), lowest + 1, 2))
-            place(jnp.where(first, 1, 0), 1, pair[:, :rows])
-            place(1, 0, pair[:, rows:])
-            right = jnp.where(first, above[3][...], above[1][...])
-            place(jnp.where(first, 0, 1), 1, product_of(right, left_of(jnp.where(first, 3, 1), lowest + 1, 1)))
-            place(0, 0, product_of(above[0][...], left_of(0, lowest, 1)))
-
-
-def tiles(late, place, factor, here, above, below):
-    order = (0, 3, 1, 2) if late else (0, 3, 1)
-    arrays = [here[r] for r in (0, 3, 1, 2)] + [above[r] for r in order] + [below[r] for r in order]
+            four = product(2, 4, 4)
+            for i, (core, p) in enumerate(((1, 1), (1, 0), (0, 1), (0, 0))):
+                place(core, 0, p, four[:, i * rows : (i + 1) * rows])
+            place(0, 1, 0, product(3, 1, 1))
+            place(1, 1, 0, product(1, 3, 1))
+            place(0, 1, 1, product(0, 2, 1))
+            place(1, 1, 1, product(0, 4, 1))
+
+
+def tiles(stage, place, factor, pieces, carried):
+    _, _, above = pieces
+    arrays = [pieces[plane][r] for plane, r in SCALED[stage]] + [above[r] for r in RIGHT[stage]]
     rows, width = arrays[0].shape
     half = rows // 2
     vmem = pl.BlockSpec(memory_space=pltpu.VMEM)
-    keep, give = pl.pallas_call(
-        functools.partial(tiles_kernel, late),
-        in_specs=[pl.BlockSpec(memory_space=pltpu.SMEM)] + [vmem] * (1 + len(arrays)),
-        out_specs=[vmem] * 2,
-        out_shape=[
-            jax.ShapeDtypeStruct((8, half, 2 * rows), jnp.float32),
-            jax.ShapeDtypeStruct((8, half, 2 * rows), jnp.bfloat16),
-        ],
-        scratch_shapes=[pltpu.VMEM((3 * NY * rows, width), jnp.bfloat16)],
-        compiler_params=pltpu.CompilerParams(vmem_limit_bytes=28 * 2**20),
+    first = 2 + len(arrays)
+    partial = jax.ShapeDtypeStruct((8, half, 2 * rows), jnp.float32)
+    return pl.pallas_call(
+        functools.partial(tiles_kernel, stage),
+        in_specs=[pl.BlockSpec(memory_space=pltpu.SMEM)] + [vmem] * (1 + len(arrays) + len(carried)),
+        out_specs=[vmem] * 3,
+        out_shape=[jax.ShapeDtypeStruct((3 * NY * rows, width), jnp.bfloat16), partial, partial],
+        input_output_aliases={first + i: i for i in range(len(carried))},
+        compiler_params=pltpu.CompilerParams(vmem_limit_bytes=24 * 2**20),
         cost_estimate=pl.CostEstimate(
-            flops=32 * rows * rows * width, bytes_accessed=12 * rows * width * 2, transcendentals=0
+            flops=20 * rows * rows * width, bytes_accessed=12 * rows * width * 2, transcendentals=0
         ),
-    )(place, factor, *arrays)
-    shape = (2, 4, half, 2 * rows) if late else (4, 2, half, 2 * rows)
-    return keep.reshape(shape), give.reshape(shape)
+    )(place, factor, *arrays, *carried)
 
 
 def local_fn(blocks):
@@ -192,7 +193,10 @@
         factor = step_size[:, None] / (jnp.sqrt(second_moment) + EPSILON) * width ** (-0.5)
         factor = lax.dynamic_slice(factor, (zero, starts[0]), (1, quarter), allow_negative_indices=False)
         place = jnp.stack([y, c])
-        keep, give = tiles(False, place, factor, here, above, below)
+        pieces = (below, here, above)
+        carried = tiles("prep", place, factor, pieces, ())
+        left, keep, give = tiles("early", place, factor, pieces, carried)
+        keep, give = (value.reshape(4, 2, rows // 2, 2 * rows) for value in (keep, give))
 
         def low_of(x):
             return x < 2
@@ -203,13 +207,12 @@
         def wide(value):
             return value.astype(jnp.float32)
 
-        given = send(give, lambda e, x, c: (e, x, 1 - c))
-        total = keep + wide(given)
+        total = keep + send(give, lambda e, x, c: (e, x, 1 - c))
         early = pick(total, 0, 0)
         arrived_early = [send(narrow(pick(total, t, 0)), lambda e, x, c, t=t: (e, x + t, c)) for t in (1, 3, 2)]
-        keep, give = tiles(True, place, factor, here, above, below)
-        given = send(give, lambda e, x, c: (e, x, 1 - c))
-        total = keep + wide(given)
+        left, keep, give = tiles("late", place, factor, pieces, (left,))
+        keep, give = (value.reshape(2, 4, rows // 2, 2 * rows) for value in (keep, give))
+        total = keep + send(give, lambda e, x, c: (e, x, 1 - c))
 
         def rest(e, c):
             return ring(e, 3 if c == 0 else 1)
@@ -237,7 +240,7 @@
             bottom = bottom + wide(value)
         top = wide(ay2) + jnp.where(low, 0.0, upper_own[1])
         final = jnp.concatenate([top, bottom], axis=0) + wide(ey1) + wide(mixed) + jnp.where(low, early[0], 0.0)
-        final = jnp.where(weight > 0, final, 0.0)
+        final = narrow(jnp.where(weight > 0, final, 0.0))
 
         def deliver(first):
             def move(e, x, c):
@@ -254,7 +257,7 @@
         def later(tile):
             return jnp.concatenate([tile[:, :rows], tile[:, rows:]], axis=0)
 
-        one, two = later(one), later(two)
+        one, two = later(wide(one)), later(wide(two))
         backward = jnp.concatenate([two, one], axis=1)
         forward = jnp.concatenate([two.T, one.T], axis=1)
         return jnp.where(later_block, forward, backward)

time: 184 us -> 168 us (0.913)
  the two profiles are of different devices: /device:TPU:5 before, /device:TPU:1 now
where the time goes in v4:
time: 168 us
  waiting for transfers between devices  71.6 us (43%)
  starting transfers between devices  64.7 us (39%)
  Pallas kernels  21.5 us (13%)
  local copies, waits for them, and re-layouts  4.42 us (3%)
  other arithmetic  3.61 us (2%)
  between operations  2.26 us (1%)
    ppermute x30, waiting for transfers between devices, send(): return lax.ppermute(value, AXES, pairs)  71.6 us
    ppermute x30, starting transfers between devices, send(): return lax.ppermute(value, AXES, pairs)  64.7 us
    pallas_call x3, Pallas kernels, tiles(): pl.pallas_call(functools.partial(tiles_kernel, stage), in_specs=[pl.Block...  21.5 us
  transfers between devices with their start and end apart: 30, of which 13 were waited for; matrix products, arithmetic and copies ran while one was open for 2% of the time, Pallas kernels for 13%

profile of v4, /device:TPU:1, one launch (start us, length us, event | category | flops | bytes accessed | tf_op | source)
XLA Modules:
  0.0 168.1 jit_solution(9554696073846837245)
XLA Ops:
  0.0 2.1 %constant_dynamic-slice_fusion.2 = (bf16[320,1024]{1,0:T(8,128)(2,1)S(1)}, bf16[320,1024]{1,0:T(8,128)(2,1)S(1)}) fusion(bf16[320,4096]{1,0:T(8,128)(2,1)} %bitcast.86, s32[]{:T(128)S(6)} %mul.24, s32[]{:T(128)S(6)} %mul.22), kind=kLoop, calls=%fused_computation.50 | loop fusion | bytes 2621448 | tf_op jit(solution)/shard_map/dynamic_slice | solution.py:163
  2.1 2.2 %collective-permute-start.5 = (bf16[320,1024]{1,0:T(8,128)(2,1)S(1)}, bf16[320,1024]{1,0:T(8,128)(2,1)S(1)}, u32[]{:S(2)}, u32[]{:S(2)}) collective-permute-start(bf16[320,1024]{1,0:T(8,128)(2,1)S(1)} %get-tuple-element.46), channel_id=1, source_target_pairs={{0,8},{1,9},{2,10},{3,11},{4,12},{5,13},{6,14},{7,15},{8,16},{9,17... | collective-permute-start | bytes 1966088 | tf_op jit(solution)/shard_map/ppermute | solution.py:135
  5.0 2.7 %collective-permute-start.1 = (bf16[320,1024]{1,0:T(8,128)(2,1)S(1)}, bf16[320,1024]{1,0:T(8,128)(2,1)S(1)}, u32[]{:S(2)}, u32[]{:S(2)}) collective-permute-start(bf16[320,1024]{1,0:T(8,128)(2,1)S(1)} %get-tuple-element.71), channel_id=1, source_target_pairs={{0,16},{1,17},{2,18},{3,19},{4,20},{5,21},{6,22},{7,23},{8,24},{9,... | collective-permute-start | bytes 1966088 | tf_op jit(solution)/shard_map/ppermute | solution.py:135
  10.4 3.9 %collective-permute-start.4 = (bf16[320,1024]{1,0:T(8,128)(2,1)S(1)}, bf16[320,1024]{1,0:T(8,128)(2,1)S(1)}, u32[]{:S(2)}, u32[]{:S(2)}) collective-permute-start(bf16[320,1024]{1,0:T(8,128)(2,1)S(1)} %get-tuple-element.70.refs_2_), channel_id=1, source_target_pairs={{0,224},{1,225},{2,226},{3,227},{4,228},{5,229},{6,230},{7,231},{8... | collective-permute-start | bytes 1966088 | tf_op jit(solution)/shard_map/ppermute | solution.py:135
  14.3 3.9 %collective-permute-done.5.refs_3_ = bf16[320,1024]{1,0:T(8,128)(2,1)S(1)} collective-permute-done((bf16[320,1024]{1,0:T(8,128)(2,1)S(1)}, bf16[320,1024]{1,0:T(8,128)(2,1)S(1)}, u32[]{:S(2)}, u32[]{:S(2)}) %collective-permute-start.5) | collective-permute-done | bytes 655392 | tf_op jit(solution)/shard_map/ppermute | solution.py:135
  18.3 3.3 %collective-permute-start.11 = (bf16[320,1024]{1,0:T(8,128)(2,1)S(1)}, bf16[320,1024]{1,0:T(8,128)(2,1)S(1)}, u32[]{:S(2)}, u32[]{:S(2)}) collective-permute-start(bf16[320,1024]{1,0:T(8,128)(2,1)S(1)} %collective-permute-done.5.refs_3_), channel_id=1, source_target_pairs={{0,32},{1,33},{2,34},{3,35},{4,36},{5,37},{6,38},{7,39},{8,40},{9,... | collective-permute-start | bytes 1966088 | tf_op jit(solution)/shard_map/ppermute | solution.py:135
  21.6 13.5 %collective-permute-done.1.refs_7_ = bf16[320,1024]{1,0:T(8,128)(2,1)S(1)} collective-permute-done((bf16[320,1024]{1,0:T(8,128)(2,1)S(1)}, bf16[320,1024]{1,0:T(8,128)(2,1)S(1)}, u32[]{:S(2)}, u32[]{:S(2)}) %collective-permute-start.1) | collective-permute-done | bytes 655392 | tf_op jit(solution)/shard_map/ppermute | solution.py:135
  35.1 5.6 %collective-permute-start.6 = (bf16[320,1024]{1,0:T(8,128)(2,1)S(1)}, bf16[320,1024]{1,0:T(8,128)(2,1)S(1)}, u32[]{:S(2)}, u32[]{:S(2)}) collective-permute-start(bf16[320,1024]{1,0:T(8,128)(2,1)S(1)} %collective-permute-done.5.refs_3_), channel_id=1, source_target_pairs={{0,224},{1,225},{2,226},{3,227},{4,228},{5,229},{6,230},{7,231},{8... | collective-permute-start | bytes 1966088 | tf_op jit(solution)/shard_map/ppermute | solution.py:135
  42.3 2.6 %collective-permute-start.3 = (bf16[320,1024]{1,0:T(8,128)(2,1)S(1)}, bf16[320,1024]{1,0:T(8,128)(2,1)S(1)}, u32[]{:S(2)}, u32[]{:S(2)}) collective-permute-start(bf16[320,1024]{1,0:T(8,128)(2,1)S(1)} %collective-permute-done.1.refs_7_), channel_id=1, source_target_pairs={{0,224},{1,225},{2,226},{3,227},{4,228},{5,229},{6,230},{7,231},{8... | collective-permute-start | bytes 1966088 | tf_op jit(solution)/shard_map/ppermute | solution.py:135
  46.4 6.9 %collective-permute-done.6.refs_5_.refs_9_.refs_3_ = bf16[320,1024]{1,0:T(8,128)(2,1)S(1)} collective-permute-done((bf16[320,1024]{1,0:T(8,128)(2,1)S(1)}, bf16[320,1024]{1,0:T(8,128)(2,1)S(1)}, u32[]{:S(2)}, u32[]{:S(2)}) %collective-permute-start.6) | collective-permute-done | bytes 655392 | tf_op jit(solution)/shard_map/ppermute | solution.py:135
  53.2 5.5 %shard_map.55 = (bf16[3840,1024]{1,0:T(8,128)(2,1)S(1)}, f32[8,160,640]{2,1,0:T(8,128)S(1)}, f32[8,160,640]{2,1,0:T(8,128)S(1)}) custom-call(s32[2]{0:T(128)S(1)} %pad_add_fusion.place_ref, f32[1,1024]{1,0:T(1,128)S(1)} %divide_multiply_fusion.factor_ref, bf16[320,1024]{1,0:T(8,128)(2,1)S(1)} %collective-permute-done.10.refs_0_, ...), custom_call_target="tpu_custom_call" | custom-call | flops 2097152000 | bytes 7864320 | tf_op jit(solution)/shard_map/pallas_call | solution.py:107
  58.8 8.5 %collective-permute-done.8.refs_1_.refs_4_ = bf16[320,1024]{1,0:T(8,128)(2,1)S(1)} collective-permute-done((bf16[320,1024]{1,0:T(8,128)(2,1)S(1)}, bf16[320,1024]{1,0:T(8,128)(2,1)S(1)}, u32[]{:S(2)}, u32[]{:S(2)}) %collective-permute-start.8) | collective-permute-done | bytes 655392 | tf_op jit(solution)/shard_map/ppermute | solution.py:135
  67.3 6.7 %shard_map.56 = (bf16[3840,1024]{1,0:T(8,128)(2,1)S(1)}, f32[8,160,640]{2,1,0:T(8,128)S(1)}, f32[8,160,640]{2,1,0:T(8,128)S(1)}) custom-call(s32[2]{0:T(128)S(1)} %pad_add_fusion.place_ref, f32[1,1024]{1,0:T(1,128)S(1)} %divide_multiply_fusion.factor_ref, ...), custom_call_target="tpu_custom_call", output_to_operand_aliasing={{0}: (7, {}), {1}: (8, {}), {2}: (9, {})} | custom-call | flops 2097152000 | bytes 7864320 | tf_op jit(solution)/shard_map/pallas_call | solution.py:107
  74.0 4.5 %collective-permute-start.13 = (f32[4,2,160,640]{3,2,1,0:T(8,128)S(1)}, f32[4,2,160,640]{3,2,1,0:T(8,128)S(1)}, u32[]{:S(2)}, u32[]{:S(2)}) collective-permute-start(f32[4,2,160,640]{3,2,1,0:T(8,128)S(1)} %bitcast.84), channel_id=1, source_target_pairs={{0,1},{1,0},{2,3},{3,2},{4,5},{5,4},{6,7},{7,6},{8,9},{9,8},{10,11... | collective-permute-start | bytes 9830408 | tf_op jit(solution)/shard_map/ppermute | solution.py:135
  78.5 2.8 %collective-permute-done.3.refs_1_.refs_5_ = bf16[320,1024]{1,0:T(8,128)(2,1)S(1)} collective-permute-done((bf16[320,1024]{1,0:T(8,128)(2,1)S(1)}, bf16[320,1024]{1,0:T(8,128)(2,1)S(1)}, u32[]{:S(2)}, u32[]{:S(2)}) %collective-permute-start.3) | collective-permute-done | bytes 655392 | tf_op jit(solution)/shard_map/ppermute | solution.py:135
  81.3 9.3 %shard_map.57 = (bf16[3840,1024]{1,0:T(8,128)(2,1)S(1)}, f32[8,160,640]{2,1,0:T(8,128)S(1)}, f32[8,160,640]{2,1,0:T(8,128)S(1)}) custom-call(s32[2]{0:T(128)S(1)} %pad_add_fusion.place_ref, f32[1,1024]{1,0:T(1,128)S(1)} %divide_multiply_fusion.factor_ref, bf16[320,1024]{1,0:T(8,128)(2,1)S(1)} %collective-permute-done.2.refs_0_, ...), custom_call_target="tpu_custom_call", output_to_operand_aliasing={{0}: (8, {})} | custom-call | flops 2097152000 | bytes 7864320 | tf_op jit(solution)/shard_map/pallas_call | solution.py:107
  90.6 2.5 %collective-permute-start.12 = (f32[2,4,160,640]{3,2,1,0:T(8,128)S(1)}, f32[2,4,160,640]{3,2,1,0:T(8,128)S(1)}, u32[]{:S(2)}, u32[]{:S(2)}) collective-permute-start(f32[2,4,160,640]{3,2,1,0:T(8,128)S(1)} %bitcast.85), channel_id=1, source_target_pairs={{0,1},{1,0},{2,3},{3,2},{4,5},{5,4},{6,7},{7,6},{8,9},{9,8},{10,11... | collective-permute-start | bytes 9830408 | tf_op jit(solution)/shard_map/ppermute | solution.py:135
  93.9 1.9 %collective-permute-start = (f32[8]{0:T(128)S(1)}, f32[8]{0:T(128)S(1)}, u32[]{:S(2)}, u32[]{:S(2)}) collective-permute-start(f32[8]{0:T(128)S(1)} %convert_reduce_fusion), channel_id=1, source_target_pairs={{0,8},{1,25},{2,234},{3,251},{4,244},{5,5},{6,22},{7,39},{8,16},{9... | collective-permute-start | bytes 104 | tf_op jit(solution)/shard_map/ppermute | solution.py:135
  95.8 4.5 %collective-permute-done = f32[8]{0:T(128)S(1)} collective-permute-done((f32[8]{0:T(128)S(1)}, f32[8]{0:T(128)S(1)}, u32[]{:S(2)}, u32[]{:S(2)}) %collective-permute-start) | collective-permute-done | bytes 64 | tf_op jit(solution)/shard_map/ppermute | solution.py:135
  102.2 2.7 %collective-permute-start.15 = (bf16[2,160,640]{2,1,0:T(8,128)(2,1)S(1)}, bf16[2,160,640]{2,1,0:T(8,128)(2,1)S(1)}, u32[]{:S(2)}, u32[]{:S(2)}) collective-permute-start(bf16[2,160,640]{2,1,0:T(8,128)(2,1)S(1)} %get-tuple-element.68), channel_id=1, source_target_pairs={{0,6},{1,7},{2,0},{3,1},{4,2},{5,3},{6,4},{7,5},{8,14},{9,15},{10,... | collective-permute-start | bytes 1228808 | tf_op jit(solution)/shard_map/ppermute | solution.py:135
  107.5 6.0 %collective-permute-done.22 = bf16[2,80,640]{2,1,0:T(8,128)(2,1)S(1)} collective-permute-done((bf16[2,80,640]{2,1,0:T(8,128)(2,1)S(1)}, bf16[2,80,640]{2,1,0:T(8,128)(2,1)S(1)}, u32[]{:S(2)}, u32[]{:S(2)}) %collective-permute-start.22) | collective-permute-done | bytes 204832 | tf_op jit(solution)/shard_map/ppermute | solution.py:135
  113.5 1.8 %collective-permute-start.18 = (bf16[2,80,640]{2,1,0:T(8,128)(2,1)S(1)}, bf16[2,80,640]{2,1,0:T(8,128)(2,1)S(1)}, u32[]{:S(2)}, u32[]{:S(2)}) collective-permute-start(bf16[2,80,640]{2,1,0:T(8,128)(2,1)S(1)} %get-tuple-element.76), channel_id=1, source_target_pairs={{0,6},{1,7},{2,0},{3,1},{4,2},{5,3},{6,4},{7,5},{8,14},{9,15},{10,... | collective-permute-start | bytes 614408 | tf_op jit(solution)/shard_map/ppermute | solution.py:135
  115.3 7.2 %collective-permute-done.17 = bf16[2,80,640]{2,1,0:T(8,128)(2,1)S(1)} collective-permute-done((bf16[2,80,640]{2,1,0:T(8,128)(2,1)S(1)}, bf16[2,80,640]{2,1,0:T(8,128)(2,1)S(1)}, u32[]{:S(2)}, u32[]{:S(2)}) %collective-permute-start.17) | collective-permute-done | bytes 204832 | tf_op jit(solution)/shard_map/ppermute | solution.py:135
  122.6 2.3 %collective-permute-start.19 = (bf16[2,80,640]{2,1,0:T(8,128)(2,1)S(1)}, bf16[2,80,640]{2,1,0:T(8,128)(2,1)S(1)}, u32[]{:S(2)}, u32[]{:S(2)}) collective-permute-start(bf16[2,80,640]{2,1,0:T(8,128)(2,1)S(1)} %get-tuple-element.75), channel_id=1, source_target_pairs={{0,4},{1,5},{2,6},{3,7},{4,0},{5,1},{6,2},{7,3},{8,12},{9,13},{10,... | collective-permute-start | bytes 614408 | tf_op jit(solution)/shard_map/ppermute | solution.py:135
  124.9 3.0 %collective-permute-start.21 = (bf16[4,80,640]{2,1,0:T(8,128)(2,1)S(1)}, bf16[4,80,640]{2,1,0:T(8,128)(2,1)S(1)}, u32[]{:S(2)}, u32[]{:S(2)}) collective-permute-start(bf16[4,80,640]{2,1,0:T(8,128)(2,1)S(1)} %slice_bitcast_fusion.2), channel_id=1, source_target_pairs={{0,16},{1,17},{2,18},{3,19},{4,20},{5,21},{6,22},{7,23},{8,24},{9,... | collective-permute-start | bytes 1228808 | tf_op jit(solution)/shard_map/ppermute | solution.py:135
  131.0 4.1 %collective-permute-start.27 = (bf16[160,640]{1,0:T(8,128)(2,1)S(1)}, bf16[160,640]{1,0:T(8,128)(2,1)S(1)}, u32[]{:S(2)}, u32[]{:S(2)}) collective-permute-start(bf16[160,640]{1,0:T(8,128)(2,1)S(1)} %select_convert_fusion), channel_id=1, source_target_pairs={{0,24},{1,9},{2,26},{3,11},{4,28},{5,29},{6,30},{7,31},{8,0},{9,17... | collective-permute-start | bytes 614408 | tf_op jit(solution)/shard_map/ppermute | solution.py:135
  136.0 2.7 %collective-permute-start.24 = (bf16[80,640]{1,0:T(8,128)(2,1)S(1)}, bf16[80,640]{1,0:T(8,128)(2,1)S(1)}, u32[]{:S(2)}, u32[]{:S(2)}) collective-permute-start(bf16[80,640]{1,0:T(8,128)(2,1)S(1)} %get-tuple-element.79), channel_id=1, source_target_pairs={{0,6},{1,7},{2,0},{3,1},{4,2},{5,3},{6,4},{7,5},{8,14},{9,15},{10,... | collective-permute-start | bytes 307208 | tf_op jit(solution)/shard_map/ppermute | solution.py:135
  138.6 4.6 %collective-permute-done.20 = bf16[80,640]{1,0:T(8,128)(2,1)S(1)} collective-permute-done((bf16[80,640]{1,0:T(8,128)(2,1)S(1)}, bf16[80,640]{1,0:T(8,128)(2,1)S(1)}, u32[]{:S(2)}, u32[]{:S(2)}) %collective-permute-start.20) | collective-permute-done | bytes 102432 | tf_op jit(solution)/shard_map/ppermute | solution.py:135
  144.6 3.9 %collective-permute-done.25 = bf16[80,640]{1,0:T(8,128)(2,1)S(1)} collective-permute-done((bf16[80,640]{1,0:T(8,128)(2,1)S(1)}, bf16[80,640]{1,0:T(8,128)(2,1)S(1)}, u32[]{:S(2)}, u32[]{:S(2)}) %collective-permute-start.25) | collective-permute-done | bytes 102432 | tf_op jit(solution)/shard_map/ppermute | solution.py:135
  148.7 4.6 %collective-permute-start.28 = (bf16[160,640]{1,0:T(8,128)(2,1)S(1)}, bf16[160,640]{1,0:T(8,128)(2,1)S(1)}, u32[]{:S(2)}, u32[]{:S(2)}) collective-permute-start(bf16[160,640]{1,0:T(8,128)(2,1)S(1)} %fusion.8), channel_id=1, source_target_pairs={{0,254},{1,239},{2,28},{3,13},{4,35},{5,34},{6,33},{7,32},{8,6},{9... | collective-permute-start | bytes 614408 | tf_op jit(solution)/shard_map/ppermute | solution.py:135
  153.3 4.5 %collective-permute-start.29 = (bf16[160,640]{1,0:T(8,128)(2,1)S(1)}, bf16[160,640]{1,0:T(8,128)(2,1)S(1)}, u32[]{:S(2)}, u32[]{:S(2)}) collective-permute-start(bf16[160,640]{1,0:T(8,128)(2,1)S(1)} %fusion.8), channel_id=1, source_target_pairs={{0,33},{1,32},{2,35},{3,34},{4,20},{5,5},{6,246},{7,231},{8,41},{9... | collective-permute-start | bytes 614408 | tf_op jit(solution)/shard_map/ppermute | solution.py:135
  158.5 7.9 %collective-permute-done.29 = bf16[160,640]{1,0:T(8,128)(2,1)S(1)} collective-permute-done((bf16[160,640]{1,0:T(8,128)(2,1)S(1)}, bf16[160,640]{1,0:T(8,128)(2,1)S(1)}, u32[]{:S(2)}, u32[]{:S(2)}) %collective-permute-start.29) | collective-permute-done | bytes 204832 | tf_op jit(solution)/shard_map/ppermute | solution.py:135
  (69 shorter events, 17.5 us)
Async XLA Ops:
  0.0 4.3 %copy-start = (bf16[1,320,4096]{2,1,0:T(8,128)(2,1)S(1)}, bf16[1,320,4096]{2,1,0:T(8,128)(2,1)}, u32[]{:S(2)}) copy-start(bf16[1,320,4096]{2,1,0:T(8,128)(2,1)} %param.5) | copy-start | bytes 7864324
  2.1 16.2 %collective-permute-start.5 = (bf16[320,1024]{1,0:T(8,128)(2,1)S(1)}, bf16[320,1024]{1,0:T(8,128)(2,1)S(1)}, u32[]{:S(2)}, u32[]{:S(2)}) collective-permute-start(bf16[320,1024]{1,0:T(8,128)(2,1)S(1)} %get-tuple-element.46), channel_id=1, source_target_pairs={{0,8},{1,9},{2,10},{3,11},{4,12},{5,13},{6,14},{7,15},{8,16},{9,17... | collective-permute-start | bytes 1966088 | tf_op jit(solution)/shard_map/ppermute | solution.py:135
  5.0 30.1 %collective-permute-start.1 = (bf16[320,1024]{1,0:T(8,128)(2,1)S(1)}, bf16[320,1024]{1,0:T(8,128)(2,1)S(1)}, u32[]{:S(2)}, u32[]{:S(2)}) collective-permute-start(bf16[320,1024]{1,0:T(8,128)(2,1)S(1)} %get-tuple-element.71), channel_id=1, source_target_pairs={{0,16},{1,17},{2,18},{3,19},{4,20},{5,21},{6,22},{7,23},{8,24},{9,... | collective-permute-start | bytes 1966088 | tf_op jit(solution)/shard_map/ppermute | solution.py:135
  7.7 33.0 %collective-permute-start.7 = (bf16[320,1024]{1,0:T(8,128)(2,1)S(1)}, bf16[320,1024]{1,0:T(8,128)(2,1)S(1)}, u32[]{:S(2)}, u32[]{:S(2)}) collective-permute-start(bf16[320,1024]{1,0:T(8,128)(2,1)S(1)} %get-tuple-element.47), channel_id=1, source_target_pairs={{0,24},{1,25},{2,26},{3,27},{4,28},{5,29},{6,30},{7,31},{8,0},{9,1... | collective-permute-start | bytes 1966088 | tf_op jit(solution)/shard_map/ppermute | solution.py:135
  8.8 32.7 %collective-permute-start.10 = (bf16[320,1024]{1,0:T(8,128)(2,1)S(1)}, bf16[320,1024]{1,0:T(8,128)(2,1)S(1)}, u32[]{:S(2)}, u32[]{:S(2)}) collective-permute-start(bf16[320,1024]{1,0:T(8,128)(2,1)S(1)} %get-tuple-element.70.refs_2_), channel_id=1, source_target_pairs={{0,32},{1,33},{2,34},{3,35},{4,36},{5,37},{6,38},{7,39},{8,40},{9,... | collective-permute-start | bytes 1966088 | tf_op jit(solution)/shard_map/ppermute | solution.py:135
  10.4 31.8 %collective-permute-start.4 = (bf16[320,1024]{1,0:T(8,128)(2,1)S(1)}, bf16[320,1024]{1,0:T(8,128)(2,1)S(1)}, u32[]{:S(2)}, u32[]{:S(2)}) collective-permute-start(bf16[320,1024]{1,0:T(8,128)(2,1)S(1)} %get-tuple-element.70.refs_2_), channel_id=1, source_target_pairs={{0,224},{1,225},{2,226},{3,227},{4,228},{5,229},{6,230},{7,231},{8... | collective-permute-start | bytes 1966088 | tf_op jit(solution)/shard_map/ppermute | solution.py:135
  18.3 24.0 %collective-permute-start.11 = (bf16[320,1024]{1,0:T(8,128)(2,1)S(1)}, bf16[320,1024]{1,0:T(8,128)(2,1)S(1)}, u32[]{:S(2)}, u32[]{:S(2)}) collective-permute-start(bf16[320,1024]{1,0:T(8,128)(2,1)S(1)} %collective-permute-done.5.refs_3_), channel_id=1, source_target_pairs={{0,32},{1,33},{2,34},{3,35},{4,36},{5,37},{6,38},{7,39},{8,40},{9,... | collective-permute-start | bytes 1966088 | tf_op jit(solution)/shard_map/ppermute | solution.py:135
  35.1 18.1 %collective-permute-start.6 = (bf16[320,1024]{1,0:T(8,128)(2,1)S(1)}, bf16[320,1024]{1,0:T(8,128)(2,1)S(1)}, u32[]{:S(2)}, u32[]{:S(2)}) collective-permute-start(bf16[320,1024]{1,0:T(8,128)(2,1)S(1)} %collective-permute-done.5.refs_3_), channel_id=1, source_target_pairs={{0,224},{1,225},{2,226},{3,227},{4,228},{5,229},{6,230},{7,231},{8... | collective-permute-start | bytes 1966088 | tf_op jit(solution)/shard_map/ppermute | solution.py:135
  40.7 26.6 %collective-permute-start.8 = (bf16[320,1024]{1,0:T(8,128)(2,1)S(1)}, bf16[320,1024]{1,0:T(8,128)(2,1)S(1)}, u32[]{:S(2)}, u32[]{:S(2)}) collective-permute-start(bf16[320,1024]{1,0:T(8,128)(2,1)S(1)} %collective-permute-done.7.refs_6_), channel_id=1, source_target_pairs={{0,224},{1,225},{2,226},{3,227},{4,228},{5,229},{6,230},{7,231},{8... | collective-permute-start | bytes 1966088 | tf_op jit(solution)/shard_map/ppermute | solution.py:135
  41.4 25.9 %collective-permute-start.9 = (bf16[320,1024]{1,0:T(8,128)(2,1)S(1)}, bf16[320,1024]{1,0:T(8,128)(2,1)S(1)}, u32[]{:S(2)}, u32[]{:S(2)}) collective-permute-start(bf16[320,1024]{1,0:T(8,128)(2,1)S(1)} %collective-permute-done.7.refs_6_), channel_id=1, source_target_pairs={{0,32},{1,33},{2,34},{3,35},{4,36},{5,37},{6,38},{7,39},{8,40},{9,... | collective-permute-start | bytes 1966088 | tf_op jit(solution)/shard_map/ppermute | solution.py:135
  42.2 36.4 %collective-permute-start.2 = (bf16[320,1024]{1,0:T(8,128)(2,1)S(1)}, bf16[320,1024]{1,0:T(8,128)(2,1)S(1)}, u32[]{:S(2)}, u32[]{:S(2)}) collective-permute-start(bf16[320,1024]{1,0:T(8,128)(2,1)S(1)} %collective-permute-done.1.refs_7_), channel_id=1, source_target_pairs={{0,32},{1,33},{2,34},{3,35},{4,36},{5,37},{6,38},{7,39},{8,40},{9,... | collective-permute-start | bytes 1966088 | tf_op jit(solution)/shard_map/ppermute | solution.py:135
  42.3 39.1 %collective-permute-start.3 = (bf16[320,1024]{1,0:T(8,128)(2,1)S(1)}, bf16[320,1024]{1,0:T(8,128)(2,1)S(1)}, u32[]{:S(2)}, u32[]{:S(2)}) collective-permute-start(bf16[320,1024]{1,0:T(8,128)(2,1)S(1)} %collective-permute-done.1.refs_7_), channel_id=1, source_target_pairs={{0,224},{1,225},{2,226},{3,227},{4,228},{5,229},{6,230},{7,231},{8... | collective-permute-start | bytes 1966088 | tf_op jit(solution)/shard_map/ppermute | solution.py:135
  74.0 27.5 %collective-permute-start.13 = (f32[4,2,160,640]{3,2,1,0:T(8,128)S(1)}, f32[4,2,160,640]{3,2,1,0:T(8,128)S(1)}, u32[]{:S(2)}, u32[]{:S(2)}) collective-permute-start(f32[4,2,160,640]{3,2,1,0:T(8,128)S(1)} %bitcast.84), channel_id=1, source_target_pairs={{0,1},{1,0},{2,3},{3,2},{4,5},{5,4},{6,7},{7,6},{8,9},{9,8},{10,11... | collective-permute-start | bytes 9830408 | tf_op jit(solution)/shard_map/ppermute | solution.py:135
  81.3 12.5 %copy-start.1 = (s32[1,8]{1,0:T(1,128)S(1)}, s32[1,8]{1,0:T(1,128)}, u32[]{:S(2)}) copy-start(s32[1,8]{1,0:T(1,128)} %param.8) | copy-start | bytes 100
  90.6 15.0 %collective-permute-start.12 = (f32[2,4,160,640]{3,2,1,0:T(8,128)S(1)}, f32[2,4,160,640]{3,2,1,0:T(8,128)S(1)}, u32[]{:S(2)}, u32[]{:S(2)}) collective-permute-start(f32[2,4,160,640]{3,2,1,0:T(8,128)S(1)} %bitcast.85), channel_id=1, source_target_pairs={{0,1},{1,0},{2,3},{3,2},{4,5},{5,4},{6,7},{7,6},{8,9},{9,8},{10,11... | collective-permute-start | bytes 9830408 | tf_op jit(solution)/shard_map/ppermute | solution.py:135
  93.9 6.4 %collective-permute-start = (f32[8]{0:T(128)S(1)}, f32[8]{0:T(128)S(1)}, u32[]{:S(2)}, u32[]{:S(2)}) collective-permute-start(f32[8]{0:T(128)S(1)} %convert_reduce_fusion), channel_id=1, source_target_pairs={{0,8},{1,25},{2,234},{3,251},{4,244},{5,5},{6,22},{7,39},{8,16},{9... | collective-permute-start | bytes 104 | tf_op jit(solution)/shard_map/ppermute | solution.py:135
  102.1 22.8 %collective-permute-start.14 = (bf16[2,160,640]{2,1,0:T(8,128)(2,1)S(1)}, bf16[2,160,640]{2,1,0:T(8,128)(2,1)S(1)}, u32[]{:S(2)}, u32[]{:S(2)}) collective-permute-start(bf16[2,160,640]{2,1,0:T(8,128)(2,1)S(1)} %get-tuple-element.69), channel_id=1, source_target_pairs={{0,2},{1,3},{2,4},{3,5},{4,6},{5,7},{6,0},{7,1},{8,10},{9,11},{10,... | collective-permute-start | bytes 1228808 | tf_op jit(solution)/shard_map/ppermute | solution.py:135
  102.2 25.7 %collective-permute-start.15 = (bf16[2,160,640]{2,1,0:T(8,128)(2,1)S(1)}, bf16[2,160,640]{2,1,0:T(8,128)(2,1)S(1)}, u32[]{:S(2)}, u32[]{:S(2)}) collective-permute-start(bf16[2,160,640]{2,1,0:T(8,128)(2,1)S(1)} %get-tuple-element.68), channel_id=1, source_target_pairs={{0,6},{1,7},{2,0},{3,1},{4,2},{5,3},{6,4},{7,5},{8,14},{9,15},{10,... | collective-permute-start | bytes 1228808 | tf_op jit(solution)/shard_map/ppermute | solution.py:135
  104.8 23.0 %collective-permute-start.16 = (bf16[2,160,640]{2,1,0:T(8,128)(2,1)S(1)}, bf16[2,160,640]{2,1,0:T(8,128)(2,1)S(1)}, u32[]{:S(2)}, u32[]{:S(2)}) collective-permute-start(bf16[2,160,640]{2,1,0:T(8,128)(2,1)S(1)} %get-tuple-element.67), channel_id=1, source_target_pairs={{0,4},{1,5},{2,6},{3,7},{4,0},{5,1},{6,2},{7,3},{8,12},{9,13},{10,... | collective-permute-start | bytes 1228808 | tf_op jit(solution)/shard_map/ppermute | solution.py:135
  106.3 16.2 %collective-permute-start.17 = (bf16[2,80,640]{2,1,0:T(8,128)(2,1)S(1)}, bf16[2,80,640]{2,1,0:T(8,128)(2,1)S(1)}, u32[]{:S(2)}, u32[]{:S(2)}) collective-permute-start(bf16[2,80,640]{2,1,0:T(8,128)(2,1)S(1)} %get-tuple-element.74), channel_id=1, source_target_pairs={{0,2},{1,3},{2,4},{3,5},{4,6},{5,7},{6,0},{7,1},{8,10},{9,11},{10,... | collective-permute-start | bytes 614408 | tf_op jit(solution)/shard_map/ppermute | solution.py:135
  107.3 6.2 %collective-permute-start.22 = (bf16[2,80,640]{2,1,0:T(8,128)(2,1)S(1)}, bf16[2,80,640]{2,1,0:T(8,128)(2,1)S(1)}, u32[]{:S(2)}, u32[]{:S(2)}) collective-permute-start(bf16[2,80,640]{2,1,0:T(8,128)(2,1)S(1)} %slice_bitcast_fusion.3), channel_id=1, source_target_pairs={{0,24},{1,9},{2,26},{3,11},{4,28},{5,13},{6,30},{7,15},{8,0},{9,17... | collective-permute-start | bytes 614408 | tf_op jit(solution)/shard_map/ppermute | solution.py:135
  113.5 16.2 %collective-permute-start.18 = (bf16[2,80,640]{2,1,0:T(8,128)(2,1)S(1)}, bf16[2,80,640]{2,1,0:T(8,128)(2,1)S(1)}, u32[]{:S(2)}, u32[]{:S(2)}) collective-permute-start(bf16[2,80,640]{2,1,0:T(8,128)(2,1)S(1)} %get-tuple-element.76), channel_id=1, source_target_pairs={{0,6},{1,7},{2,0},{3,1},{4,2},{5,3},{6,4},{7,5},{8,14},{9,15},{10,... | collective-permute-start | bytes 614408 | tf_op jit(solution)/shard_map/ppermute | solution.py:135
  122.6 8.2 %collective-permute-start.19 = (bf16[2,80,640]{2,1,0:T(8,128)(2,1)S(1)}, bf16[2,80,640]{2,1,0:T(8,128)(2,1)S(1)}, u32[]{:S(2)}, u32[]{:S(2)}) collective-permute-start(bf16[2,80,640]{2,1,0:T(8,128)(2,1)S(1)} %get-tuple-element.75), channel_id=1, source_target_pairs={{0,4},{1,5},{2,6},{3,7},{4,0},{5,1},{6,2},{7,3},{8,12},{9,13},{10,... | collective-permute-start | bytes 614408 | tf_op jit(solution)/shard_map/ppermute | solution.py:135
  124.9 10.8 %collective-permute-start.21 = (bf16[4,80,640]{2,1,0:T(8,128)(2,1)S(1)}, bf16[4,80,640]{2,1,0:T(8,128)(2,1)S(1)}, u32[]{:S(2)}, u32[]{:S(2)}) collective-permute-start(bf16[4,80,640]{2,1,0:T(8,128)(2,1)S(1)} %slice_bitcast_fusion.2), channel_id=1, source_target_pairs={{0,16},{1,17},{2,18},{3,19},{4,20},{5,21},{6,22},{7,23},{8,24},{9,... | collective-permute-start | bytes 1228808 | tf_op jit(solution)/shard_map/ppermute | solution.py:135
  128.0 20.5 %collective-permute-start.26 = (bf16[160,640]{1,0:T(8,128)(2,1)S(1)}, bf16[160,640]{1,0:T(8,128)(2,1)S(1)}, u32[]{:S(2)}, u32[]{:S(2)}) collective-permute-start(bf16[160,640]{1,0:T(8,128)(2,1)S(1)} %fusion.14), channel_id=1, source_target_pairs={{0,8},{1,25},{2,10},{3,27},{4,12},{5,13},{6,14},{7,15},{8,16},{9,1... | collective-permute-start | bytes 614408 | tf_op jit(solution)/shard_map/ppermute | solution.py:135
  131.0 17.6 %collective-permute-start.27 = (bf16[160,640]{1,0:T(8,128)(2,1)S(1)}, bf16[160,640]{1,0:T(8,128)(2,1)S(1)}, u32[]{:S(2)}, u32[]{:S(2)}) collective-permute-start(bf16[160,640]{1,0:T(8,128)(2,1)S(1)} %select_convert_fusion), channel_id=1, source_target_pairs={{0,24},{1,9},{2,26},{3,11},{4,28},{5,29},{6,30},{7,31},{8,0},{9,17... | collective-permute-start | bytes 614408 | tf_op jit(solution)/shard_map/ppermute | solution.py:135
  135.0 8.2 %collective-permute-start.20 = (bf16[80,640]{1,0:T(8,128)(2,1)S(1)}, bf16[80,640]{1,0:T(8,128)(2,1)S(1)}, u32[]{:S(2)}, u32[]{:S(2)}) collective-permute-start(bf16[80,640]{1,0:T(8,128)(2,1)S(1)} %get-tuple-element.81), channel_id=1, source_target_pairs={{0,16},{1,17},{2,18},{3,19},{4,20},{5,21},{6,22},{7,23},{8,24},{9,... | collective-permute-start | bytes 307208 | tf_op jit(solution)/shard_map/ppermute | solution.py:135
  135.9 8.7 %collective-permute-start.23 = (bf16[80,640]{1,0:T(8,128)(2,1)S(1)}, bf16[80,640]{1,0:T(8,128)(2,1)S(1)}, u32[]{:S(2)}, u32[]{:S(2)}) collective-permute-start(bf16[80,640]{1,0:T(8,128)(2,1)S(1)} %get-tuple-element.77), channel_id=1, source_target_pairs={{0,2},{1,3},{2,4},{3,5},{4,6},{5,7},{6,0},{7,1},{8,10},{9,11},{10,... | collective-permute-start | bytes 307208 | tf_op jit(solution)/shard_map/ppermute | solution.py:135
  136.0 8.6 %collective-permute-start.24 = (bf16[80,640]{1,0:T(8,128)(2,1)S(1)}, bf16[80,640]{1,0:T(8,128)(2,1)S(1)}, u32[]{:S(2)}, u32[]{:S(2)}) collective-permute-start(bf16[80,640]{1,0:T(8,128)(2,1)S(1)} %get-tuple-element.79), channel_id=1, source_target_pairs={{0,6},{1,7},{2,0},{3,1},{4,2},{5,3},{6,4},{7,5},{8,14},{9,15},{10,... | collective-permute-start | bytes 307208 | tf_op jit(solution)/shard_map/ppermute | solution.py:135
  143.2 5.3 %collective-permute-start.25 = (bf16[80,640]{1,0:T(8,128)(2,1)S(1)}, bf16[80,640]{1,0:T(8,128)(2,1)S(1)}, u32[]{:S(2)}, u32[]{:S(2)}) collective-permute-start(bf16[80,640]{1,0:T(8,128)(2,1)S(1)} %get-tuple-element.78), channel_id=1, source_target_pairs={{0,4},{1,5},{2,6},{3,7},{4,0},{5,1},{6,2},{7,3},{8,12},{9,13},{10,... | collective-permute-start | bytes 307208 | tf_op jit(solution)/shard_map/ppermute | solution.py:135
  148.7 9.7 %collective-permute-start.28 = (bf16[160,640]{1,0:T(8,128)(2,1)S(1)}, bf16[160,640]{1,0:T(8,128)(2,1)S(1)}, u32[]{:S(2)}, u32[]{:S(2)}) collective-permute-start(bf16[160,640]{1,0:T(8,128)(2,1)S(1)} %fusion.8), channel_id=1, source_target_pairs={{0,254},{1,239},{2,28},{3,13},{4,35},{5,34},{6,33},{7,32},{8,6},{9... | collective-permute-start | bytes 614408 | tf_op jit(solution)/shard_map/ppermute | solution.py:135
  153.3 13.1 %collective-permute-start.29 = (bf16[160,640]{1,0:T(8,128)(2,1)S(1)}, bf16[160,640]{1,0:T(8,128)(2,1)S(1)}, u32[]{:S(2)}, u32[]{:S(2)}) collective-permute-start(bf16[160,640]{1,0:T(8,128)(2,1)S(1)} %fusion.8), channel_id=1, source_target_pairs={{0,33},{1,32},{2,35},{3,34},{4,20},{5,5},{6,246},{7,231},{8,41},{9... | collective-permute-start | bytes 614408 | tf_op jit(solution)/shard_map/ppermute | solution.py:135

commit v5 on v4

--- a/solution.py
+++ b/solution.py
@@ -35,11 +35,13 @@
 
 
 SCALED = {
-    "prep": tuple((plane, r) for plane in (0, 1, 2) for r in (0, 3)) + ((1, 1), (1, 2)),
+    "prep": tuple((plane, r) for plane in (0, 1, 2) for r in (0, 3)) + ((1, 1),),
     "early": ((0, 1), (2, 1)),
+    "mid": ((1, 2),),
     "late": ((0, 2), (2, 2)),
 }
-RIGHT = {"prep": (0, 3), "early": (0, 3, 1), "late": (0, 3, 1, 2)}
+RIGHT = {"prep": (0, 3), "early": (0, 3, 1), "mid": (0, 3, 1), "late": (0, 3, 1, 2)}
+SPLIT = ((0, 0, 3, 1), (1, 0, 1, 3), (0, 1, 0, 2))
 
 
 def tiles_kernel(stage, place_ref, factor_ref, *refs):
@@ -53,47 +55,49 @@
     for (plane, rel), ref in zip(SCALED[stage], scaled):
         scale_into(left_ref, ref, factor_ref, (plane * NY + lax.rem(y + rel, NY)) * rows)
 
+    def product(far, r, offset, blocks):
+        start = (lax.rem(y + r, NY) + 2 * NY - 4 * far - offset) * rows
+        left = left_ref[pl.ds(pl.multiple_of(start, CHUNK), blocks * rows), :]
+        return lax.dot_general(above[r][...], left, (((1,), (1,)), ((), ())), preferred_element_type=jnp.float32)
+
+    def place(far, core, slot, p, tile):
+        spot = owner(far, p)
+        index = spot * 2 + slot if stage in ("prep", "early") else slot * 4 + spot
+
+        @pl.when(c == core)
+        def _():
+            fill(keep_ref, index, tile)
+
+        @pl.when(c != core)
+        def _():
+            fill(give_ref, index, tile)
+
     @pl.loop(0, 2)
     def _(far):
-        def product(r, offset, blocks):
-            start = (lax.rem(y + r, NY) + 2 * NY - 4 * far - offset) * rows
-            left = left_ref[pl.ds(pl.multiple_of(start, CHUNK), blocks * rows), :]
-            return lax.dot_general(
-                above[r][...], left, (((1,), (1,)), ((), ())), preferred_element_type=jnp.float32
-            )
-
-        def place(core, slot, p, tile):
-            spot = owner(far, p)
-            index = slot * 4 + spot if stage == "late" else spot * 2 + slot
-
-            @pl.when(c == core)
-            def _():
-                fill(keep_ref, index, tile)
-
-            @pl.when(c != core)
-            def _():
-                fill(give_ref, index, tile)
-
         if stage == "prep":
-            place(0, 0, 0, product(0, 1, 1))
-            pair = product(3, 4, 2)
-            place(1, 0, 1, pair[:, :rows])
-            place(1, 1, 0, pair[:, rows:])
+            place(far, 0, 0, 0, product(far, 0, 1, 1))
+            pair = product(far, 3, 4, 2)
+            place(far, 1, 0, 1, pair[:, :rows])
+            place(far, 1, 1, 0, pair[:, rows:])
         elif stage == "early":
-            pair = product(1, 2, 2)
-            place(0, 1, 1, pair[:, :rows])
-            place(0, 1, 0, pair[:, rows:])
-            place(0, 0, 1, product(3, 2, 1))
-            place(1, 1, 1, product(1, 4, 1))
-            place(1, 0, 0, product(0, 3, 1))
+            pair = product(far, 1, 2, 2)
+            place(far, 0, 1, 1, pair[:, :rows])
+            place(far, 0, 1, 0, pair[:, rows:])
+            place(far, 0, 0, 1, product(far, 3, 2, 1))
+            place(far, 1, 1, 1, product(far, 1, 4, 1))
+            place(far, 1, 0, 0, product(far, 0, 3, 1))
+        elif stage == "mid":
+            place(far, 1, 1, 1, product(far, 0, 4, 1))
         else:
-            four = product(2, 4, 4)
+            four = product(far, 2, 4, 4)
             for i, (core, p) in enumerate(((1, 1), (1, 0), (0, 1), (0, 0))):
-                place(core, 0, p, four[:, i * rows : (i + 1) * rows])
-            place(0, 1, 0, product(3, 1, 1))
-            place(1, 1, 0, product(1, 3, 1))
-            place(0, 1, 1, product(0, 2, 1))
-            place(1, 1, 1, product(0, 4, 1))
+                place(far, core, 0, p, four[:, i * rows : (i + 1) * rows])
+
+    if stage in ("mid", "late"):
+        for core, p, r, offset in SPLIT:
+            far = jnp.where(lax.rem(y + r, NY) < offset, 0, 1)
+            far = 1 - far if stage == "late" else far
+            place(far, core, 1, p, product(far, r, offset, 1))
 
 
 def tiles(stage, place, factor, pieces, carried):
@@ -196,6 +200,7 @@
         pieces = (below, here, above)
         carried = tiles("prep", place, factor, pieces, ())
         left, keep, give = tiles("early", place, factor, pieces, carried)
+        carried = tiles("mid", place, factor, pieces, (left,))
         keep, give = (value.reshape(4, 2, rows // 2, 2 * rows) for value in (keep, give))
 
         def low_of(x):
@@ -210,7 +215,7 @@
         total = keep + send(give, lambda e, x, c: (e, x, 1 - c))
         early = pick(total, 0, 0)
         arrived_early = [send(narrow(pick(total, t, 0)), lambda e, x, c, t=t: (e, x + t, c)) for t in (1, 3, 2)]
-        left, keep, give = tiles("late", place, factor, pieces, (left,))
+        left, keep, give = tiles("late", place, factor, pieces, carried)
         keep, give = (value.reshape(2, 4, rows // 2, 2 * rows) for value in (keep, give))
         total = keep + send(give, lambda e, x, c: (e, x, 1 - c))
 

time: 168 us -> 162 us (0.964)
  waiting for transfers between devices: 71.6 us -> 63.4 us
    ppermute x30, waiting for transfers between devices: 71.6 us -> 63.4 us  [send(): return lax.ppermute(value, AXES, pairs)]
    pallas_call x3 -> x4, Pallas kernels: 21.5 us -> 22.1 us  [tiles(): pl.pallas_call(functools.partial(tiles_kernel, stage), in_specs=[pl.Block...]
  transfers between devices with their start and end apart: 30 -> 30, of which waited for: 13 -> 12; matrix products, arithmetic and copies ran while one was open for 2% -> 3% of each run, Pallas kernels for 13% -> 10%
where the time goes in v5:
time: 162 us
  starting transfers between devices  65.6 us (40%)
  waiting for transfers between devices  63.4 us (39%)
  Pallas kernels  22.1 us (14%)
  local copies, waits for them, and re-layouts  4.41 us (3%)
  other arithmetic  3.75 us (2%)
  between operations  2.28 us (1%)
    ppermute x30, starting transfers between devices, send(): return lax.ppermute(value, AXES, pairs)  65.6 us
    ppermute x30, waiting for transfers between devices, send(): return lax.ppermute(value, AXES, pairs)  63.4 us
    pallas_call x4, Pallas kernels, tiles(): pl.pallas_call(functools.partial(tiles_kernel, stage), in_specs=[pl.Block...  22.1 us
  transfers between devices with their start and end apart: 30, of which 12 were waited for; matrix products, arithmetic and copies ran while one was open for 3% of the time, Pallas kernels for 10%

profile of v5, /device:TPU:1, one launch (start us, length us, event | category | flops | bytes accessed | tf_op | source)
XLA Modules:
  0.0 161.6 jit_solution(6653659043068499705)
XLA Ops:
  0.0 2.1 %constant_dynamic-slice_fusion.2 = (bf16[320,1024]{1,0:T(8,128)(2,1)S(1)}, bf16[320,1024]{1,0:T(8,128)(2,1)S(1)}) fusion(bf16[320,4096]{1,0:T(8,128)(2,1)} %bitcast.86, s32[]{:T(128)S(6)} %mul.24, s32[]{:T(128)S(6)} %mul.22), kind=kLoop, calls=%fused_computation.50 | loop fusion | bytes 2621448 | tf_op jit(solution)/shard_map/dynamic_slice | solution.py:167
  2.1 2.2 %collective-permute-start.5 = (bf16[320,1024]{1,0:T(8,128)(2,1)S(1)}, bf16[320,1024]{1,0:T(8,128)(2,1)S(1)}, u32[]{:S(2)}, u32[]{:S(2)}) collective-permute-start(bf16[320,1024]{1,0:T(8,128)(2,1)S(1)} %get-tuple-element.49), channel_id=1, source_target_pairs={{0,8},{1,9},{2,10},{3,11},{4,12},{5,13},{6,14},{7,15},{8,16},{9,17... | collective-permute-start | bytes 1966088 | tf_op jit(solution)/shard_map/ppermute | solution.py:139
  6.6 1.6 collective-permute-start.1
  8.2 1.6 %collective-permute-start.10 = (bf16[320,1024]{1,0:T(8,128)(2,1)S(1)}, bf16[320,1024]{1,0:T(8,128)(2,1)S(1)}, u32[]{:S(2)}, u32[]{:S(2)}) collective-permute-start(bf16[320,1024]{1,0:T(8,128)(2,1)S(1)} %get-tuple-element.76.refs_2_), channel_id=1, source_target_pairs={{0,32},{1,33},{2,34},{3,35},{4,36},{5,37},{6,38},{7,39},{8,40},{9,... | collective-permute-start | bytes 1966088 | tf_op jit(solution)/shard_map/ppermute | solution.py:139
  9.8 3.9 %collective-permute-start.4 = (bf16[320,1024]{1,0:T(8,128)(2,1)S(1)}, bf16[320,1024]{1,0:T(8,128)(2,1)S(1)}, u32[]{:S(2)}, u32[]{:S(2)}) collective-permute-start(bf16[320,1024]{1,0:T(8,128)(2,1)S(1)} %get-tuple-element.76.refs_2_), channel_id=1, source_target_pairs={{0,224},{1,225},{2,226},{3,227},{4,228},{5,229},{6,230},{7,231},{8... | collective-permute-start | bytes 1966088 | tf_op jit(solution)/shard_map/ppermute | solution.py:139
  13.7 4.5 %collective-permute-done.5.refs_3_ = bf16[320,1024]{1,0:T(8,128)(2,1)S(1)} collective-permute-done((bf16[320,1024]{1,0:T(8,128)(2,1)S(1)}, bf16[320,1024]{1,0:T(8,128)(2,1)S(1)}, u32[]{:S(2)}, u32[]{:S(2)}) %collective-permute-start.5) | collective-permute-done | bytes 655392 | tf_op jit(solution)/shard_map/ppermute | solution.py:139
  18.3 3.3 %collective-permute-start.11 = (bf16[320,1024]{1,0:T(8,128)(2,1)S(1)}, bf16[320,1024]{1,0:T(8,128)(2,1)S(1)}, u32[]{:S(2)}, u32[]{:S(2)}) collective-permute-start(bf16[320,1024]{1,0:T(8,128)(2,1)S(1)} %collective-permute-done.5.refs_3_), channel_id=1, source_target_pairs={{0,32},{1,33},{2,34},{3,35},{4,36},{5,37},{6,38},{7,39},{8,40},{9,... | collective-permute-start | bytes 1966088 | tf_op jit(solution)/shard_map/ppermute | solution.py:139
  21.6 3.9 %collective-permute-start.6 = (bf16[320,1024]{1,0:T(8,128)(2,1)S(1)}, bf16[320,1024]{1,0:T(8,128)(2,1)S(1)}, u32[]{:S(2)}, u32[]{:S(2)}) collective-permute-start(bf16[320,1024]{1,0:T(8,128)(2,1)S(1)} %collective-permute-done.5.refs_3_), channel_id=1, source_target_pairs={{0,224},{1,225},{2,226},{3,227},{4,228},{5,229},{6,230},{7,231},{8... | collective-permute-start | bytes 1966088 | tf_op jit(solution)/shard_map/ppermute | solution.py:139
  25.6 9.5 %collective-permute-done.1.refs_0_ = bf16[320,1024]{1,0:T(8,128)(2,1)S(1)} collective-permute-done((bf16[320,1024]{1,0:T(8,128)(2,1)S(1)}, bf16[320,1024]{1,0:T(8,128)(2,1)S(1)}, u32[]{:S(2)}, u32[]{:S(2)}) %collective-permute-start.1) | collective-permute-done | bytes 655392 | tf_op jit(solution)/shard_map/ppermute | solution.py:139
  35.1 1.6 %collective-permute-start.9 = (bf16[320,1024]{1,0:T(8,128)(2,1)S(1)}, bf16[320,1024]{1,0:T(8,128)(2,1)S(1)}, u32[]{:S(2)}, u32[]{:S(2)}) collective-permute-start(bf16[320,1024]{1,0:T(8,128)(2,1)S(1)} %collective-permute-done.7.refs_6_), channel_id=1, source_target_pairs={{0,32},{1,33},{2,34},{3,35},{4,36},{5,37},{6,38},{7,39},{8,40},{9,... | collective-permute-start | bytes 1966088 | tf_op jit(solution)/shard_map/ppermute | solution.py:139
  36.8 3.9 %collective-permute-start.8 = (bf16[320,1024]{1,0:T(8,128)(2,1)S(1)}, bf16[320,1024]{1,0:T(8,128)(2,1)S(1)}, u32[]{:S(2)}, u32[]{:S(2)}) collective-permute-start(bf16[320,1024]{1,0:T(8,128)(2,1)S(1)} %collective-permute-done.7.refs_6_), channel_id=1, source_target_pairs={{0,224},{1,225},{2,226},{3,227},{4,228},{5,229},{6,230},{7,231},{8... | collective-permute-start | bytes 1966088 | tf_op jit(solution)/shard_map/ppermute | solution.py:139
  42.2 1.5 collective-permute-start.3
  43.8 5.3 %shard_map.55 = (bf16[3840,1024]{1,0:T(8,128)(2,1)S(1)}, f32[8,160,640]{2,1,0:T(8,128)S(1)}, f32[8,160,640]{2,1,0:T(8,128)S(1)}) custom-call(s32[2]{0:T(128)S(1)} %pad_add_fusion.place_ref, f32[1,1024]{1,0:T(1,128)S(1)} %divide_multiply_fusion.factor_ref, bf16[320,1024]{1,0:T(8,128)(2,1)S(1)} %collective-permute-done.10.refs_0_, ...), custom_call_target="tpu_custom_call" | custom-call | flops 2097152000 | bytes 7864320 | tf_op jit(solution)/shard_map/pallas_call | solution.py:111
  49.1 6.0 %collective-permute-done.9.refs_0_ = bf16[320,1024]{1,0:T(8,128)(2,1)S(1)} collective-permute-done((bf16[320,1024]{1,0:T(8,128)(2,1)S(1)}, bf16[320,1024]{1,0:T(8,128)(2,1)S(1)}, u32[]{:S(2)}, u32[]{:S(2)}) %collective-permute-start.9) | collective-permute-done | bytes 655392 | tf_op jit(solution)/shard_map/ppermute | solution.py:139
  55.1 6.7 %shard_map.56 = (bf16[3840,1024]{1,0:T(8,128)(2,1)S(1)}, f32[8,160,640]{2,1,0:T(8,128)S(1)}, f32[8,160,640]{2,1,0:T(8,128)S(1)}) custom-call(s32[2]{0:T(128)S(1)} %pad_add_fusion.place_ref, f32[1,1024]{1,0:T(1,128)S(1)} %divide_multiply_fusion.factor_ref, ...), custom_call_target="tpu_custom_call", output_to_operand_aliasing={{0}: (7, {}), {1}: (8, {}), {2}: (9, {})} | custom-call | flops 2097152000 | bytes 7864320 | tf_op jit(solution)/shard_map/pallas_call | solution.py:111
  61.8 4.0 %shard_map.57 = (bf16[3840,1024]{1,0:T(8,128)(2,1)S(1)}, f32[8,160,640]{2,1,0:T(8,128)S(1)}, f32[8,160,640]{2,1,0:T(8,128)S(1)}) custom-call(s32[2]{0:T(128)S(1)} %pad_add_fusion.place_ref, f32[1,1024]{1,0:T(1,128)S(1)} %divide_multiply_fusion.factor_ref, bf16[320,1024]{1,0:T(8,128)(2,1)S(1)} %collective-permute-done.1.refs_0_, ...), custom_call_target="tpu_custom_call", output_to_operand_aliasing={{0}: (6, {})} | custom-call | flops 2097152000 | bytes 7864320 | tf_op jit(solution)/shard_map/pallas_call | solution.py:111
  65.8 3.3 %collective-permute-done.3.refs_1_.refs_5_ = bf16[320,1024]{1,0:T(8,128)(2,1)S(1)} collective-permute-done((bf16[320,1024]{1,0:T(8,128)(2,1)S(1)}, bf16[320,1024]{1,0:T(8,128)(2,1)S(1)}, u32[]{:S(2)}, u32[]{:S(2)}) %collective-permute-start.3) | collective-permute-done | bytes 655392 | tf_op jit(solution)/shard_map/ppermute | solution.py:139
  69.1 6.1 %shard_map.58 = (bf16[3840,1024]{1,0:T(8,128)(2,1)S(1)}, f32[8,160,640]{2,1,0:T(8,128)S(1)}, f32[8,160,640]{2,1,0:T(8,128)S(1)}) custom-call(s32[2]{0:T(128)S(1)} %pad_add_fusion.place_ref, f32[1,1024]{1,0:T(1,128)S(1)} %divide_multiply_fusion.factor_ref, ...), custom_call_target="tpu_custom_call", output_to_operand_aliasing={{0}: (8, {}), {1}: (9, {}), {2}: (10, {})} | custom-call | flops 2097152000 | bytes 7864320 | tf_op jit(solution)/shard_map/pallas_call | solution.py:111
  75.2 11.5 %collective-permute-start.12 = (f32[2,4,160,640]{3,2,1,0:T(8,128)S(1)}, f32[2,4,160,640]{3,2,1,0:T(8,128)S(1)}, u32[]{:S(2)}, u32[]{:S(2)}) collective-permute-start(f32[2,4,160,640]{3,2,1,0:T(8,128)S(1)} %bitcast.84), channel_id=1, source_target_pairs={{0,1},{1,0},{2,3},{3,2},{4,5},{5,4},{6,7},{7,6},{8,9},{9,8},{10,11... | collective-permute-start | bytes 9830408 | tf_op jit(solution)/shard_map/ppermute | solution.py:139
  87.7 2.9 %collective-permute-start = (f32[8]{0:T(128)S(1)}, f32[8]{0:T(128)S(1)}, u32[]{:S(2)}, u32[]{:S(2)}) collective-permute-start(f32[8]{0:T(128)S(1)} %convert_reduce_fusion), channel_id=1, source_target_pairs={{0,8},{1,25},{2,234},{3,251},{4,244},{5,5},{6,22},{7,39},{8,16},{9... | collective-permute-start | bytes 104 | tf_op jit(solution)/shard_map/ppermute | solution.py:139
  90.6 3.5 %collective-permute-done = f32[8]{0:T(128)S(1)} collective-permute-done((f32[8]{0:T(128)S(1)}, f32[8]{0:T(128)S(1)}, u32[]{:S(2)}, u32[]{:S(2)}) %collective-permute-start) | collective-permute-done | bytes 64 | tf_op jit(solution)/shard_map/ppermute | solution.py:139
  96.2 2.1 %collective-permute-start.21 = (bf16[4,80,640]{2,1,0:T(8,128)(2,1)S(1)}, bf16[4,80,640]{2,1,0:T(8,128)(2,1)S(1)}, u32[]{:S(2)}, u32[]{:S(2)}) collective-permute-start(bf16[4,80,640]{2,1,0:T(8,128)(2,1)S(1)} %slice_bitcast_fusion.2), channel_id=1, source_target_pairs={{0,16},{1,17},{2,18},{3,19},{4,20},{5,21},{6,22},{7,23},{8,24},{9,... | collective-permute-start | bytes 1228808 | tf_op jit(solution)/shard_map/ppermute | solution.py:139
  100.3 2.6 %collective-permute-start.15 = (bf16[2,160,640]{2,1,0:T(8,128)(2,1)S(1)}, bf16[2,160,640]{2,1,0:T(8,128)(2,1)S(1)}, u32[]{:S(2)}, u32[]{:S(2)}) collective-permute-start(bf16[2,160,640]{2,1,0:T(8,128)(2,1)S(1)} %get-tuple-element.74), channel_id=1, source_target_pairs={{0,6},{1,7},{2,0},{3,1},{4,2},{5,3},{6,4},{7,5},{8,14},{9,15},{10,... | collective-permute-start | bytes 1228808 | tf_op jit(solution)/shard_map/ppermute | solution.py:139
  103.0 7.9 %collective-permute-done.22 = bf16[2,80,640]{2,1,0:T(8,128)(2,1)S(1)} collective-permute-done((bf16[2,80,640]{2,1,0:T(8,128)(2,1)S(1)}, bf16[2,80,640]{2,1,0:T(8,128)(2,1)S(1)}, u32[]{:S(2)}, u32[]{:S(2)}) %collective-permute-start.22) | collective-permute-done | bytes 204832 | tf_op jit(solution)/shard_map/ppermute | solution.py:139
  112.4 2.2 %collective-permute-start.19 = (bf16[2,80,640]{2,1,0:T(8,128)(2,1)S(1)}, bf16[2,80,640]{2,1,0:T(8,128)(2,1)S(1)}, u32[]{:S(2)}, u32[]{:S(2)}) collective-permute-start(bf16[2,80,640]{2,1,0:T(8,128)(2,1)S(1)} %get-tuple-element.81), channel_id=1, source_target_pairs={{0,4},{1,5},{2,6},{3,7},{4,0},{5,1},{6,2},{7,3},{8,12},{9,13},{10,... | collective-permute-start | bytes 614408 | tf_op jit(solution)/shard_map/ppermute | solution.py:139
  114.7 12.4 %collective-permute-done.17 = bf16[2,80,640]{2,1,0:T(8,128)(2,1)S(1)} collective-permute-done((bf16[2,80,640]{2,1,0:T(8,128)(2,1)S(1)}, bf16[2,80,640]{2,1,0:T(8,128)(2,1)S(1)}, u32[]{:S(2)}, u32[]{:S(2)}) %collective-permute-start.17) | collective-permute-done | bytes 204832 | tf_op jit(solution)/shard_map/ppermute | solution.py:139
  129.2 1.9 %collective-permute-start.24 = (bf16[80,640]{1,0:T(8,128)(2,1)S(1)}, bf16[80,640]{1,0:T(8,128)(2,1)S(1)}, u32[]{:S(2)}, u32[]{:S(2)}) collective-permute-start(bf16[80,640]{1,0:T(8,128)(2,1)S(1)} %get-tuple-element.85), channel_id=1, source_target_pairs={{0,6},{1,7},{2,0},{3,1},{4,2},{5,3},{6,4},{7,5},{8,14},{9,15},{10,... | collective-permute-start | bytes 307208 | tf_op jit(solution)/shard_map/ppermute | solution.py:139
  134.3 5.3 %collective-permute-done.20 = bf16[80,640]{1,0:T(8,128)(2,1)S(1)} collective-permute-done((bf16[80,640]{1,0:T(8,128)(2,1)S(1)}, bf16[80,640]{1,0:T(8,128)(2,1)S(1)}, u32[]{:S(2)}, u32[]{:S(2)}) %collective-permute-start.20) | collective-permute-done | bytes 102432 | tf_op jit(solution)/shard_map/ppermute | solution.py:139
  139.7 5.7 %collective-permute-done.27 = bf16[160,640]{1,0:T(8,128)(2,1)S(1)} collective-permute-done((bf16[160,640]{1,0:T(8,128)(2,1)S(1)}, bf16[160,640]{1,0:T(8,128)(2,1)S(1)}, u32[]{:S(2)}, u32[]{:S(2)}) %collective-permute-start.27) | collective-permute-done | bytes 204832 | tf_op jit(solution)/shard_map/ppermute | solution.py:139
  145.6 2.1 %collective-permute-start.28 = (bf16[160,640]{1,0:T(8,128)(2,1)S(1)}, bf16[160,640]{1,0:T(8,128)(2,1)S(1)}, u32[]{:S(2)}, u32[]{:S(2)}) collective-permute-start(bf16[160,640]{1,0:T(8,128)(2,1)S(1)} %fusion.8), channel_id=1, source_target_pairs={{0,254},{1,239},{2,28},{3,13},{4,35},{5,34},{6,33},{7,32},{8,6},{9... | collective-permute-start | bytes 614408 | tf_op jit(solution)/shard_map/ppermute | solution.py:139
  147.7 7.5 %collective-permute-start.29 = (bf16[160,640]{1,0:T(8,128)(2,1)S(1)}, bf16[160,640]{1,0:T(8,128)(2,1)S(1)}, u32[]{:S(2)}, u32[]{:S(2)}) collective-permute-start(bf16[160,640]{1,0:T(8,128)(2,1)S(1)} %fusion.8), channel_id=1, source_target_pairs={{0,33},{1,32},{2,35},{3,34},{4,20},{5,5},{6,246},{7,231},{8,41},{9... | collective-permute-start | bytes 614408 | tf_op jit(solution)/shard_map/ppermute | solution.py:139
  155.9 4.0 %collective-permute-done.29 = bf16[160,640]{1,0:T(8,128)(2,1)S(1)} collective-permute-done((bf16[160,640]{1,0:T(8,128)(2,1)S(1)}, bf16[160,640]{1,0:T(8,128)(2,1)S(1)}, u32[]{:S(2)}, u32[]{:S(2)}) %collective-permute-start.29) | collective-permute-done | bytes 204832 | tf_op jit(solution)/shard_map/ppermute | solution.py:139
  (70 shorter events, 16.3 us)
Async XLA Ops:
  0.0 5.8 %copy-start = (bf16[1,320,4096]{2,1,0:T(8,128)(2,1)S(1)}, bf16[1,320,4096]{2,1,0:T(8,128)(2,1)}, u32[]{:S(2)}) copy-start(bf16[1,320,4096]{2,1,0:T(8,128)(2,1)} %param.5) | copy-start | bytes 7864324
  2.1 16.2 %collective-permute-start.5 = (bf16[320,1024]{1,0:T(8,128)(2,1)S(1)}, bf16[320,1024]{1,0:T(8,128)(2,1)S(1)}, u32[]{:S(2)}, u32[]{:S(2)}) collective-permute-start(bf16[320,1024]{1,0:T(8,128)(2,1)S(1)} %get-tuple-element.49), channel_id=1, source_target_pairs={{0,8},{1,9},{2,10},{3,11},{4,12},{5,13},{6,14},{7,15},{8,16},{9,17... | collective-permute-start | bytes 1966088 | tf_op jit(solution)/shard_map/ppermute | solution.py:139
  4.3 17.3 %collective-permute-start.7 = (bf16[320,1024]{1,0:T(8,128)(2,1)S(1)}, bf16[320,1024]{1,0:T(8,128)(2,1)S(1)}, u32[]{:S(2)}, u32[]{:S(2)}) collective-permute-start(bf16[320,1024]{1,0:T(8,128)(2,1)S(1)} %get-tuple-element.50), channel_id=1, source_target_pairs={{0,24},{1,25},{2,26},{3,27},{4,28},{5,29},{6,30},{7,31},{8,0},{9,1... | collective-permute-start | bytes 1966088 | tf_op jit(solution)/shard_map/ppermute | solution.py:139
  6.6 28.6 %collective-permute-start.1 = (bf16[320,1024]{1,0:T(8,128)(2,1)S(1)}, bf16[320,1024]{1,0:T(8,128)(2,1)S(1)}, u32[]{:S(2)}, u32[]{:S(2)}) collective-permute-start(bf16[320,1024]{1,0:T(8,128)(2,1)S(1)} %get-tuple-element.77), channel_id=1, source_target_pairs={{0,16},{1,17},{2,18},{3,19},{4,20},{5,21},{6,22},{7,23},{8,24},{9,... | collective-permute-start | bytes 1966088 | tf_op jit(solution)/shard_map/ppermute | solution.py:139
  8.2 28.6 %collective-permute-start.10 = (bf16[320,1024]{1,0:T(8,128)(2,1)S(1)}, bf16[320,1024]{1,0:T(8,128)(2,1)S(1)}, u32[]{:S(2)}, u32[]{:S(2)}) collective-permute-start(bf16[320,1024]{1,0:T(8,128)(2,1)S(1)} %get-tuple-element.76.refs_2_), channel_id=1, source_target_pairs={{0,32},{1,33},{2,34},{3,35},{4,36},{5,37},{6,38},{7,39},{8,40},{9,... | collective-permute-start | bytes 1966088 | tf_op jit(solution)/shard_map/ppermute | solution.py:139
  9.8 32.3 %collective-permute-start.4 = (bf16[320,1024]{1,0:T(8,128)(2,1)S(1)}, bf16[320,1024]{1,0:T(8,128)(2,1)S(1)}, u32[]{:S(2)}, u32[]{:S(2)}) collective-permute-start(bf16[320,1024]{1,0:T(8,128)(2,1)S(1)} %get-tuple-element.76.refs_2_), channel_id=1, source_target_pairs={{0,224},{1,225},{2,226},{3,227},{4,228},{5,229},{6,230},{7,231},{8... | collective-permute-start | bytes 1966088 | tf_op jit(solution)/shard_map/ppermute | solution.py:139
  18.3 25.4 %collective-permute-start.11 = (bf16[320,1024]{1,0:T(8,128)(2,1)S(1)}, bf16[320,1024]{1,0:T(8,128)(2,1)S(1)}, u32[]{:S(2)}, u32[]{:S(2)}) collective-permute-start(bf16[320,1024]{1,0:T(8,128)(2,1)S(1)} %collective-permute-done.5.refs_3_), channel_id=1, source_target_pairs={{0,32},{1,33},{2,34},{3,35},{4,36},{5,37},{6,38},{7,39},{8,40},{9,... | collective-permute-start | bytes 1966088 | tf_op jit(solution)/shard_map/ppermute | solution.py:139
  21.6 22.2 %collective-permute-start.6 = (bf16[320,1024]{1,0:T(8,128)(2,1)S(1)}, bf16[320,1024]{1,0:T(8,128)(2,1)S(1)}, u32[]{:S(2)}, u32[]{:S(2)}) collective-permute-start(bf16[320,1024]{1,0:T(8,128)(2,1)S(1)} %collective-permute-done.5.refs_3_), channel_id=1, source_target_pairs={{0,224},{1,225},{2,226},{3,227},{4,228},{5,229},{6,230},{7,231},{8... | collective-permute-start | bytes 1966088 | tf_op jit(solution)/shard_map/ppermute | solution.py:139
  35.1 20.0 %collective-permute-start.9 = (bf16[320,1024]{1,0:T(8,128)(2,1)S(1)}, bf16[320,1024]{1,0:T(8,128)(2,1)S(1)}, u32[]{:S(2)}, u32[]{:S(2)}) collective-permute-start(bf16[320,1024]{1,0:T(8,128)(2,1)S(1)} %collective-permute-done.7.refs_6_), channel_id=1, source_target_pairs={{0,32},{1,33},{2,34},{3,35},{4,36},{5,37},{6,38},{7,39},{8,40},{9,... | collective-permute-start | bytes 1966088 | tf_op jit(solution)/shard_map/ppermute | solution.py:139
  36.8 18.3 %collective-permute-start.8 = (bf16[320,1024]{1,0:T(8,128)(2,1)S(1)}, bf16[320,1024]{1,0:T(8,128)(2,1)S(1)}, u32[]{:S(2)}, u32[]{:S(2)}) collective-permute-start(bf16[320,1024]{1,0:T(8,128)(2,1)S(1)} %collective-permute-done.7.refs_6_), channel_id=1, source_target_pairs={{0,224},{1,225},{2,226},{3,227},{4,228},{5,229},{6,230},{7,231},{8... | collective-permute-start | bytes 1966088 | tf_op jit(solution)/shard_map/ppermute | solution.py:139
  42.2 26.9 %collective-permute-start.3 = (bf16[320,1024]{1,0:T(8,128)(2,1)S(1)}, bf16[320,1024]{1,0:T(8,128)(2,1)S(1)}, u32[]{:S(2)}, u32[]{:S(2)}) collective-permute-start(bf16[320,1024]{1,0:T(8,128)(2,1)S(1)} %collective-permute-done.1.refs_0_), channel_id=1, source_target_pairs={{0,224},{1,225},{2,226},{3,227},{4,228},{5,229},{6,230},{7,231},{8... | collective-permute-start | bytes 1966088 | tf_op jit(solution)/shard_map/ppermute | solution.py:139
  43.7 25.4 %collective-permute-start.2 = (bf16[320,1024]{1,0:T(8,128)(2,1)S(1)}, bf16[320,1024]{1,0:T(8,128)(2,1)S(1)}, u32[]{:S(2)}, u32[]{:S(2)}) collective-permute-start(bf16[320,1024]{1,0:T(8,128)(2,1)S(1)} %collective-permute-done.1.refs_0_), channel_id=1, source_target_pairs={{0,32},{1,33},{2,34},{3,35},{4,36},{5,37},{6,38},{7,39},{8,40},{9,... | collective-permute-start | bytes 1966088 | tf_op jit(solution)/shard_map/ppermute | solution.py:139
  69.1 18.4 %copy-start.1 = (s32[1,8]{1,0:T(1,128)S(1)}, s32[1,8]{1,0:T(1,128)}, u32[]{:S(2)}) copy-start(s32[1,8]{1,0:T(1,128)} %param.8) | copy-start | bytes 100
  75.2 20.1 %collective-permute-start.12 = (f32[2,4,160,640]{3,2,1,0:T(8,128)S(1)}, f32[2,4,160,640]{3,2,1,0:T(8,128)S(1)}, u32[]{:S(2)}, u32[]{:S(2)}) collective-permute-start(f32[2,4,160,640]{3,2,1,0:T(8,128)S(1)} %bitcast.84), channel_id=1, source_target_pairs={{0,1},{1,0},{2,3},{3,2},{4,5},{5,4},{6,7},{7,6},{8,9},{9,8},{10,11... | collective-permute-start | bytes 9830408 | tf_op jit(solution)/shard_map/ppermute | solution.py:139
  86.8 11.5 %collective-permute-start.13 = (f32[4,2,160,640]{3,2,1,0:T(8,128)S(1)}, f32[4,2,160,640]{3,2,1,0:T(8,128)S(1)}, u32[]{:S(2)}, u32[]{:S(2)}) collective-permute-start(f32[4,2,160,640]{3,2,1,0:T(8,128)S(1)} %bitcast.85), channel_id=1, source_target_pairs={{0,1},{1,0},{2,3},{3,2},{4,5},{5,4},{6,7},{7,6},{8,9},{9,8},{10,11... | collective-permute-start | bytes 9830408 | tf_op jit(solution)/shard_map/ppermute | solution.py:139
  87.7 6.4 %collective-permute-start = (f32[8]{0:T(128)S(1)}, f32[8]{0:T(128)S(1)}, u32[]{:S(2)}, u32[]{:S(2)}) collective-permute-start(f32[8]{0:T(128)S(1)} %convert_reduce_fusion), channel_id=1, source_target_pairs={{0,8},{1,25},{2,234},{3,251},{4,244},{5,5},{6,22},{7,39},{8,16},{9... | collective-permute-start | bytes 104 | tf_op jit(solution)/shard_map/ppermute | solution.py:139
  96.0 15.0 %collective-permute-start.22 = (bf16[2,80,640]{2,1,0:T(8,128)(2,1)S(1)}, bf16[2,80,640]{2,1,0:T(8,128)(2,1)S(1)}, u32[]{:S(2)}, u32[]{:S(2)}) collective-permute-start(bf16[2,80,640]{2,1,0:T(8,128)(2,1)S(1)} %slice_bitcast_fusion.3), channel_id=1, source_target_pairs={{0,24},{1,9},{2,26},{3,11},{4,28},{5,13},{6,30},{7,15},{8,0},{9,17... | collective-permute-start | bytes 614408 | tf_op jit(solution)/shard_map/ppermute | solution.py:139
  96.2 16.2 %collective-permute-start.21 = (bf16[4,80,640]{2,1,0:T(8,128)(2,1)S(1)}, bf16[4,80,640]{2,1,0:T(8,128)(2,1)S(1)}, u32[]{:S(2)}, u32[]{:S(2)}) collective-permute-start(bf16[4,80,640]{2,1,0:T(8,128)(2,1)S(1)} %slice_bitcast_fusion.2), channel_id=1, source_target_pairs={{0,16},{1,17},{2,18},{3,19},{4,20},{5,21},{6,22},{7,23},{8,24},{9,... | collective-permute-start | bytes 1228808 | tf_op jit(solution)/shard_map/ppermute | solution.py:139
  98.8 28.3 %collective-permute-start.16 = (bf16[2,160,640]{2,1,0:T(8,128)(2,1)S(1)}, bf16[2,160,640]{2,1,0:T(8,128)(2,1)S(1)}, u32[]{:S(2)}, u32[]{:S(2)}) collective-permute-start(bf16[2,160,640]{2,1,0:T(8,128)(2,1)S(1)} %get-tuple-element.73), channel_id=1, source_target_pairs={{0,4},{1,5},{2,6},{3,7},{4,0},{5,1},{6,2},{7,3},{8,12},{9,13},{10,... | collective-permute-start | bytes 1228808 | tf_op jit(solution)/shard_map/ppermute | solution.py:139
  100.3 28.3 %collective-permute-start.15 = (bf16[2,160,640]{2,1,0:T(8,128)(2,1)S(1)}, bf16[2,160,640]{2,1,0:T(8,128)(2,1)S(1)}, u32[]{:S(2)}, u32[]{:S(2)}) collective-permute-start(bf16[2,160,640]{2,1,0:T(8,128)(2,1)S(1)} %get-tuple-element.74), channel_id=1, source_target_pairs={{0,6},{1,7},{2,0},{3,1},{4,2},{5,3},{6,4},{7,5},{8,14},{9,15},{10,... | collective-permute-start | bytes 1228808 | tf_op jit(solution)/shard_map/ppermute | solution.py:139
  102.9 26.3 %collective-permute-start.14 = (bf16[2,160,640]{2,1,0:T(8,128)(2,1)S(1)}, bf16[2,160,640]{2,1,0:T(8,128)(2,1)S(1)}, u32[]{:S(2)}, u32[]{:S(2)}) collective-permute-start(bf16[2,160,640]{2,1,0:T(8,128)(2,1)S(1)} %get-tuple-element.75), channel_id=1, source_target_pairs={{0,2},{1,3},{2,4},{3,5},{4,6},{5,7},{6,0},{7,1},{8,10},{9,11},{10,... | collective-permute-start | bytes 1228808 | tf_op jit(solution)/shard_map/ppermute | solution.py:139
  110.9 16.2 %collective-permute-start.17 = (bf16[2,80,640]{2,1,0:T(8,128)(2,1)S(1)}, bf16[2,80,640]{2,1,0:T(8,128)(2,1)S(1)}, u32[]{:S(2)}, u32[]{:S(2)}) collective-permute-start(bf16[2,80,640]{2,1,0:T(8,128)(2,1)S(1)} %get-tuple-element.80), channel_id=1, source_target_pairs={{0,2},{1,3},{2,4},{3,5},{4,6},{5,7},{6,0},{7,1},{8,10},{9,11},{10,... | collective-permute-start | bytes 614408 | tf_op jit(solution)/shard_map/ppermute | solution.py:139
  112.4 18.9 %collective-permute-start.19 = (bf16[2,80,640]{2,1,0:T(8,128)(2,1)S(1)}, bf16[2,80,640]{2,1,0:T(8,128)(2,1)S(1)}, u32[]{:S(2)}, u32[]{:S(2)}) collective-permute-start(bf16[2,80,640]{2,1,0:T(8,128)(2,1)S(1)} %get-tuple-element.81), channel_id=1, source_target_pairs={{0,4},{1,5},{2,6},{3,7},{4,0},{5,1},{6,2},{7,3},{8,12},{9,13},{10,... | collective-permute-start | bytes 614408 | tf_op jit(solution)/shard_map/ppermute | solution.py:139
  127.1 6.1 %collective-permute-start.18 = (bf16[2,80,640]{2,1,0:T(8,128)(2,1)S(1)}, bf16[2,80,640]{2,1,0:T(8,128)(2,1)S(1)}, u32[]{:S(2)}, u32[]{:S(2)}) collective-permute-start(bf16[2,80,640]{2,1,0:T(8,128)(2,1)S(1)} %get-tuple-element.82), channel_id=1, source_target_pairs={{0,6},{1,7},{2,0},{3,1},{4,2},{5,3},{6,4},{7,5},{8,14},{9,15},{10,... | collective-permute-start | bytes 614408 | tf_op jit(solution)/shard_map/ppermute | solution.py:139
  127.1 12.5 %collective-permute-start.23 = (bf16[80,640]{1,0:T(8,128)(2,1)S(1)}, bf16[80,640]{1,0:T(8,128)(2,1)S(1)}, u32[]{:S(2)}, u32[]{:S(2)}) collective-permute-start(bf16[80,640]{1,0:T(8,128)(2,1)S(1)} %get-tuple-element.83), channel_id=1, source_target_pairs={{0,2},{1,3},{2,4},{3,5},{4,6},{5,7},{6,0},{7,1},{8,10},{9,11},{10,... | collective-permute-start | bytes 307208 | tf_op jit(solution)/shard_map/ppermute | solution.py:139
  128.6 11.1 %collective-permute-start.25 = (bf16[80,640]{1,0:T(8,128)(2,1)S(1)}, bf16[80,640]{1,0:T(8,128)(2,1)S(1)}, u32[]{:S(2)}, u32[]{:S(2)}) collective-permute-start(bf16[80,640]{1,0:T(8,128)(2,1)S(1)} %get-tuple-element.84), channel_id=1, source_target_pairs={{0,4},{1,5},{2,6},{3,7},{4,0},{5,1},{6,2},{7,3},{8,12},{9,13},{10,... | collective-permute-start | bytes 307208 | tf_op jit(solution)/shard_map/ppermute | solution.py:139
  129.2 10.4 %collective-permute-start.24 = (bf16[80,640]{1,0:T(8,128)(2,1)S(1)}, bf16[80,640]{1,0:T(8,128)(2,1)S(1)}, u32[]{:S(2)}, u32[]{:S(2)}) collective-permute-start(bf16[80,640]{1,0:T(8,128)(2,1)S(1)} %get-tuple-element.85), channel_id=1, source_target_pairs={{0,6},{1,7},{2,0},{3,1},{4,2},{5,3},{6,4},{7,5},{8,14},{9,15},{10,... | collective-permute-start | bytes 307208 | tf_op jit(solution)/shard_map/ppermute | solution.py:139
  131.3 8.4 %collective-permute-start.26 = (bf16[160,640]{1,0:T(8,128)(2,1)S(1)}, bf16[160,640]{1,0:T(8,128)(2,1)S(1)}, u32[]{:S(2)}, u32[]{:S(2)}) collective-permute-start(bf16[160,640]{1,0:T(8,128)(2,1)S(1)} %fusion.14), channel_id=1, source_target_pairs={{0,8},{1,25},{2,10},{3,27},{4,12},{5,13},{6,14},{7,15},{8,16},{9,1... | collective-permute-start | bytes 614408 | tf_op jit(solution)/shard_map/ppermute | solution.py:139
  133.4 6.2 %collective-permute-start.20 = (bf16[80,640]{1,0:T(8,128)(2,1)S(1)}, bf16[80,640]{1,0:T(8,128)(2,1)S(1)}, u32[]{:S(2)}, u32[]{:S(2)}) collective-permute-start(bf16[80,640]{1,0:T(8,128)(2,1)S(1)} %get-tuple-element.87), channel_id=1, source_target_pairs={{0,16},{1,17},{2,18},{3,19},{4,20},{5,21},{6,22},{7,23},{8,24},{9,... | collective-permute-start | bytes 307208 | tf_op jit(solution)/shard_map/ppermute | solution.py:139
  139.6 5.8 %collective-permute-start.27 = (bf16[160,640]{1,0:T(8,128)(2,1)S(1)}, bf16[160,640]{1,0:T(8,128)(2,1)S(1)}, u32[]{:S(2)}, u32[]{:S(2)}) collective-permute-start(bf16[160,640]{1,0:T(8,128)(2,1)S(1)} %select_convert_fusion), channel_id=1, source_target_pairs={{0,24},{1,9},{2,26},{3,11},{4,28},{5,29},{6,30},{7,31},{8,0},{9,17... | collective-permute-start | bytes 614408 | tf_op jit(solution)/shard_map/ppermute | solution.py:139
  145.6 10.3 %collective-permute-start.28 = (bf16[160,640]{1,0:T(8,128)(2,1)S(1)}, bf16[160,640]{1,0:T(8,128)(2,1)S(1)}, u32[]{:S(2)}, u32[]{:S(2)}) collective-permute-start(bf16[160,640]{1,0:T(8,128)(2,1)S(1)} %fusion.8), channel_id=1, source_target_pairs={{0,254},{1,239},{2,28},{3,13},{4,35},{5,34},{6,33},{7,32},{8,6},{9... | collective-permute-start | bytes 614408 | tf_op jit(solution)/shard_map/ppermute | solution.py:139
  147.7 12.2 %collective-permute-start.29 = (bf16[160,640]{1,0:T(8,128)(2,1)S(1)}, bf16[160,640]{1,0:T(8,128)(2,1)S(1)}, u32[]{:S(2)}, u32[]{:S(2)}) collective-permute-start(bf16[160,640]{1,0:T(8,128)(2,1)S(1)} %fusion.8), channel_id=1, source_target_pairs={{0,33},{1,32},{2,35},{3,34},{4,20},{5,5},{6,246},{7,231},{8,41},{9... | collective-permute-start | bytes 614408 | tf_op jit(solution)/shard_map/ppermute | solution.py:139

commit v6 on v5

--- a/solution.py
+++ b/solution.py
@@ -62,7 +62,7 @@
 
     def place(far, core, slot, p, tile):
         spot = owner(far, p)
-        index = spot * 2 + slot if stage in ("prep", "early") else slot * 4 + spot
+        index = slot * 4 + spot
 
         @pl.when(c == core)
         def _():
@@ -146,7 +146,7 @@
         rows = grads.shape[1]
         reach = partners.shape[1]
         quarter = width // NY
-        part = rows // 4
+        part = rows * 3 // 10
         own = grads[0]
         e = lax.axis_index("ex")
         k = lax.axis_index("ckpt")
@@ -201,11 +201,14 @@
         carried = tiles("prep", place, factor, pieces, ())
         left, keep, give = tiles("early", place, factor, pieces, carried)
         carried = tiles("mid", place, factor, pieces, (left,))
-        keep, give = (value.reshape(4, 2, rows // 2, 2 * rows) for value in (keep, give))
+        keep, give = (value.reshape(2, 4, rows // 2, 2 * rows) for value in (keep, give))
 
         def low_of(x):
             return x < 2
 
+        def pick_both(array, i):
+            return jnp.stack([pick(array[0], i, 0), pick(array[1], i, 0)])
+
         def narrow(value):
             return value.astype(jnp.bfloat16)
 
@@ -213,8 +216,7 @@
             return value.astype(jnp.float32)
 
         total = keep + send(give, lambda e, x, c: (e, x, 1 - c))
-        early = pick(total, 0, 0)
-        arrived_early = [send(narrow(pick(total, t, 0)), lambda e, x, c, t=t: (e, x + t, c)) for t in (1, 3, 2)]
+        early = total
         left, keep, give = tiles("late", place, factor, pieces, carried)
         keep, give = (value.reshape(2, 4, rows // 2, 2 * rows) for value in (keep, give))
         total = keep + send(give, lambda e, x, c: (e, x, 1 - c))
@@ -222,29 +224,39 @@
         def rest(e, c):
             return ring(e, 3 if c == 0 else 1)
 
+        upper, lower = early[:, :, :part], early[:, :, part:]
+        early_upper = pick_both(upper, 0)
+        arrived_early = [send(narrow(pick_both(upper, t)), lambda e, x, c, t=t: (e, x + t, c)) for t in (1, 3, 2)]
+        ea = send(narrow(lower[1, :2]), lambda e, x, c: (ring(e, 1 if c == 0 else 3), x, c))
+        eb = send(narrow(lower[1, 2:]), lambda e, x, c: (ring(e, 1), x, c))
+        ec = send(narrow(lower[0, 2:]), lambda e, x, c: (ring(e, 3), x, c))
+        early_home = lower[0, :2]
+
         upper, lower = total[:, :, :part], total[:, :, part:]
         by2 = send(narrow(lower[0]), lambda e, x, c: (ring(e, 2), x, c))
         by1 = send(narrow(lower[1, :2]), lambda e, x, c: (rest(e, c), x, c))
-        upper_own = pick(upper, 0, 1)
-        arrived = [send(narrow(pick(upper, t, 1)), lambda e, x, c, t=t: (e, x + t, c)) for t in (1, 3, 2)]
+        upper_own = pick_both(upper, 0)
+        arrived = [send(narrow(pick_both(upper, t)), lambda e, x, c, t=t: (e, x + t, c)) for t in (1, 3, 2)]
+        ea, eb, ec, by2 = lax.optimization_barrier((ea, eb, ec, by2))
         lower_own = wide(by2) + jnp.concatenate([wide(by1), lower[1, 2:]], axis=0)
+        lower_own = lower_own + jnp.concatenate([early_home + wide(ea), wide(eb) + wide(ec)], axis=0)
         bottom = pick(lower_own, 0, 0)
         bottom_arrived = [send(narrow(pick(lower_own, t, 0)), lambda e, x, c, t=t: (e, x + t, c)) for t in (1, 3, 2)]
         arrived_early, arrived[0] = lax.optimization_barrier((arrived_early, arrived[0]))
         for value in arrived_early:
-            early = early + wide(value)
+            early_upper = early_upper + wide(value)
+        ey1 = send(narrow(early_upper[1]), lambda e, x, c: (ring(e, 3 if low_of(x) and c == 1 else 1), x, c))
         for value in arrived:
             upper_own = upper_own + wide(value)
         ay2 = send(narrow(upper_own[0]), lambda e, x, c: (ring(e, 2), x, c))
-        ey1 = send(narrow(early[1]), lambda e, x, c: (ring(e, 3 if low_of(x) and c == 1 else 1), x, c))
-        padded = jnp.concatenate([upper_own[1], jnp.zeros_like(upper_own[1])], axis=0)
         mixed = send(
-            narrow(jnp.where(low, padded, early[0])), lambda e, x, c: (rest(e, c) if low_of(x) else ring(e, 3), x, c)
+            narrow(jnp.where(low, upper_own[1], early_upper[0])),
+            lambda e, x, c: (rest(e, c) if low_of(x) else ring(e, 3), x, c),
         )
         for value in bottom_arrived:
             bottom = bottom + wide(value)
-        top = wide(ay2) + jnp.where(low, 0.0, upper_own[1])
-        final = jnp.concatenate([top, bottom], axis=0) + wide(ey1) + wide(mixed) + jnp.where(low, early[0], 0.0)
+        top = jnp.where(low, early_upper[0], upper_own[1]) + wide(ey1) + wide(ay2) + wide(mixed)
+        final = jnp.concatenate([top, bottom], axis=0)
         final = narrow(jnp.where(weight > 0, final, 0.0))
 
         def deliver(first):

time: 162 us -> 159 us (0.981)
  waiting for transfers between devices: 63.4 us -> 58.2 us
    ppermute x30 -> x33, waiting for transfers between devices: 63.4 us -> 58.2 us  [send(): return lax.ppermute(value, AXES, pairs)]
    ppermute x30 -> x33, starting transfers between devices: 65.6 us -> 66 us  [send(): return lax.ppermute(value, AXES, pairs)]
  transfers between devices with their start and end apart: 30 -> 33, of which waited for: 12 -> 17; matrix products, arithmetic and copies ran while one was open for 3% -> 2% of each run, Pallas kernels for 10% -> 10%
where the time goes in v6:
time: 159 us; the launch traced here: 157 us
  starting transfers between devices  66 us (42%)
  waiting for transfers between devices  58.2 us (37%)
  Pallas kernels  22.2 us (14%)
  local copies, waits for them, and re-layouts  4.6 us (3%)
  other arithmetic  3.87 us (2%)
  between operations  2.32 us (1%)
    ppermute x33, starting transfers between devices, send(): return lax.ppermute(value, AXES, pairs)  66 us
    ppermute x33, waiting for transfers between devices, send(): return lax.ppermute(value, AXES, pairs)  58.2 us
    pallas_call x4, Pallas kernels, tiles(): pl.pallas_call(functools.partial(tiles_kernel, stage), in_specs=[pl.Block...  22.2 us
  transfers between devices with their start and end apart: 33, of which 17 were waited for; matrix products, arithmetic and copies ran while one was open for 2% of the time, Pallas kernels for 10%

profile of v6, /device:TPU:1, one launch (start us, length us, event | category | flops | bytes accessed | tf_op | source)
XLA Modules:
  0.0 157.2 jit_solution(7326833946561998493)
XLA Ops:
  0.0 2.1 %constant_dynamic-slice_fusion.2 = (bf16[320,1024]{1,0:T(8,128)(2,1)S(1)}, bf16[320,1024]{1,0:T(8,128)(2,1)S(1)}) fusion(bf16[320,4096]{1,0:T(8,128)(2,1)} %bitcast.94, s32[]{:T(128)S(6)} %mul.24, s32[]{:T(128)S(6)} %mul.22), kind=kLoop, calls=%fused_computation.77 | loop fusion | bytes 2621448 | tf_op jit(solution)/shard_map/dynamic_slice | solution.py:167
  2.1 2.2 %collective-permute-start.5 = (bf16[320,1024]{1,0:T(8,128)(2,1)S(1)}, bf16[320,1024]{1,0:T(8,128)(2,1)S(1)}, u32[]{:S(2)}, u32[]{:S(2)}) collective-permute-start(bf16[320,1024]{1,0:T(8,128)(2,1)S(1)} %get-tuple-element.54), channel_id=1, source_target_pairs={{0,8},{1,9},{2,10},{3,11},{4,12},{5,13},{6,14},{7,15},{8,16},{9,17... | collective-permute-start | bytes 1966088 | tf_op jit(solution)/shard_map/ppermute | solution.py:139
  8.2 1.6 %collective-permute-start.7 = (bf16[320,1024]{1,0:T(8,128)(2,1)S(1)}, bf16[320,1024]{1,0:T(8,128)(2,1)S(1)}, u32[]{:S(2)}, u32[]{:S(2)}) collective-permute-start(bf16[320,1024]{1,0:T(8,128)(2,1)S(1)} %get-tuple-element.87.refs_2_), channel_id=1, source_target_pairs={{0,32},{1,33},{2,34},{3,35},{4,36},{5,37},{6,38},{7,39},{8,40},{9,... | collective-permute-start | bytes 1966088 | tf_op jit(solution)/shard_map/ppermute | solution.py:139
  9.8 3.9 %collective-permute-start.4 = (bf16[320,1024]{1,0:T(8,128)(2,1)S(1)}, bf16[320,1024]{1,0:T(8,128)(2,1)S(1)}, u32[]{:S(2)}, u32[]{:S(2)}) collective-permute-start(bf16[320,1024]{1,0:T(8,128)(2,1)S(1)} %get-tuple-element.87.refs_2_), channel_id=1, source_target_pairs={{0,224},{1,225},{2,226},{3,227},{4,228},{5,229},{6,230},{7,231},{8... | collective-permute-start | bytes 1966088 | tf_op jit(solution)/shard_map/ppermute | solution.py:139
  13.7 4.5 %collective-permute-done.5.refs_3_ = bf16[320,1024]{1,0:T(8,128)(2,1)S(1)} collective-permute-done((bf16[320,1024]{1,0:T(8,128)(2,1)S(1)}, bf16[320,1024]{1,0:T(8,128)(2,1)S(1)}, u32[]{:S(2)}, u32[]{:S(2)}) %collective-permute-start.5) | collective-permute-done | bytes 655392 | tf_op jit(solution)/shard_map/ppermute | solution.py:139
  18.3 3.3 %collective-permute-start.8 = (bf16[320,1024]{1,0:T(8,128)(2,1)S(1)}, bf16[320,1024]{1,0:T(8,128)(2,1)S(1)}, u32[]{:S(2)}, u32[]{:S(2)}) collective-permute-start(bf16[320,1024]{1,0:T(8,128)(2,1)S(1)} %collective-permute-done.5.refs_3_), channel_id=1, source_target_pairs={{0,32},{1,33},{2,34},{3,35},{4,36},{5,37},{6,38},{7,39},{8,40},{9,... | collective-permute-start | bytes 1966088 | tf_op jit(solution)/shard_map/ppermute | solution.py:139
  21.6 3.9 %collective-permute-start.6 = (bf16[320,1024]{1,0:T(8,128)(2,1)S(1)}, bf16[320,1024]{1,0:T(8,128)(2,1)S(1)}, u32[]{:S(2)}, u32[]{:S(2)}) collective-permute-start(bf16[320,1024]{1,0:T(8,128)(2,1)S(1)} %collective-permute-done.5.refs_3_), channel_id=1, source_target_pairs={{0,224},{1,225},{2,226},{3,227},{4,228},{5,229},{6,230},{7,231},{8... | collective-permute-start | bytes 1966088 | tf_op jit(solution)/shard_map/ppermute | solution.py:139
  25.6 9.5 %collective-permute-done.13.refs_0_ = bf16[320,1024]{1,0:T(8,128)(2,1)S(1)} collective-permute-done((bf16[320,1024]{1,0:T(8,128)(2,1)S(1)}, bf16[320,1024]{1,0:T(8,128)(2,1)S(1)}, u32[]{:S(2)}, u32[]{:S(2)}) %collective-permute-start.13) | collective-permute-done | bytes 655392 | tf_op jit(solution)/shard_map/ppermute | solution.py:139
  35.1 5.6 %collective-permute-start.3 = (bf16[320,1024]{1,0:T(8,128)(2,1)S(1)}, bf16[320,1024]{1,0:T(8,128)(2,1)S(1)}, u32[]{:S(2)}, u32[]{:S(2)}) collective-permute-start(bf16[320,1024]{1,0:T(8,128)(2,1)S(1)} %collective-permute-done.1.refs_6_), channel_id=1, source_target_pairs={{0,224},{1,225},{2,226},{3,227},{4,228},{5,229},{6,230},{7,231},{8... | collective-permute-start | bytes 1966088 | tf_op jit(solution)/shard_map/ppermute | solution.py:139
  42.2 2.7 %collective-permute-start.15 = (bf16[320,1024]{1,0:T(8,128)(2,1)S(1)}, bf16[320,1024]{1,0:T(8,128)(2,1)S(1)}, u32[]{:S(2)}, u32[]{:S(2)}) collective-permute-start(bf16[320,1024]{1,0:T(8,128)(2,1)S(1)} %collective-permute-done.13.refs_0_), channel_id=1, source_target_pairs={{0,224},{1,225},{2,226},{3,227},{4,228},{5,229},{6,230},{7,231},{8... | collective-permute-start | bytes 1966088 | tf_op jit(solution)/shard_map/ppermute | solution.py:139
  45.0 5.3 %shard_map.55 = (bf16[3840,1024]{1,0:T(8,128)(2,1)S(1)}, f32[8,160,640]{2,1,0:T(8,128)S(1)}, f32[8,160,640]{2,1,0:T(8,128)S(1)}) custom-call(s32[2]{0:T(128)S(1)} %pad_add_fusion.place_ref, f32[1,1024]{1,0:T(1,128)S(1)} %divide_multiply_fusion.factor_ref, bf16[320,1024]{1,0:T(8,128)(2,1)S(1)} %collective-permute-done.7.refs_0_, ...), custom_call_target="tpu_custom_call" | custom-call | flops 2097152000 | bytes 7864320 | tf_op jit(solution)/shard_map/pallas_call | solution.py:111
  50.3 4.7 %collective-permute-done.3.refs_1_.refs_4_.refs_3_ = bf16[320,1024]{1,0:T(8,128)(2,1)S(1)} collective-permute-done((bf16[320,1024]{1,0:T(8,128)(2,1)S(1)}, bf16[320,1024]{1,0:T(8,128)(2,1)S(1)}, u32[]{:S(2)}, u32[]{:S(2)}) %collective-permute-start.3) | collective-permute-done | bytes 655392 | tf_op jit(solution)/shard_map/ppermute | solution.py:139
  56.4 6.8 %shard_map.56 = (bf16[3840,1024]{1,0:T(8,128)(2,1)S(1)}, f32[8,160,640]{2,1,0:T(8,128)S(1)}, f32[8,160,640]{2,1,0:T(8,128)S(1)}) custom-call(s32[2]{0:T(128)S(1)} %pad_add_fusion.place_ref, f32[1,1024]{1,0:T(1,128)S(1)} %divide_multiply_fusion.factor_ref, ...), custom_call_target="tpu_custom_call", output_to_operand_aliasing={{0}: (7, {}), {1}: (8, {}), {2}: (9, {})} | custom-call | flops 2097152000 | bytes 7864320 | tf_op jit(solution)/shard_map/pallas_call | solution.py:111
  63.2 4.0 %shard_map.57 = (bf16[3840,1024]{1,0:T(8,128)(2,1)S(1)}, f32[8,160,640]{2,1,0:T(8,128)S(1)}, f32[8,160,640]{2,1,0:T(8,128)S(1)}) custom-call(s32[2]{0:T(128)S(1)} %pad_add_fusion.place_ref, f32[1,1024]{1,0:T(1,128)S(1)} %divide_multiply_fusion.factor_ref, bf16[320,1024]{1,0:T(8,128)(2,1)S(1)} %collective-permute-done.13.refs_0_, ...), custom_call_target="tpu_custom_call", output_to_operand_aliasing={{0}: (6, {})} | custom-call | flops 2097152000 | bytes 7864320 | tf_op jit(solution)/shard_map/pallas_call | solution.py:111
  67.1 1.9 %collective-permute-done.15.refs_1_.refs_5_ = bf16[320,1024]{1,0:T(8,128)(2,1)S(1)} collective-permute-done((bf16[320,1024]{1,0:T(8,128)(2,1)S(1)}, bf16[320,1024]{1,0:T(8,128)(2,1)S(1)}, u32[]{:S(2)}, u32[]{:S(2)}) %collective-permute-start.15) | collective-permute-done | bytes 655392 | tf_op jit(solution)/shard_map/ppermute | solution.py:139
  70.4 6.1 %shard_map.58 = (bf16[3840,1024]{1,0:T(8,128)(2,1)S(1)}, f32[8,160,640]{2,1,0:T(8,128)S(1)}, f32[8,160,640]{2,1,0:T(8,128)S(1)}) custom-call(s32[2]{0:T(128)S(1)} %pad_add_fusion.place_ref, f32[1,1024]{1,0:T(1,128)S(1)} %divide_multiply_fusion.factor_ref, ...), custom_call_target="tpu_custom_call", output_to_operand_aliasing={{0}: (8, {}), {1}: (9, {}), {2}: (10, {})} | custom-call | flops 2097152000 | bytes 7864320 | tf_op jit(solution)/shard_map/pallas_call | solution.py:111
  76.5 10.2 %collective-permute-start.16 = (f32[2,4,160,640]{3,2,1,0:T(8,128)S(1)}, f32[2,4,160,640]{3,2,1,0:T(8,128)S(1)}, u32[]{:S(2)}, u32[]{:S(2)}) collective-permute-start(f32[2,4,160,640]{3,2,1,0:T(8,128)S(1)} %bitcast.92), channel_id=1, source_target_pairs={{0,1},{1,0},{2,3},{3,2},{4,5},{5,4},{6,7},{7,6},{8,9},{9,8},{10,11... | collective-permute-start | bytes 9830408 | tf_op jit(solution)/shard_map/ppermute | solution.py:139
  87.7 2.9 %collective-permute-start = (f32[8]{0:T(128)S(1)}, f32[8]{0:T(128)S(1)}, u32[]{:S(2)}, u32[]{:S(2)}) collective-permute-start(f32[8]{0:T(128)S(1)} %convert_reduce_fusion), channel_id=1, source_target_pairs={{0,8},{1,25},{2,234},{3,251},{4,244},{5,5},{6,22},{7,39},{8,16},{9... | collective-permute-start | bytes 104 | tf_op jit(solution)/shard_map/ppermute | solution.py:139
  90.6 3.5 %collective-permute-done = f32[8]{0:T(128)S(1)} collective-permute-done((f32[8]{0:T(128)S(1)}, f32[8]{0:T(128)S(1)}, u32[]{:S(2)}, u32[]{:S(2)}) %collective-permute-start) | collective-permute-done | bytes 64 | tf_op jit(solution)/shard_map/ppermute | solution.py:139
  100.9 1.6 %collective-permute-start.12 = (bf16[2,96,640]{2,1,0:T(8,128)(2,1)S(1)}, bf16[2,96,640]{2,1,0:T(8,128)(2,1)S(1)}, u32[]{:S(2)}, u32[]{:S(2)}) collective-permute-start(bf16[2,96,640]{2,1,0:T(8,128)(2,1)S(1)} %pad_maximum_fusion.3), channel_id=1, source_target_pairs={{0,4},{1,5},{2,6},{3,7},{4,0},{5,1},{6,2},{7,3},{8,12},{9,13},{10,... | collective-permute-start | bytes 737288 | tf_op jit(solution)/shard_map/ppermute | solution.py:139
  103.2 5.0 %collective-permute-done.27 = bf16[2,64,640]{2,1,0:T(8,128)(2,1)S(1)} collective-permute-done((bf16[2,64,640]{2,1,0:T(8,128)(2,1)S(1)}, bf16[2,64,640]{2,1,0:T(8,128)(2,1)S(1)}, u32[]{:S(2)}, u32[]{:S(2)}) %collective-permute-start.27) | collective-permute-done | bytes 163872 | tf_op jit(solution)/shard_map/ppermute | solution.py:139
  111.0 2.2 %collective-permute-start.19 = (bf16[2,96,640]{2,1,0:T(8,128)(2,1)S(1)}, bf16[2,96,640]{2,1,0:T(8,128)(2,1)S(1)}, u32[]{:S(2)}, u32[]{:S(2)}) collective-permute-start(bf16[2,96,640]{2,1,0:T(8,128)(2,1)S(1)} %pad_maximum_fusion.6), channel_id=1, source_target_pairs={{0,4},{1,5},{2,6},{3,7},{4,0},{5,1},{6,2},{7,3},{8,12},{9,13},{10,... | collective-permute-start | bytes 737288 | tf_op jit(solution)/shard_map/ppermute | solution.py:139
  113.2 3.9 %collective-permute-done.17 = bf16[2,96,640]{2,1,0:T(8,128)(2,1)S(1)} collective-permute-done((bf16[2,96,640]{2,1,0:T(8,128)(2,1)S(1)}, bf16[2,96,640]{2,1,0:T(8,128)(2,1)S(1)}, u32[]{:S(2)}, u32[]{:S(2)}) %collective-permute-start.17) | collective-permute-done | bytes 245792 | tf_op jit(solution)/shard_map/ppermute | solution.py:139
  117.3 4.1 %collective-permute-done.19 = bf16[2,96,640]{2,1,0:T(8,128)(2,1)S(1)} collective-permute-done((bf16[2,96,640]{2,1,0:T(8,128)(2,1)S(1)}, bf16[2,96,640]{2,1,0:T(8,128)(2,1)S(1)}, u32[]{:S(2)}, u32[]{:S(2)}) %collective-permute-start.19) | collective-permute-done | bytes 245792 | tf_op jit(solution)/shard_map/ppermute | solution.py:139
  121.6 2.8 %collective-permute-done.18 = bf16[2,96,640]{2,1,0:T(8,128)(2,1)S(1)} collective-permute-done((bf16[2,96,640]{2,1,0:T(8,128)(2,1)S(1)}, bf16[2,96,640]{2,1,0:T(8,128)(2,1)S(1)}, u32[]{:S(2)}, u32[]{:S(2)}) %collective-permute-start.18) | collective-permute-done | bytes 245792 | tf_op jit(solution)/shard_map/ppermute | solution.py:139
  124.5 3.0 %collective-permute-start.20 = (bf16[96,640]{1,0:T(8,128)(2,1)S(1)}, bf16[96,640]{1,0:T(8,128)(2,1)S(1)}, u32[]{:S(2)}, u32[]{:S(2)}) collective-permute-start(bf16[96,640]{1,0:T(8,128)(2,1)S(1)} %get-tuple-element.109), channel_id=1, source_target_pairs={{0,8},{1,25},{2,10},{3,27},{4,12},{5,13},{6,14},{7,15},{8,16},{9,1... | collective-permute-start | bytes 368648 | tf_op jit(solution)/shard_map/ppermute | solution.py:139
  130.4 3.2 %collective-permute-start.30 = (bf16[64,640]{1,0:T(8,128)(2,1)S(1)}, bf16[64,640]{1,0:T(8,128)(2,1)S(1)}, u32[]{:S(2)}, u32[]{:S(2)}) collective-permute-start(bf16[64,640]{1,0:T(8,128)(2,1)S(1)} %get-tuple-element.107), channel_id=1, source_target_pairs={{0,4},{1,5},{2,6},{3,7},{4,0},{5,1},{6,2},{7,3},{8,12},{9,13},{10,... | collective-permute-start | bytes 245768 | tf_op jit(solution)/shard_map/ppermute | solution.py:139
  133.6 1.8 %collective-permute-done.20 = bf16[96,640]{1,0:T(8,128)(2,1)S(1)} collective-permute-done((bf16[96,640]{1,0:T(8,128)(2,1)S(1)}, bf16[96,640]{1,0:T(8,128)(2,1)S(1)}, u32[]{:S(2)}, u32[]{:S(2)}) %collective-permute-start.20) | collective-permute-done | bytes 122912 | tf_op jit(solution)/shard_map/ppermute | solution.py:139
  136.1 2.5 %collective-permute-done.22 = bf16[96,640]{1,0:T(8,128)(2,1)S(1)} collective-permute-done((bf16[96,640]{1,0:T(8,128)(2,1)S(1)}, bf16[96,640]{1,0:T(8,128)(2,1)S(1)}, u32[]{:S(2)}, u32[]{:S(2)}) %collective-permute-start.22) | collective-permute-done | bytes 122912 | tf_op jit(solution)/shard_map/ppermute | solution.py:139
  138.8 5.8 %collective-permute-start.32 = (bf16[160,640]{1,0:T(8,128)(2,1)S(1)}, bf16[160,640]{1,0:T(8,128)(2,1)S(1)}, u32[]{:S(2)}, u32[]{:S(2)}) collective-permute-start(bf16[160,640]{1,0:T(8,128)(2,1)S(1)} %fusion.5), channel_id=1, source_target_pairs={{0,33},{1,32},{2,35},{3,34},{4,20},{5,5},{6,246},{7,231},{8,41},{9... | collective-permute-start | bytes 614408 | tf_op jit(solution)/shard_map/ppermute | solution.py:139
  145.7 8.0 %collective-permute-done.32 = bf16[160,640]{1,0:T(8,128)(2,1)S(1)} collective-permute-done((bf16[160,640]{1,0:T(8,128)(2,1)S(1)}, bf16[160,640]{1,0:T(8,128)(2,1)S(1)}, u32[]{:S(2)}, u32[]{:S(2)}) %collective-permute-start.32) | collective-permute-done | bytes 204832 | tf_op jit(solution)/shard_map/ppermute | solution.py:139
  153.8 1.8 %collective-permute-done.31 = bf16[160,640]{1,0:T(8,128)(2,1)S(1)} collective-permute-done((bf16[160,640]{1,0:T(8,128)(2,1)S(1)}, bf16[160,640]{1,0:T(8,128)(2,1)S(1)}, u32[]{:S(2)}, u32[]{:S(2)}) %collective-permute-start.31) | collective-permute-done | bytes 204832 | tf_op jit(solution)/shard_map/ppermute | solution.py:139
  (86 shorter events, 24.1 us)
Async XLA Ops:
  2.1 16.2 %collective-permute-start.5 = (bf16[320,1024]{1,0:T(8,128)(2,1)S(1)}, bf16[320,1024]{1,0:T(8,128)(2,1)S(1)}, u32[]{:S(2)}, u32[]{:S(2)}) collective-permute-start(bf16[320,1024]{1,0:T(8,128)(2,1)S(1)} %get-tuple-element.54), channel_id=1, source_target_pairs={{0,8},{1,9},{2,10},{3,11},{4,12},{5,13},{6,14},{7,15},{8,16},{9,17... | collective-permute-start | bytes 1966088 | tf_op jit(solution)/shard_map/ppermute | solution.py:139
  4.3 17.3 %collective-permute-start.1 = (bf16[320,1024]{1,0:T(8,128)(2,1)S(1)}, bf16[320,1024]{1,0:T(8,128)(2,1)S(1)}, u32[]{:S(2)}, u32[]{:S(2)}) collective-permute-start(bf16[320,1024]{1,0:T(8,128)(2,1)S(1)} %get-tuple-element.52), channel_id=1, source_target_pairs={{0,24},{1,25},{2,26},{3,27},{4,28},{5,29},{6,30},{7,31},{8,0},{9,1... | collective-permute-start | bytes 1966088 | tf_op jit(solution)/shard_map/ppermute | solution.py:139
  6.6 28.6 %collective-permute-start.13 = (bf16[320,1024]{1,0:T(8,128)(2,1)S(1)}, bf16[320,1024]{1,0:T(8,128)(2,1)S(1)}, u32[]{:S(2)}, u32[]{:S(2)}) collective-permute-start(bf16[320,1024]{1,0:T(8,128)(2,1)S(1)} %get-tuple-element.88), channel_id=1, source_target_pairs={{0,16},{1,17},{2,18},{3,19},{4,20},{5,21},{6,22},{7,23},{8,24},{9,... | collective-permute-start | bytes 1966088 | tf_op jit(solution)/shard_map/ppermute | solution.py:139
  8.2 32.5 %collective-permute-start.7 = (bf16[320,1024]{1,0:T(8,128)(2,1)S(1)}, bf16[320,1024]{1,0:T(8,128)(2,1)S(1)}, u32[]{:S(2)}, u32[]{:S(2)}) collective-permute-start(bf16[320,1024]{1,0:T(8,128)(2,1)S(1)} %get-tuple-element.87.refs_2_), channel_id=1, source_target_pairs={{0,32},{1,33},{2,34},{3,35},{4,36},{5,37},{6,38},{7,39},{8,40},{9,... | collective-permute-start | bytes 1966088 | tf_op jit(solution)/shard_map/ppermute | solution.py:139
  9.8 32.3 %collective-permute-start.4 = (bf16[320,1024]{1,0:T(8,128)(2,1)S(1)}, bf16[320,1024]{1,0:T(8,128)(2,1)S(1)}, u32[]{:S(2)}, u32[]{:S(2)}) collective-permute-start(bf16[320,1024]{1,0:T(8,128)(2,1)S(1)} %get-tuple-element.87.refs_2_), channel_id=1, source_target_pairs={{0,224},{1,225},{2,226},{3,227},{4,228},{5,229},{6,230},{7,231},{8... | collective-permute-start | bytes 1966088 | tf_op jit(solution)/shard_map/ppermute | solution.py:139
  18.3 26.6 %collective-permute-start.8 = (bf16[320,1024]{1,0:T(8,128)(2,1)S(1)}, bf16[320,1024]{1,0:T(8,128)(2,1)S(1)}, u32[]{:S(2)}, u32[]{:S(2)}) collective-permute-start(bf16[320,1024]{1,0:T(8,128)(2,1)S(1)} %collective-permute-done.5.refs_3_), channel_id=1, source_target_pairs={{0,32},{1,33},{2,34},{3,35},{4,36},{5,37},{6,38},{7,39},{8,40},{9,... | collective-permute-start | bytes 1966088 | tf_op jit(solution)/shard_map/ppermute | solution.py:139
  21.6 23.4 %collective-permute-start.6 = (bf16[320,1024]{1,0:T(8,128)(2,1)S(1)}, bf16[320,1024]{1,0:T(8,128)(2,1)S(1)}, u32[]{:S(2)}, u32[]{:S(2)}) collective-permute-start(bf16[320,1024]{1,0:T(8,128)(2,1)S(1)} %collective-permute-done.5.refs_3_), channel_id=1, source_target_pairs={{0,224},{1,225},{2,226},{3,227},{4,228},{5,229},{6,230},{7,231},{8... | collective-permute-start | bytes 1966088 | tf_op jit(solution)/shard_map/ppermute | solution.py:139
  35.1 19.9 %collective-permute-start.3 = (bf16[320,1024]{1,0:T(8,128)(2,1)S(1)}, bf16[320,1024]{1,0:T(8,128)(2,1)S(1)}, u32[]{:S(2)}, u32[]{:S(2)}) collective-permute-start(bf16[320,1024]{1,0:T(8,128)(2,1)S(1)} %collective-permute-done.1.refs_6_), channel_id=1, source_target_pairs={{0,224},{1,225},{2,226},{3,227},{4,228},{5,229},{6,230},{7,231},{8... | collective-permute-start | bytes 1966088 | tf_op jit(solution)/shard_map/ppermute | solution.py:139
  40.7 15.7 %collective-permute-start.2 = (bf16[320,1024]{1,0:T(8,128)(2,1)S(1)}, bf16[320,1024]{1,0:T(8,128)(2,1)S(1)}, u32[]{:S(2)}, u32[]{:S(2)}) collective-permute-start(bf16[320,1024]{1,0:T(8,128)(2,1)S(1)} %collective-permute-done.1.refs_6_), channel_id=1, source_target_pairs={{0,32},{1,33},{2,34},{3,35},{4,36},{5,37},{6,38},{7,39},{8,40},{9,... | collective-permute-start | bytes 1966088 | tf_op jit(solution)/shard_map/ppermute | solution.py:139
  42.2 26.9 %collective-permute-start.15 = (bf16[320,1024]{1,0:T(8,128)(2,1)S(1)}, bf16[320,1024]{1,0:T(8,128)(2,1)S(1)}, u32[]{:S(2)}, u32[]{:S(2)}) collective-permute-start(bf16[320,1024]{1,0:T(8,128)(2,1)S(1)} %collective-permute-done.13.refs_0_), channel_id=1, source_target_pairs={{0,224},{1,225},{2,226},{3,227},{4,228},{5,229},{6,230},{7,231},{8... | collective-permute-start | bytes 1966088 | tf_op jit(solution)/shard_map/ppermute | solution.py:139
  44.9 25.5 %collective-permute-start.14 = (bf16[320,1024]{1,0:T(8,128)(2,1)S(1)}, bf16[320,1024]{1,0:T(8,128)(2,1)S(1)}, u32[]{:S(2)}, u32[]{:S(2)}) collective-permute-start(bf16[320,1024]{1,0:T(8,128)(2,1)S(1)} %collective-permute-done.13.refs_0_), channel_id=1, source_target_pairs={{0,32},{1,33},{2,34},{3,35},{4,36},{5,37},{6,38},{7,39},{8,40},{9,... | collective-permute-start | bytes 1966088 | tf_op jit(solution)/shard_map/ppermute | solution.py:139
  76.5 18.8 %collective-permute-start.16 = (f32[2,4,160,640]{3,2,1,0:T(8,128)S(1)}, f32[2,4,160,640]{3,2,1,0:T(8,128)S(1)}, u32[]{:S(2)}, u32[]{:S(2)}) collective-permute-start(f32[2,4,160,640]{3,2,1,0:T(8,128)S(1)} %bitcast.92), channel_id=1, source_target_pairs={{0,1},{1,0},{2,3},{3,2},{4,5},{5,4},{6,7},{7,6},{8,9},{9,8},{10,11... | collective-permute-start | bytes 9830408 | tf_op jit(solution)/shard_map/ppermute | solution.py:139
  86.8 10.2 %collective-permute-start.9 = (f32[2,4,160,640]{3,2,1,0:T(8,128)S(1)}, f32[2,4,160,640]{3,2,1,0:T(8,128)S(1)}, u32[]{:S(2)}, u32[]{:S(2)}) collective-permute-start(f32[2,4,160,640]{3,2,1,0:T(8,128)S(1)} %bitcast.93), channel_id=1, source_target_pairs={{0,1},{1,0},{2,3},{3,2},{4,5},{5,4},{6,7},{7,6},{8,9},{9,8},{10,11... | collective-permute-start | bytes 9830408 | tf_op jit(solution)/shard_map/ppermute | solution.py:139
  87.7 6.4 %collective-permute-start = (f32[8]{0:T(128)S(1)}, f32[8]{0:T(128)S(1)}, u32[]{:S(2)}, u32[]{:S(2)}) collective-permute-start(f32[8]{0:T(128)S(1)} %convert_reduce_fusion), channel_id=1, source_target_pairs={{0,8},{1,25},{2,234},{3,251},{4,244},{5,5},{6,22},{7,39},{8,16},{9... | collective-permute-start | bytes 104 | tf_op jit(solution)/shard_map/ppermute | solution.py:139
  97.8 10.5 %collective-permute-start.10 = (bf16[2,96,640]{2,1,0:T(8,128)(2,1)S(1)}, bf16[2,96,640]{2,1,0:T(8,128)(2,1)S(1)}, u32[]{:S(2)}, u32[]{:S(2)}) collective-permute-start(bf16[2,96,640]{2,1,0:T(8,128)(2,1)S(1)} %pad_maximum_fusion.1), channel_id=1, source_target_pairs={{0,2},{1,3},{2,4},{3,5},{4,6},{5,7},{6,0},{7,1},{8,10},{9,11},{10,... | collective-permute-start | bytes 737288 | tf_op jit(solution)/shard_map/ppermute | solution.py:139
  99.3 10.5 %collective-permute-start.11 = (bf16[2,96,640]{2,1,0:T(8,128)(2,1)S(1)}, bf16[2,96,640]{2,1,0:T(8,128)(2,1)S(1)}, u32[]{:S(2)}, u32[]{:S(2)}) collective-permute-start(bf16[2,96,640]{2,1,0:T(8,128)(2,1)S(1)} %pad_maximum_fusion.2), channel_id=1, source_target_pairs={{0,6},{1,7},{2,0},{3,1},{4,2},{5,3},{6,4},{7,5},{8,14},{9,15},{10,... | collective-permute-start | bytes 737288 | tf_op jit(solution)/shard_map/ppermute | solution.py:139
  100.9 10.1 %collective-permute-start.12 = (bf16[2,96,640]{2,1,0:T(8,128)(2,1)S(1)}, bf16[2,96,640]{2,1,0:T(8,128)(2,1)S(1)}, u32[]{:S(2)}, u32[]{:S(2)}) collective-permute-start(bf16[2,96,640]{2,1,0:T(8,128)(2,1)S(1)} %pad_maximum_fusion.3), channel_id=1, source_target_pairs={{0,4},{1,5},{2,6},{3,7},{4,0},{5,1},{6,2},{7,3},{8,12},{9,13},{10,... | collective-permute-start | bytes 737288 | tf_op jit(solution)/shard_map/ppermute | solution.py:139
  102.5 5.7 %collective-permute-start.27 = (bf16[2,64,640]{2,1,0:T(8,128)(2,1)S(1)}, bf16[2,64,640]{2,1,0:T(8,128)(2,1)S(1)}, u32[]{:S(2)}, u32[]{:S(2)}) collective-permute-start(bf16[2,64,640]{2,1,0:T(8,128)(2,1)S(1)} %slice_bitcast_fusion.3), channel_id=1, source_target_pairs={{0,24},{1,9},{2,26},{3,11},{4,28},{5,13},{6,30},{7,15},{8,0},{9,17... | collective-permute-start | bytes 491528 | tf_op jit(solution)/shard_map/ppermute | solution.py:139
  102.7 14.5 %collective-permute-start.17 = (bf16[2,96,640]{2,1,0:T(8,128)(2,1)S(1)}, bf16[2,96,640]{2,1,0:T(8,128)(2,1)S(1)}, u32[]{:S(2)}, u32[]{:S(2)}) collective-permute-start(bf16[2,96,640]{2,1,0:T(8,128)(2,1)S(1)} %pad_maximum_fusion.4), channel_id=1, source_target_pairs={{0,2},{1,3},{2,4},{3,5},{4,6},{5,7},{6,0},{7,1},{8,10},{9,11},{10,... | collective-permute-start | bytes 737288 | tf_op jit(solution)/shard_map/ppermute | solution.py:139
  108.2 19.3 %collective-permute-start.25 = (bf16[2,64,640]{2,1,0:T(8,128)(2,1)S(1)}, bf16[2,64,640]{2,1,0:T(8,128)(2,1)S(1)}, u32[]{:S(2)}, u32[]{:S(2)}) collective-permute-start(bf16[2,64,640]{2,1,0:T(8,128)(2,1)S(1)} %get-tuple-element.91), channel_id=1, source_target_pairs={{0,24},{1,25},{2,26},{3,27},{4,28},{5,29},{6,30},{7,31},{8,0},{9,1... | collective-permute-start | bytes 491528 | tf_op jit(solution)/shard_map/ppermute | solution.py:139
  108.3 19.2 %collective-permute-start.24 = (bf16[2,64,640]{2,1,0:T(8,128)(2,1)S(1)}, bf16[2,64,640]{2,1,0:T(8,128)(2,1)S(1)}, u32[]{:S(2)}, u32[]{:S(2)}) collective-permute-start(bf16[2,64,640]{2,1,0:T(8,128)(2,1)S(1)} %get-tuple-element.92), channel_id=1, source_target_pairs={{0,8},{1,9},{2,10},{3,11},{4,12},{5,13},{6,14},{7,15},{8,16},{9,17... | collective-permute-start | bytes 491528 | tf_op jit(solution)/shard_map/ppermute | solution.py:139
  109.8 19.0 %collective-permute-start.23 = (bf16[2,64,640]{2,1,0:T(8,128)(2,1)S(1)}, bf16[2,64,640]{2,1,0:T(8,128)(2,1)S(1)}, u32[]{:S(2)}, u32[]{:S(2)}) collective-permute-start(bf16[2,64,640]{2,1,0:T(8,128)(2,1)S(1)} %get-tuple-element.93), channel_id=1, source_target_pairs={{0,8},{1,25},{2,10},{3,27},{4,12},{5,29},{6,14},{7,31},{8,16},{9,1... | collective-permute-start | bytes 491528 | tf_op jit(solution)/shard_map/ppermute | solution.py:139
  111.0 10.4 %collective-permute-start.19 = (bf16[2,96,640]{2,1,0:T(8,128)(2,1)S(1)}, bf16[2,96,640]{2,1,0:T(8,128)(2,1)S(1)}, u32[]{:S(2)}, u32[]{:S(2)}) collective-permute-start(bf16[2,96,640]{2,1,0:T(8,128)(2,1)S(1)} %pad_maximum_fusion.6), channel_id=1, source_target_pairs={{0,4},{1,5},{2,6},{3,7},{4,0},{5,1},{6,2},{7,3},{8,12},{9,13},{10,... | collective-permute-start | bytes 737288 | tf_op jit(solution)/shard_map/ppermute | solution.py:139
  117.2 7.2 %collective-permute-start.18 = (bf16[2,96,640]{2,1,0:T(8,128)(2,1)S(1)}, bf16[2,96,640]{2,1,0:T(8,128)(2,1)S(1)}, u32[]{:S(2)}, u32[]{:S(2)}) collective-permute-start(bf16[2,96,640]{2,1,0:T(8,128)(2,1)S(1)} %pad_maximum_fusion.5), channel_id=1, source_target_pairs={{0,6},{1,7},{2,0},{3,1},{4,2},{5,3},{6,4},{7,5},{8,14},{9,15},{10,... | collective-permute-start | bytes 737288 | tf_op jit(solution)/shard_map/ppermute | solution.py:139
  121.4 7.8 %collective-permute-start.26 = (bf16[4,64,640]{2,1,0:T(8,128)(2,1)S(1)}, bf16[4,64,640]{2,1,0:T(8,128)(2,1)S(1)}, u32[]{:S(2)}, u32[]{:S(2)}) collective-permute-start(bf16[4,64,640]{2,1,0:T(8,128)(2,1)S(1)} %slice_bitcast_fusion.2), channel_id=1, source_target_pairs={{0,16},{1,17},{2,18},{3,19},{4,20},{5,21},{6,22},{7,23},{8,24},{9,... | collective-permute-start | bytes 983048 | tf_op jit(solution)/shard_map/ppermute | solution.py:139
  124.5 10.9 %collective-permute-start.20 = (bf16[96,640]{1,0:T(8,128)(2,1)S(1)}, bf16[96,640]{1,0:T(8,128)(2,1)S(1)}, u32[]{:S(2)}, u32[]{:S(2)}) collective-permute-start(bf16[96,640]{1,0:T(8,128)(2,1)S(1)} %get-tuple-element.109), channel_id=1, source_target_pairs={{0,8},{1,25},{2,10},{3,27},{4,12},{5,13},{6,14},{7,15},{8,16},{9,1... | collective-permute-start | bytes 368648 | tf_op jit(solution)/shard_map/ppermute | solution.py:139
  127.5 11.1 %collective-permute-start.22 = (bf16[96,640]{1,0:T(8,128)(2,1)S(1)}, bf16[96,640]{1,0:T(8,128)(2,1)S(1)}, u32[]{:S(2)}, u32[]{:S(2)}) collective-permute-start(bf16[96,640]{1,0:T(8,128)(2,1)S(1)} %get-tuple-element.110), channel_id=1, source_target_pairs={{0,24},{1,9},{2,26},{3,11},{4,28},{5,29},{6,30},{7,31},{8,0},{9,17... | collective-permute-start | bytes 368648 | tf_op jit(solution)/shard_map/ppermute | solution.py:139
  127.5 11.1 %collective-permute-start.21 = (bf16[96,640]{1,0:T(8,128)(2,1)S(1)}, bf16[96,640]{1,0:T(8,128)(2,1)S(1)}, u32[]{:S(2)}, u32[]{:S(2)}) collective-permute-start(bf16[96,640]{1,0:T(8,128)(2,1)S(1)} %get-tuple-element.111), channel_id=1, source_target_pairs={{0,16},{1,17},{2,18},{3,19},{4,20},{5,21},{6,22},{7,23},{8,24},{9,... | collective-permute-start | bytes 368648 | tf_op jit(solution)/shard_map/ppermute | solution.py:139
  129.4 9.3 %collective-permute-start.28 = (bf16[64,640]{1,0:T(8,128)(2,1)S(1)}, bf16[64,640]{1,0:T(8,128)(2,1)S(1)}, u32[]{:S(2)}, u32[]{:S(2)}) collective-permute-start(bf16[64,640]{1,0:T(8,128)(2,1)S(1)} %get-tuple-element.106), channel_id=1, source_target_pairs={{0,2},{1,3},{2,4},{3,5},{4,6},{5,7},{6,0},{7,1},{8,10},{9,11},{10,... | collective-permute-start | bytes 245768 | tf_op jit(solution)/shard_map/ppermute | solution.py:139
  130.4 8.3 %collective-permute-start.30 = (bf16[64,640]{1,0:T(8,128)(2,1)S(1)}, bf16[64,640]{1,0:T(8,128)(2,1)S(1)}, u32[]{:S(2)}, u32[]{:S(2)}) collective-permute-start(bf16[64,640]{1,0:T(8,128)(2,1)S(1)} %get-tuple-element.107), channel_id=1, source_target_pairs={{0,4},{1,5},{2,6},{3,7},{4,0},{5,1},{6,2},{7,3},{8,12},{9,13},{10,... | collective-permute-start | bytes 245768 | tf_op jit(solution)/shard_map/ppermute | solution.py:139
  138.8 14.9 %collective-permute-start.32 = (bf16[160,640]{1,0:T(8,128)(2,1)S(1)}, bf16[160,640]{1,0:T(8,128)(2,1)S(1)}, u32[]{:S(2)}, u32[]{:S(2)}) collective-permute-start(bf16[160,640]{1,0:T(8,128)(2,1)S(1)} %fusion.5), channel_id=1, source_target_pairs={{0,33},{1,32},{2,35},{3,34},{4,20},{5,5},{6,246},{7,231},{8,41},{9... | collective-permute-start | bytes 614408 | tf_op jit(solution)/shard_map/ppermute | solution.py:139
  144.6 11.0 %collective-permute-start.31 = (bf16[160,640]{1,0:T(8,128)(2,1)S(1)}, bf16[160,640]{1,0:T(8,128)(2,1)S(1)}, u32[]{:S(2)}, u32[]{:S(2)}) collective-permute-start(bf16[160,640]{1,0:T(8,128)(2,1)S(1)} %fusion.5), channel_id=1, source_target_pairs={{0,254},{1,239},{2,28},{3,13},{4,35},{5,34},{6,33},{7,32},{8,6},{9... | collective-permute-start | bytes 614408 | tf_op jit(solution)/shard_map/ppermute | solution.py:139
  (3 other events, 26.2 us)
